TPU v7x, 256 devices: a whole 4x4x8 slice. The times are simulated.
256 devices in a mesh: patch: 32 (over y, x, core), rhs: 8 (over z).
Axes of the slice: x: 4, y: 4, z: 8, core: 2. Of those that a mesh axis runs over, the one named last changes fastest.
Arguments:
- rhs_vectors: float32 [256, 16, 384], P('patch', 'rhs'), may hold values from -8 to 8
- near_blocks: bfloat16 [256, 4, 384, 384], P('patch'), may hold values from -1 to 5, as said below
- neighbours: int32 [256, 4], P('patch'), may hold values from 0 to 255, as said below
- up_maps: float32 [256, 64, 384], P('patch'), may hold values from -0.3125 to 0.3125
- shift_up: float32 [256, 64, 64], P('patch'), may hold values from -0.25 to 0.25
- far_lists: int32 [32, 4], P('patch'), may hold values from 0 to 31, as said below
- translations: float32 [32, 4, 64, 64], P('patch'), may hold values from -0.375 to 0.375
- shift_down: float32 [256, 64, 64], P('patch'), may hold values from -0.75 to 0.75
- down_maps: float32 [256, 384, 64], P('patch'), may hold values from -0.375 to 0.375
Outputs:
- solution: float32 [256, 16, 384], P('patch', 'rhs')
- residual: float32 [256, 16, 384], P('patch', 'rhs')
Inputs may be any that keep to these rules, and one draw needn't show every extreme that they name: `neighbours`: entry 0 of each row is the patch itself; every other entry names a patch of the same cell or of the cell just before or just after it, cyclically. `far_lists`: entry 0 of each row names the cell just before or just after the row's own cell, cyclically, and for cell 0 the cell just before it; every other entry names a cell other than the row's own. `near_blocks`: the blocks keep the operator's symmetric part positive definite.
All inputs are finite; a program needn't handle non-finite values.
Results may differ from a plain program's by a relative error of at most 0.008.
The roundings to bfloat16 on the way count: a program that leaves them out, or rounds other values in their place, can miss the bound.
Values may be sent and summed in bfloat16 or wider, within the bound.
No kernel may reach another device: no remote copies, remote signals or barrier semaphores. Data moves between devices by JAX's collectives and lax.ppermute only.
A program may use at most 64 MiB of HBM per device.

v0:
```python
import jax
import jax.numpy as jnp
from jax import lax
from jax.sharding import PartitionSpec as P

ITERS = 2


HIGH = lax.Precision.HIGHEST


def from_everyone(array, axis):
    devices = lax.axis_size(axis)
    return lax.all_to_all(
        jnp.broadcast_to(array[None], (devices, *array.shape)), axis, 0, 0, tiled=True
    )


def taken_together(array, axis):
    return from_everyone(array, axis).sum(axis=0)


def with_halo(block, sides, width):
    for axis, dim in sides:
        count = lax.axis_size(axis)
        forward = [(i, i + 1) for i in range(count - 1)]
        forward.append((count - 1, 0))
        backward = [(target, source) for source, target in forward]
        low = lax.ppermute(
            lax.slice_in_dim(block, block.shape[dim] - width, None, axis=dim), axis, forward
        )
        high = lax.ppermute(lax.slice_in_dim(block, 0, width, axis=dim), axis, backward)
        block = jnp.concatenate([low, block, high], axis=dim)
    return block


def laid_out(parts, dim):
    parts = jnp.moveaxis(parts, 0, dim)
    lengths = parts.shape
    return parts.reshape(*lengths[:dim], lengths[dim] * lengths[dim + 1], *lengths[dim + 2 :])


def collect(array, axis, dim):
    parts = from_everyone(array, axis)
    return laid_out(parts, dim)


def spd_solve(matrix, right):
    factor = jnp.linalg.cholesky(matrix)
    return jax.scipy.linalg.cho_solve((factor, True), right)


def gram(left, right):
    return jnp.einsum("pkw,plw->kl", left, right, precision=HIGH)


def mix(field, coeffs):
    return jnp.einsum("pkw,kl->plw", field, coeffs, precision=HIGH)


def residual_sum(residual):
    return taken_together(gram(residual, residual), "patch")


def apply_operator(
    field,
    near_blocks,
    neighbours,
    up_maps,
    shift_up,
    far_lists,
    translations,
    shift_down,
    down_maps,
):
    patches = field.shape[0]
    count = lax.axis_size("patch")
    first = lax.axis_index("patch") * patches - patches
    rounded = field.astype(jnp.bfloat16)
    widened = with_halo(rounded, (("patch", 0),), patches)
    local_ids = jnp.mod(neighbours - first, patches * count)
    picked = widened[local_ids]
    near = jnp.einsum("pjvw,pjkw->pkv", near_blocks, picked, preferred_element_type=jnp.float32)
    moments = jnp.einsum("pew,pkw->pke", up_maps, field, precision=HIGH)
    cell_moment = jnp.einsum("pfe,pke->kf", shift_up, moments, precision=HIGH)
    sources = far_lists[0]
    table = translations[0]
    piece = collect(cell_moment[None], "patch", 0)
    labels = jnp.arange(piece.shape[0], dtype=jnp.int32)
    select = (sources[:, None] == labels[None, :]).astype(jnp.float32)
    chosen = jnp.einsum("ji,ike->jke", select, piece, precision=HIGH)
    local_exp = jnp.zeros_like(cell_moment) + jnp.einsum(
        "jfe,jke->kf", table, chosen, precision=HIGH
    )
    patch_exp = jnp.einsum("pfe,ke->pkf", shift_down, local_exp, precision=HIGH)
    far = jnp.einsum("pvf,pkf->pkv", down_maps, patch_exp, precision=HIGH)
    return near + far


def on_device(
    rhs_vectors,
    near_blocks,
    neighbours,
    up_maps,
    shift_up,
    far_lists,
    translations,
    shift_down,
    down_maps,
):
    my_cols = rhs_vectors.shape[1]
    offset = lax.axis_index("rhs") * my_cols
    residual = collect(rhs_vectors, "rhs", 1)
    solution = jnp.zeros_like(residual)
    direction = residual
    current = jnp.zeros((residual.shape[1], residual.shape[1]), jnp.float32)
    for step in range(ITERS):
        image = apply_operator(
            direction,
            near_blocks,
            neighbours,
            up_maps,
            shift_up,
            far_lists,
            translations,
            shift_down,
            down_maps,
        )
        if step == 0:
            current = residual_sum(residual)
        curve = taken_together(gram(direction, image), "patch")
        curve = 0.5 * (curve + curve.T)
        alpha = spd_solve(curve, current)
        solution = solution + mix(direction, alpha)
        residual = residual - mix(image, alpha)
        if step + 1 < ITERS:
            following = residual_sum(residual)
            beta = spd_solve(current, following)
            direction = residual + mix(direction, beta)
            current = following
    solution_mine = lax.dynamic_slice_in_dim(solution, offset, my_cols, 1)
    residual_mine = lax.dynamic_slice_in_dim(residual, offset, my_cols, 1)
    return (solution_mine, residual_mine)


def solution(mesh):
    return jax.shard_map(
        on_device,
        mesh=mesh,
        in_specs=(
            P("patch", "rhs", None),
            P("patch", None, None, None),
            P("patch", None),
            P("patch", None, None),
            P("patch", None, None),
            P("patch", None),
            P("patch", None, None, None),
            P("patch", None, None),
            P("patch", None, None),
        ),
        out_specs=(P("patch", "rhs", None), P("patch", "rhs", None)),
        check_vma=False,
    )
```

profile of v0, /device:TPU:1, one launch (start us, length us, event | category | flops | bytes accessed | tf_op | source)
XLA Modules:
  0.0 139.1 jit_solution(15504959503871310235)
XLA Ops:
  0.6 1.5 %broadcast_in_dim.16 = f32[8,8,2,384]{3,2,1,0:T(2,128)} broadcast(f32[8,2,384]{2,1,0:T(2,128)} %param.12), dimensions={1,2,3} | broadcast | bytes 221184 | tf_op jit(solution)/shard_map/broadcast_in_dim | solution.py:15
  2.2 9.0 %all-to-all-start = ((f32[8,8,2,384]{3,2,1,0:T(2,128)}), f32[8,8,2,384]{3,2,1,0:T(2,128)S(1)}, u32[]{:S(2)}, u32[]{:S(2)}) async-start(f32[8,8,2,384]{3,2,1,0:T(2,128)} %broadcast_in_dim.16), calls=%async_computation | async-start | bytes 393216 | tf_op jit(solution)/shard_map/all_to_all | solution.py:14
  11.2 0.7 compare_select_fusion
  12.0 8.1 %all-to-all-done = f32[8,8,2,384]{3,2,1,0:T(2,128)S(1)} async-done(((f32[8,8,2,384]{3,2,1,0:T(2,128)}), f32[8,8,2,384]{3,2,1,0:T(2,128)S(1)}, u32[]{:S(2)}, u32[]{:S(2)}) %all-to-all-start) | async-done | bytes 196640 | tf_op jit(solution)/shard_map/all_to_all | solution.py:14
  20.4 0.3 convolution_bitcast_fusion.14
  20.8 2.5 %collective-permute-start.1 = (bf16[8,16,384]{2,1,0:T(8,128)(2,1)S(1)}, bf16[8,16,384]{2,1,0:T(8,128)(2,1)S(1)}, u32[]{:S(2)}, u32[]{:S(2)}) collective-permute-start(bf16[8,16,384]{2,1,0:T(8,128)(2,1)S(1)} %convert_element_type.8), channel_id=1, source_target_pairs={{8,0},{16,8},{24,16},{32,24},{40,32},{48,40},{56,48},{64,56},{72,6... | collective-permute-start | bytes 294920 | tf_op jit(solution)/shard_map/ppermute | solution.py:32
  23.3 1.2 collective-permute-start
  24.5 2.1 %fusion.39 = f32[8,16,64]{2,1,0:T(8,128)S(1)} fusion(f32[8,16,384]{2,1,0:T(8,128)S(1)} %reshape.35, f32[8,64,384]{2,1,0:T(8,128)} %param.15), kind=kOutput, calls=%fused_computation.83 | convolution fusion | flops 37748736 | bytes 1015808 | tf_op jit(solution)/shard_map/pew,pkw->pke/dot_general | solution.py:84
  26.6 0.7 reshape.76
  27.3 8.2 %all-to-all-start.3 = ((f32[32,1,256]{2,1,0:T(1,128)}), f32[32,1,256]{2,1,0:T(1,128)S(1)}, u32[]{:S(2)}, u32[]{:S(2)}) async-start(f32[32,1,256]{2,1,0:T(1,128)} %reshape.76), calls=%async_computation.3 | async-start | bytes 65536 | tf_op jit(solution)/shard_map/all_to_all | solution.py:14
  35.5 1.2 convolution_bitcast_fusion.11
  36.8 0.8 reshape.78
  37.6 5.1 %all-to-all-done.3 = f32[32,1,256]{2,1,0:T(1,128)S(1)} async-done(((f32[32,1,256]{2,1,0:T(1,128)}), f32[32,1,256]{2,1,0:T(1,128)S(1)}, u32[]{:S(2)}, u32[]{:S(2)}) %all-to-all-start.3) | async-done | bytes 32800 | tf_op jit(solution)/shard_map/all_to_all | solution.py:14
  42.8 3.9 %all-to-all-start.1 = ((f32[32,1,1024]{2,1,0:T(1,128)}), f32[32,1,1024]{2,1,0:T(1,128)S(1)}, u32[]{:S(2)}, u32[]{:S(2)}) async-start(f32[32,1,1024]{2,1,0:T(1,128)} %reshape.78), calls=%async_computation.1 | async-start | bytes 262144 | tf_op jit(solution)/shard_map/all_to_all | solution.py:14
  46.7 0.5 broadcast.84
  47.2 0.7 reduce.4
  48.2 1.5 %cholesky.70 = f32[16,16]{1,0:T(8,128)S(1)} custom-call(f32[16,16]{1,0:T(8,128)S(1)} %fusion.26), custom_call_target="Cholesky" | custom-call | tf_op jit(solution)/shard_map/jit(cholesky)/cholesky | solution.py:49
  49.7 0.6 gather_fusion
  50.4 6.3 %convolution_bitcast_fusion.4 = f32[8,16,384]{2,1,0:T(8,128)S(1)} fusion(bf16[8,4,16,384]{3,2,1,0:T(8,128)(2,1)S(1)} %bitcast.151, bf16[8,4,384,384]{3,2,1,0:T(8,128)(2,1)} %param.13), kind=kOutput, calls=%fused_computation.10 | convolution fusion | flops 150994944 | bytes 10027008 | tf_op jit(solution)/shard_map/pjvw,pjkw->pkv/dot_general | solution.py:83
  56.7 1.0 reduce.5
  58.3 0.7 convolution_bitcast_fusion.6
  59.0 0.6 convolution_add_fusion.1
  59.7 0.3 convolution_bitcast_fusion.15
  60.2 0.8 reshape.80
  60.9 7.5 %all-to-all-start.2 = ((f32[32,1,256]{2,1,0:T(1,128)}), f32[32,1,256]{2,1,0:T(1,128)S(1)}, u32[]{:S(2)}, u32[]{:S(2)}) async-start(f32[32,1,256]{2,1,0:T(1,128)} %reshape.80), calls=%async_computation.2 | async-start | bytes 65536 | tf_op jit(solution)/shard_map/all_to_all | solution.py:14
  68.4 0.7 compare_reduce_fusion.1
  69.1 6.6 %all-to-all-done.2 = f32[32,1,256]{2,1,0:T(1,128)S(1)} async-done(((f32[32,1,256]{2,1,0:T(1,128)}), f32[32,1,256]{2,1,0:T(1,128)S(1)}, u32[]{:S(2)}, u32[]{:S(2)}) %all-to-all-start.2) | async-done | bytes 32800 | tf_op jit(solution)/shard_map/all_to_all | solution.py:14
  75.6 0.7 reduce.6
  76.7 1.5 %cholesky.59 = f32[16,16]{1,0:T(8,128)S(1)} custom-call(f32[16,16]{1,0:T(8,128)S(1)} %fusion.30), custom_call_target="Cholesky" | custom-call | tf_op jit(solution)/shard_map/jit(cholesky)/cholesky | solution.py:49
  78.2 0.6 compare_reduce_fusion.2
  78.8 0.6 fusion.15
  79.5 1.2 custom-call.9
  81.1 0.3 fusion.1
  81.5 0.3 convolution_bitcast_fusion.13
  81.9 0.8 reshape.82
  82.6 3.9 %all-to-all-start.4 = ((f32[32,1,256]{2,1,0:T(1,128)}), f32[32,1,256]{2,1,0:T(1,128)S(1)}, u32[]{:S(2)}, u32[]{:S(2)}) async-start(f32[32,1,256]{2,1,0:T(1,128)} %reshape.82), calls=%async_computation.4 | async-start | bytes 65536 | tf_op jit(solution)/shard_map/all_to_all | solution.py:14
  86.5 0.6 fusion.16
  87.2 1.2 custom-call.10
  88.4 5.5 %all-to-all-done.4 = f32[32,1,256]{2,1,0:T(1,128)S(1)} async-done(((f32[32,1,256]{2,1,0:T(1,128)}), f32[32,1,256]{2,1,0:T(1,128)S(1)}, u32[]{:S(2)}, u32[]{:S(2)}) %all-to-all-start.4) | async-done | bytes 32800 | tf_op jit(solution)/shard_map/all_to_all | solution.py:14
  93.9 0.7 reduce.7
  95.2 0.3 fusion.38
  95.5 0.5 collective-permute-start.3
  96.0 1.4 collective-permute-start.2
  97.3 0.9 fusion.41
  98.6 0.8 reshape.84
  99.5 6.6 %all-to-all-start.5 = ((f32[32,1,1024]{2,1,0:T(1,128)}), f32[32,1,1024]{2,1,0:T(1,128)S(1)}, u32[]{:S(2)}, u32[]{:S(2)}) async-start(f32[32,1,1024]{2,1,0:T(1,128)} %reshape.84), calls=%async_computation.5 | async-start | bytes 262144 | tf_op jit(solution)/shard_map/all_to_all | solution.py:14
  106.1 0.6 gather_fusion.1
  106.8 6.2 %convolution_bitcast_fusion.3 = f32[8,16,384]{2,1,0:T(8,128)S(1)} fusion(bf16[8,4,16,384]{3,2,1,0:T(8,128)(2,1)S(1)} %bitcast.150, bf16[8,4,384,384]{3,2,1,0:T(8,128)(2,1)} %param.13), kind=kOutput, calls=%fused_computation.9 | convolution fusion | flops 150994944 | bytes 10027008 | tf_op jit(solution)/shard_map/pjvw,pjkw->pkv/dot_general | solution.py:83
  113.0 0.7 all-to-all-done.5
  113.7 1.0 reduce.8
  115.2 0.7 convolution_bitcast_fusion.5
  115.9 0.6 convolution_add_fusion
  116.5 0.3 convolution_bitcast_fusion.12
  117.0 0.8 reshape.86
  117.7 6.7 %all-to-all-start.6 = ((f32[32,1,256]{2,1,0:T(1,128)}), f32[32,1,256]{2,1,0:T(1,128)S(1)}, u32[]{:S(2)}, u32[]{:S(2)}) async-start(f32[32,1,256]{2,1,0:T(1,128)} %reshape.86), calls=%async_computation.6 | async-start | bytes 65536 | tf_op jit(solution)/shard_map/all_to_all | solution.py:14
  124.8 6.9 %all-to-all-done.6 = f32[32,1,256]{2,1,0:T(1,128)S(1)} async-done(((f32[32,1,256]{2,1,0:T(1,128)}), f32[32,1,256]{2,1,0:T(1,128)S(1)}, u32[]{:S(2)}, u32[]{:S(2)}) %all-to-all-start.6) | async-done | bytes 32800 | tf_op jit(solution)/shard_map/all_to_all | solution.py:14
  131.7 0.7 reduce.9
  132.8 1.5 %cholesky.81 = f32[16,16]{1,0:T(8,128)S(1)} custom-call(f32[16,16]{1,0:T(8,128)S(1)} %fusion.21), custom_call_target="Cholesky" | custom-call | tf_op jit(solution)/shard_map/jit(cholesky)/cholesky | solution.py:49
  134.3 0.6 compare_reduce_fusion
  134.9 0.6 fusion.17
  135.6 1.2 custom-call.11
  137.2 0.3 convolution_bitcast_fusion
  137.8 0.6 dynamic-slice_subtract_fusion
  138.5 0.6 fusion.14
  (68 shorter events, 5.3 us)
Async XLA Ops:
  0.6 58.4 %copy-start = (f32[8,384,64]{1,2,0:T(8,128)S(1)}, f32[8,384,64]{1,2,0:T(8,128)}, u32[]{:S(2)}) copy-start(f32[8,384,64]{1,2,0:T(8,128)} %param.20) | copy-start | bytes 2359300
  2.2 18.0 %all-to-all-start = ((f32[8,8,2,384]{3,2,1,0:T(2,128)}), f32[8,8,2,384]{3,2,1,0:T(2,128)S(1)}, u32[]{:S(2)}, u32[]{:S(2)}) async-start(f32[8,8,2,384]{3,2,1,0:T(2,128)} %broadcast_in_dim.16), calls=%async_computation | async-start | bytes 393216 | tf_op jit(solution)/shard_map/all_to_all | solution.py:14
  20.8 28.9 %collective-permute-start.1 = (bf16[8,16,384]{2,1,0:T(8,128)(2,1)S(1)}, bf16[8,16,384]{2,1,0:T(8,128)(2,1)S(1)}, u32[]{:S(2)}, u32[]{:S(2)}) collective-permute-start(bf16[8,16,384]{2,1,0:T(8,128)(2,1)S(1)} %convert_element_type.8), channel_id=1, source_target_pairs={{8,0},{16,8},{24,16},{32,24},{40,32},{48,40},{56,48},{64,56},{72,6... | collective-permute-start | bytes 294920 | tf_op jit(solution)/shard_map/ppermute | solution.py:32
  23.3 26.4 %collective-permute-start = (bf16[8,16,384]{2,1,0:T(8,128)(2,1)S(1)}, bf16[8,16,384]{2,1,0:T(8,128)(2,1)S(1)}, u32[]{:S(2)}, u32[]{:S(2)}) collective-permute-start(bf16[8,16,384]{2,1,0:T(8,128)(2,1)S(1)} %convert_element_type.8), channel_id=1, source_target_pairs={{0,8},{8,16},{16,24},{24,32},{32,40},{40,48},{48,56},{56,64},{64,7... | collective-permute-start | bytes 294920 | tf_op jit(solution)/shard_map/ppermute | solution.py:29
  27.3 15.5 %all-to-all-start.3 = ((f32[32,1,256]{2,1,0:T(1,128)}), f32[32,1,256]{2,1,0:T(1,128)S(1)}, u32[]{:S(2)}, u32[]{:S(2)}) async-start(f32[32,1,256]{2,1,0:T(1,128)} %reshape.76), calls=%async_computation.3 | async-start | bytes 65536 | tf_op jit(solution)/shard_map/all_to_all | solution.py:14
  42.8 14.0 %all-to-all-start.1 = ((f32[32,1,1024]{2,1,0:T(1,128)}), f32[32,1,1024]{2,1,0:T(1,128)S(1)}, u32[]{:S(2)}, u32[]{:S(2)}) async-start(f32[32,1,1024]{2,1,0:T(1,128)} %reshape.78), calls=%async_computation.1 | async-start | bytes 262144 | tf_op jit(solution)/shard_map/all_to_all | solution.py:14
  49.7 8.1 %copy-start.5 = (s32[1,4]{1,0:T(1,128)S(1)}, s32[1,4]{1,0:T(1,128)}, u32[]{:S(2)}) copy-start(s32[1,4]{1,0:T(1,128)} %param.17) | copy-start | bytes 52
  49.7 8.4 %copy-start.4 = (f32[1,4,64,64]{3,2,1,0:T(8,128)S(1)}, f32[1,4,64,64]{3,2,1,0:T(8,128)}, u32[]{:S(2)}) copy-start(f32[1,4,64,64]{3,2,1,0:T(8,128)} %param.18) | copy-start | bytes 196612
  50.4 7.9 %copy-start.3 = (f32[8,64,64]{2,1,0:T(8,128)S(1)}, f32[8,64,64]{2,1,0:T(8,128)}, u32[]{:S(2)}) copy-start(f32[8,64,64]{2,1,0:T(8,128)} %param.19) | copy-start | bytes 393220
  50.4 46.9 %copy-start.1 = (f32[8,64,384]{2,1,0:T(8,128)S(1)}, f32[8,64,384]{2,1,0:T(8,128)}, u32[]{:S(2)}) copy-start(f32[8,64,384]{2,1,0:T(8,128)} %param.15) | copy-start | bytes 2359300
  50.4 47.9 %copy-start.2 = (f32[8,64,64]{2,1,0:T(8,128)S(1)}, f32[8,64,64]{2,1,0:T(8,128)}, u32[]{:S(2)}) copy-start(f32[8,64,64]{2,1,0:T(8,128)} %param.16) | copy-start | bytes 393220
  60.9 14.7 %all-to-all-start.2 = ((f32[32,1,256]{2,1,0:T(1,128)}), f32[32,1,256]{2,1,0:T(1,128)S(1)}, u32[]{:S(2)}, u32[]{:S(2)}) async-start(f32[32,1,256]{2,1,0:T(1,128)} %reshape.80), calls=%async_computation.2 | async-start | bytes 65536 | tf_op jit(solution)/shard_map/all_to_all | solution.py:14
  82.6 11.3 %all-to-all-start.4 = ((f32[32,1,256]{2,1,0:T(1,128)}), f32[32,1,256]{2,1,0:T(1,128)S(1)}, u32[]{:S(2)}, u32[]{:S(2)}) async-start(f32[32,1,256]{2,1,0:T(1,128)} %reshape.82), calls=%async_computation.4 | async-start | bytes 65536 | tf_op jit(solution)/shard_map/all_to_all | solution.py:14
  95.5 10.6 %collective-permute-start.3 = (bf16[8,16,384]{2,1,0:T(8,128)(2,1)S(1)}, bf16[8,16,384]{2,1,0:T(8,128)(2,1)S(1)}, u32[]{:S(2)}, u32[]{:S(2)}) collective-permute-start(bf16[8,16,384]{2,1,0:T(8,128)(2,1)S(1)} %get-tuple-element.4), channel_id=1, source_target_pairs={{8,0},{16,8},{24,16},{32,24},{40,32},{48,40},{56,48},{64,56},{72,6... | collective-permute-start | bytes 294920 | tf_op jit(solution)/shard_map/ppermute | solution.py:32
  96.0 10.1 %collective-permute-start.2 = (bf16[8,16,384]{2,1,0:T(8,128)(2,1)S(1)}, bf16[8,16,384]{2,1,0:T(8,128)(2,1)S(1)}, u32[]{:S(2)}, u32[]{:S(2)}) collective-permute-start(bf16[8,16,384]{2,1,0:T(8,128)(2,1)S(1)} %get-tuple-element.4), channel_id=1, source_target_pairs={{0,8},{8,16},{16,24},{24,32},{32,40},{40,48},{48,56},{56,64},{64,7... | collective-permute-start | bytes 294920 | tf_op jit(solution)/shard_map/ppermute | solution.py:29
  99.5 14.2 %all-to-all-start.5 = ((f32[32,1,1024]{2,1,0:T(1,128)}), f32[32,1,1024]{2,1,0:T(1,128)S(1)}, u32[]{:S(2)}, u32[]{:S(2)}) async-start(f32[32,1,1024]{2,1,0:T(1,128)} %reshape.84), calls=%async_computation.5 | async-start | bytes 262144 | tf_op jit(solution)/shard_map/all_to_all | solution.py:14
  117.7 14.0 %all-to-all-start.6 = ((f32[32,1,256]{2,1,0:T(1,128)}), f32[32,1,256]{2,1,0:T(1,128)S(1)}, u32[]{:S(2)}, u32[]{:S(2)}) async-start(f32[32,1,256]{2,1,0:T(1,128)} %reshape.86), calls=%async_computation.6 | async-start | bytes 65536 | tf_op jit(solution)/shard_map/all_to_all | solution.py:14
where the time goes:
time: 140 us; the launch traced here: 139 us
  starting transfers between devices  51.3 us (37%)
  waiting for transfers between devices  33 us (24%)
  matrix products  24.7 us (18%)
  other arithmetic  19.1 us (14%)
  local copies, waits for them, and re-layouts  9.84 us (7%)
    all_to_all x7, starting transfers between devices, from_everyone(): lax.all_to_all(jnp.broadcast_to(array[None], (devices, *array.shape)), ax...  45.8 us
    all_to_all x7, waiting for transfers between devices, from_everyone(): lax.all_to_all(jnp.broadcast_to(array[None], (devices, *array.shape)), ax...  33 us
    dot_general x2, matrix products, apply_operator(): jnp.einsum('pjvw,pjkw->pkv', near_blocks, picked, preferred_element_type=...  12.5 us
    another operation x9, other arithmetic, spd_solve(): factor = jnp.linalg.cholesky(matrix)  6.4 us
    another operation x6, other arithmetic, spd_solve(): return jax.scipy.linalg.cho_solve((factor, True), right)  5.62 us
    unnamed x24, local copies, waits for them, and re-layouts  5.38 us
    all_to_all x6, other arithmetic, from_everyone(): lax.all_to_all(jnp.broadcast_to(array[None], (devices, *array.shape)), ax...  4.8 us
    dot_general x2, matrix products, apply_operator(): moments = jnp.einsum('pew,pkw->pke', up_maps, field, precision=HIGH)  2.98 us
  transfers between devices with their start and end apart: 11, of which 6 were waited for; matrix products, arithmetic and copies ran while one was open for 20% of the time, Pallas kernels for 0%

commit v1 on v0

v1 whole, which is shorter than its diff:
```python
import jax
import jax.numpy as jnp
from jax import lax
from jax.sharding import PartitionSpec as P

HIGH = lax.Precision.HIGHEST


def einsum(spec, left, right):
    return jnp.einsum(spec, left, right, precision=HIGH)


def from_everyone(array, axis):
    devices = lax.axis_size(axis)
    return lax.all_to_all(
        jnp.broadcast_to(array[None], (devices, *array.shape)), axis, 0, 0, tiled=True
    )


def collect(array, axis, dim):
    parts = jnp.moveaxis(from_everyone(array, axis), 0, dim)
    lengths = parts.shape
    return parts.reshape(*lengths[:dim], lengths[dim] * lengths[dim + 1], *lengths[dim + 2 :])


def with_halo(block, axis):
    count = lax.axis_size(axis)
    forward = [(i, (i + 1) % count) for i in range(count)]
    backward = [(target, source) for source, target in forward]
    low = lax.ppermute(block, axis, forward)
    high = lax.ppermute(block, axis, backward)
    return jnp.concatenate([low, block, high], axis=0)


def spd_solve(matrix, right):
    factor = jnp.linalg.cholesky(matrix)
    return jax.scipy.linalg.cho_solve((factor, True), right)


def gram(left, right):
    return einsum("pkw,plw->kl", left, right)


def mix(field, coeffs):
    return einsum("pkw,kl->plw", field, coeffs)


def on_device(
    rhs_vectors,
    near_blocks,
    neighbours,
    up_maps,
    shift_up,
    far_lists,
    translations,
    shift_down,
    down_maps,
):
    patches, my_cols, width = rhs_vectors.shape
    count = lax.axis_size("patch")
    offset = lax.axis_index("rhs") * my_cols
    first = lax.axis_index("patch") * patches - patches
    local_ids = jnp.mod(neighbours - first, patches * count)
    sources = far_lists[0]
    labels = jnp.arange(count, dtype=jnp.int32)
    select = (sources[:, None] == labels[None, :]).astype(jnp.float32)
    table = translations[0]

    def near_of(wide):
        picked = wide.astype(jnp.bfloat16)[local_ids]
        return jnp.einsum(
            "pjvw,pjkw->pkv", near_blocks, picked, preferred_element_type=jnp.float32
        )

    def far_of(chosen):
        local_exp = einsum("jfe,jke->kf", table, chosen)
        return einsum("pvf,kf->pkv", down, local_exp)

    up = einsum("pfe,pew->pfw", shift_up, up_maps)
    down = einsum("pve,pef->pvf", down_maps, shift_down)

    residual = collect(rhs_vectors, "rhs", 1)
    cols = residual.shape[1]
    moment = einsum("pfw,pkw->kf", up, residual)
    terms = moment.shape[1]
    pieces = from_everyone(moment, "patch")
    wide_residual = with_halo(residual, "patch")
    near = near_of(wide_residual)
    chosen = einsum("ji,ike->jke", select, pieces)
    image = near + far_of(chosen)

    image_moment = einsum("pfw,pkw->kf", up, image)
    both = jnp.concatenate([residual, image], axis=1)
    grams = gram(both, both)
    payload = jnp.concatenate(
        [grams.reshape(-1), image_moment.reshape(-1)]
    ).reshape(-1, 128)
    wide_image = with_halo(image, "patch")
    gathered = from_everyone(payload, "patch").reshape(count, -1)
    grams = gathered[:, : 4 * cols * cols].sum(axis=0).reshape(2 * cols, 2 * cols)
    image_chosen = einsum("ji,ix->jx", select, gathered[:, 4 * cols * cols :])
    image_chosen = image_chosen.reshape(-1, cols, terms)
    current = grams[:cols, :cols]
    cross = grams[:cols, cols:]
    curve = 0.5 * (cross + cross.T)
    alpha = spd_solve(curve, current)
    shared = einsum("ab,bc->ac", cross, alpha)
    following = (
        current
        - shared
        - shared.T
        + einsum("ba,bc->ac", alpha, einsum("ab,bc->ac", grams[cols:, cols:], alpha))
    )
    beta = spd_solve(current, following)
    lift = beta + jnp.eye(cols, dtype=jnp.float32)

    wide_direction = mix(wide_residual, lift) - mix(wide_image, alpha)
    direction = wide_direction[patches : 2 * patches]
    residual1 = residual - mix(image, alpha)
    chosen1 = einsum("jke,kl->jle", chosen, lift) - einsum("jke,kl->jle", image_chosen, alpha)
    image1 = near_of(wide_direction) + far_of(chosen1)
    payload = jnp.concatenate([gram(direction, image1), gram(residual1, residual1)])
    both = from_everyone(payload, "patch").sum(axis=0)
    curve = both[:cols]
    curve = 0.5 * (curve + curve.T)
    alpha1 = spd_solve(curve, both[cols:])

    mine = lax.dynamic_slice_in_dim(alpha, offset, my_cols, 1)
    mine1 = lax.dynamic_slice_in_dim(alpha1, offset, my_cols, 1)
    solution_mine = mix(residual, mine) + mix(direction, mine1)
    residual_mine = lax.dynamic_slice_in_dim(residual1, offset, my_cols, 1) - mix(image1, mine1)
    return (solution_mine, residual_mine)


def solution(mesh):
    return jax.shard_map(
        on_device,
        mesh=mesh,
        in_specs=(
            P("patch", "rhs", None),
            P("patch", None, None, None),
            P("patch", None),
            P("patch", None, None),
            P("patch", None, None),
            P("patch", None),
            P("patch", None, None, None),
            P("patch", None, None),
            P("patch", None, None),
        ),
        out_specs=(P("patch", "rhs", None), P("patch", "rhs", None)),
        check_vma=False,
    )
```

time: 140 us -> 112 us (0.80)
  starting transfers between devices: 51.3 us -> 29.5 us
  waiting for transfers between devices: 33 us -> 24.9 us
  matrix products: 24.7 us -> 29.7 us
  other arithmetic: 19.1 us -> 15.5 us
    all_to_all x7 -> x4, starting transfers between devices: 45.8 us -> 26.1 us  [from_everyone(): lax.all_to_all(jnp.broadcast_to(array[None], (devices, *array.shape)), ax...]
    all_to_all x7 -> x4, waiting for transfers between devices: 33 us -> 24.8 us  [from_everyone(): lax.all_to_all(jnp.broadcast_to(array[None], (devices, *array.shape)), ax...]
    dot_general x23 -> x26, matrix products: 23.5 us -> 28.5 us  [the longest x24 15.9 us: einsum(): return jnp.einsum(spec, left, right, precision=HIGH)]
    all_to_all x6 -> x2, other arithmetic: 4.8 us -> 1.75 us  [from_everyone(): lax.all_to_all(jnp.broadcast_to(array[None], (devices, *array.shape)), ax...]
    gather x2, local copies, waits for them, and re-layouts: 1.27 us -> 3.9 us  [near_of(): picked = wide.astype(jnp.bfloat16)[local_ids]]
    unnamed x24 -> x15, local copies, waits for them, and re-layouts: 5.38 us -> 2.97 us
    ppermute x4, starting transfers between devices: 5.52 us -> 3.43 us  [the longest x2 3.42 us: with_halo(): low = lax.ppermute(block, axis, forward)]
  transfers between devices with their start and end apart: 11 -> 8, of which waited for: 6 -> 4; matrix products, arithmetic and copies ran while one was open for 20% -> 18% of each run, Pallas kernels for 0% -> 0%
where the time goes in v1:
time: 112 us; the launch traced here: 111 us
  matrix products  29.7 us (27%)
  starting transfers between devices  29.5 us (26%)
  waiting for transfers between devices  24.9 us (22%)
  other arithmetic  15.5 us (14%)
  local copies, waits for them, and re-layouts  10.9 us (10%)
    all_to_all x4, starting transfers between devices, from_everyone(): lax.all_to_all(jnp.broadcast_to(array[None], (devices, *array.shape)), ax...  26.1 us
    all_to_all x4, waiting for transfers between devices, from_everyone(): lax.all_to_all(jnp.broadcast_to(array[None], (devices, *array.shape)), ax...  24.8 us
    dot_general x24, matrix products, einsum(): return jnp.einsum(spec, left, right, precision=HIGH)  15.9 us
    dot_general x2, matrix products, near_of(): jnp.einsum('pjvw,pjkw->pkv', near_blocks, picked, preferred_element_type=...  12.6 us
    another operation x9, other arithmetic, spd_solve(): factor = jnp.linalg.cholesky(matrix)  6.4 us
    another operation x6, other arithmetic, spd_solve(): return jax.scipy.linalg.cho_solve((factor, True), right)  5.63 us
    gather x2, local copies, waits for them, and re-layouts, near_of(): picked = wide.astype(jnp.bfloat16)[local_ids]  3.9 us
    ppermute x2, starting transfers between devices, with_halo(): low = lax.ppermute(block, axis, forward)  3.42 us
  transfers between devices with their start and end apart: 8, of which 4 were waited for; matrix products, arithmetic and copies ran while one was open for 18% of the time, Pallas kernels for 0%

profile of v1, /device:TPU:1, one launch (start us, length us, event | category | flops | bytes accessed | tf_op | source)
XLA Modules:
  0.0 111.4 jit_solution(7187083684875105550)
XLA Ops:
  0.6 1.5 %broadcast_in_dim.10 = f32[8,8,2,384]{3,2,1,0:T(2,128)} broadcast(f32[8,2,384]{2,1,0:T(2,128)} %param.12), dimensions={1,2,3} | broadcast | bytes 221184 | tf_op jit(solution)/shard_map/broadcast_in_dim | solution.py:16
  2.2 9.0 %all-to-all-start = ((f32[8,8,2,384]{3,2,1,0:T(2,128)}), f32[8,8,2,384]{3,2,1,0:T(2,128)S(1)}, u32[]{:S(2)}, u32[]{:S(2)}) async-start(f32[8,8,2,384]{3,2,1,0:T(2,128)} %broadcast_in_dim.10), calls=%async_computation | async-start | bytes 393216 | tf_op jit(solution)/shard_map/all_to_all | solution.py:15
  11.2 1.7 %fusion.77 = f32[8,64,384]{2,1,0:T(8,128)S(1)} fusion(f32[8,64,64]{2,1,0:T(8,128)} %param.16, f32[8,64,384]{2,1,0:T(8,128)S(1)} %copy-done), kind=kOutput, calls=%fused_computation.126 | convolution fusion | flops 150994944 | bytes 1703936 | tf_op jit(solution)/shard_map/pfe,pew->pfw/dot_general | solution.py:10
  12.9 2.0 %fusion.78 = f32[8,384,64]{1,2,0:T(8,128)S(1)} fusion(f32[8,384,64]{1,2,0:T(8,128)} %param.20, f32[8,64,64]{2,1,0:T(8,128)} %param.19), kind=kOutput, calls=%fused_computation.127 | convolution fusion | flops 150994944 | bytes 1703936 | tf_op jit(solution)/shard_map/pve,pef->pvf/dot_general | solution.py:10
  15.0 5.2 %all-to-all-done = f32[8,8,2,384]{3,2,1,0:T(2,128)S(1)} async-done(((f32[8,8,2,384]{3,2,1,0:T(2,128)}), f32[8,8,2,384]{3,2,1,0:T(2,128)S(1)}, u32[]{:S(2)}, u32[]{:S(2)}) %all-to-all-start) | async-done | bytes 196640 | tf_op jit(solution)/shard_map/all_to_all | solution.py:15
  20.4 0.7 convolution_bitcast_fusion.8
  21.1 0.8 reshape.78
  21.9 9.5 %all-to-all-start.1 = ((f32[32,1,1024]{2,1,0:T(1,128)}), f32[32,1,1024]{2,1,0:T(1,128)S(1)}, u32[]{:S(2)}, u32[]{:S(2)}) async-start(f32[32,1,1024]{2,1,0:T(1,128)} %reshape.78), calls=%async_computation.1 | async-start | bytes 262144 | tf_op jit(solution)/shard_map/all_to_all | solution.py:15
  31.5 0.7 compare_select_fusion
  32.3 1.7 %collective-permute-start = (f32[8,16,384]{2,1,0:T(8,128)S(1)}, f32[8,16,384]{2,1,0:T(8,128)}, u32[]{:S(2)}, u32[]{:S(2)}) collective-permute-start(f32[8,16,384]{2,1,0:T(8,128)S(1)} %reshape.37), channel_id=1, source_target_pairs={{0,8},{8,16},{16,24},{24,32},{32,40},{40,48},{48,56},{56,64},{64,7... | collective-permute-start | bytes 589832 | tf_op jit(solution)/shard_map/ppermute | solution.py:30
  34.1 5.1 %all-to-all-done.1 = f32[32,1,1024]{2,1,0:T(1,128)S(1)} async-done(((f32[32,1,1024]{2,1,0:T(1,128)}), f32[32,1,1024]{2,1,0:T(1,128)S(1)}, u32[]{:S(2)}, u32[]{:S(2)}) %all-to-all-start.1) | async-done | bytes 131104 | tf_op jit(solution)/shard_map/all_to_all | solution.py:15
  39.1 0.5 broadcast.78
  39.6 0.9 reduce.4
  40.7 0.9 fusion.17
  41.6 1.1 fusion.24
  42.7 0.9 constant_dynamic-update-slice_fusion.2
  43.8 0.8 convert_element_type.10
  44.5 2.3 %gather_fusion = bf16[32,16,384]{2,1,0:T(8,128)(2,1)} fusion(bf16[24,16,384]{2,1,0:T(8,128)(2,1)} %convert_element_type.10, s32[1024]{0:T(1024)S(1)} %pad_clamp_fusion), kind=kCustom, calls=%fused_computation | custom fusion | bytes 786560 | tf_op jit(solution)/shard_map/gather | solution.py:70
  46.8 6.4 %convolution_bitcast_fusion.4 = f32[8,16,384]{2,1,0:T(8,128)S(1)} fusion(bf16[8,4,16,384]{3,2,1,0:T(8,128)(2,1)} %bitcast.163, bf16[8,4,384,384]{3,2,1,0:T(8,128)(2,1)} %param.13), kind=kOutput, calls=%fused_computation.11 | convolution fusion | flops 150994944 | bytes 10027008 | tf_op jit(solution)/shard_map/pjvw,pjkw->pkv/dot_general | solution.py:71
  53.2 0.5 fusion.2
  53.7 0.4 convolution_bitcast_fusion.6
  54.2 0.7 convolution_bitcast_fusion.7
  55.0 0.7 broadcast_in_dim.13
  55.8 3.9 %all-to-all-start.2 = ((f32[32,16,128]{2,1,0:T(8,128)}), f32[32,16,128]{2,1,0:T(8,128)S(1)}, u32[]{:S(2)}, u32[]{:S(2)}) async-start(f32[32,16,128]{2,1,0:T(8,128)} %broadcast_in_dim.13), calls=%async_computation.2 | async-start | bytes 524288 | tf_op jit(solution)/shard_map/all_to_all | solution.py:15
  59.7 1.7 %collective-permute-start.2 = (f32[8,16,384]{2,1,0:T(8,128)S(1)}, f32[8,16,384]{2,1,0:T(8,128)S(1)}, u32[]{:S(2)}, u32[]{:S(2)}) collective-permute-start(f32[8,16,384]{2,1,0:T(8,128)S(1)} %fusion.2), channel_id=1, source_target_pairs={{0,8},{8,16},{16,24},{24,32},{32,40},{40,48},{48,56},{56,64},{64,7... | collective-permute-start | bytes 589832 | tf_op jit(solution)/shard_map/ppermute | solution.py:30
  61.4 7.6 %all-to-all-done.2 = f32[32,16,128]{2,1,0:T(8,128)S(1)} async-done(((f32[32,16,128]{2,1,0:T(8,128)}), f32[32,16,128]{2,1,0:T(8,128)S(1)}, u32[]{:S(2)}, u32[]{:S(2)}) %all-to-all-start.2) | async-done | bytes 262176 | tf_op jit(solution)/shard_map/all_to_all | solution.py:15
  69.6 1.5 %cholesky.59 = f32[16,16]{1,0:T(8,128)S(1)} custom-call(f32[16,16]{1,0:T(8,128)S(1)} %fusion.52), custom_call_target="Cholesky" | custom-call | tf_op jit(solution)/shard_map/jit(cholesky)/cholesky | solution.py:36
  71.1 0.6 compare_reduce_fusion.2
  71.7 0.6 fusion.29
  72.4 1.2 %custom-call.9 = f32[1,16,16]{1,2,0:T(8,128)S(1)} custom-call(f32[1,16,16]{2,1,0:T(8,128)S(1)} %fusion.29), custom_call_target="InvertDiagBlocksLowerTriangular" | custom-call | tf_op jit(solution)/shard_map/jit(_cho_solve)/triangular_solve | solution.py:37
  73.6 0.2 fusion.50
  73.8 0.2 fusion.48
  74.0 0.2 fusion.72
  74.2 0.2 fusion.34
  74.4 0.2 fusion.20
  74.6 0.3 fusion.3
  75.0 1.5 %cholesky.70 = f32[16,16]{1,0:T(8,128)S(1)} custom-call(f32[16,16]{1,0:T(8,128)S(1)} %copy.72), custom_call_target="Cholesky" | custom-call | tf_op jit(solution)/shard_map/jit(cholesky)/cholesky | solution.py:36
  76.5 0.6 compare_reduce_fusion.1
  77.2 0.6 fusion.30
  77.8 1.2 %custom-call.10 = f32[1,16,16]{1,2,0:T(8,128)S(1)} custom-call(f32[1,16,16]{2,1,0:T(8,128)S(1)} %fusion.30), custom_call_target="InvertDiagBlocksLowerTriangular" | custom-call | tf_op jit(solution)/shard_map/jit(_cho_solve)/triangular_solve | solution.py:37
  79.3 0.2 fusion.45
  79.6 0.2 fusion.26
  79.9 0.2 fusion.4
  80.1 0.2 fusion.22
  80.4 1.5 %fusion.8 = f32[16,24,384]{2,0,1:T(8,128)S(1)} fusion(f32[8,16,384]{2,1,0:T(8,128)} %collective-permute-done.3, f32[8,16,384]{2,1,0:T(8,128)S(1)} %fusion.2, f32[8,16,384]{2,1,0:T(8,128)S(1)} %collective-permute-done.2, f32[16,16]{0,1:T(8,128)S(1)} %fusion.48), kind=kOutput, calls=%fused_computation.26 | convolution fusion | flops 28606464 | bytes 1180672 | tf_op jit(solution)/shard_map/pkw,kl->plw/dot_general | solution.py:10
  81.9 1.4 %fusion.76 = (bf16[24,16,384]{2,1,0:T(8,128)(2,1)}, f32[24,16,384]{2,1,0:T(8,128)S(1)}) fusion(f32[16,24,384]{2,0,1:T(8,128)S(1)} %fusion.8, f32[16,16,1]{1,0,2:T(8,128)S(1)} %fusion.7, f32[24,16,384]{2,1,0:T(8,128)S(1)} %constant_dynamic-update-slice_fusion), kind=kOutput, calls=%fused_computation.123 | convolution fusion | flops 28606464 | bytes 2065408 | tf_op jit(solution)/shard_map/pkw,kl->plw/dot_general | solution.py:10
  83.3 1.6 %gather_fusion.1 = bf16[32,16,384]{2,1,0:T(8,128)(2,1)S(1)} fusion(bf16[24,16,384]{2,1,0:T(8,128)(2,1)} %get-tuple-element.8, s32[1024]{0:T(1024)S(1)} %pad_clamp_fusion), kind=kCustom, calls=%fused_computation.1 | custom fusion | bytes 786560 | tf_op jit(solution)/shard_map/gather | solution.py:70
  84.9 6.2 %convolution_bitcast_fusion.3 = f32[8,16,384]{2,1,0:T(8,128)S(1)} fusion(bf16[8,4,16,384]{3,2,1,0:T(8,128)(2,1)S(1)} %bitcast.162, bf16[8,4,384,384]{3,2,1,0:T(8,128)(2,1)} %param.13), kind=kOutput, calls=%fused_computation.10 | convolution fusion | flops 150994944 | bytes 10027008 | tf_op jit(solution)/shard_map/pjvw,pjkw->pkv/dot_general | solution.py:71
  91.1 0.4 convolution_bitcast_fusion.10
  91.5 0.5 fusion.1
  92.0 0.3 convolution_bitcast_fusion.9
  92.5 0.8 reshape.80
  93.3 3.6 %all-to-all-start.3 = ((f32[32,1,512]{2,1,0:T(1,128)}), f32[32,1,512]{2,1,0:T(1,128)S(1)}, u32[]{:S(2)}, u32[]{:S(2)}) async-start(f32[32,1,512]{2,1,0:T(1,128)} %reshape.80), calls=%async_computation.3 | async-start | bytes 131072 | tf_op jit(solution)/shard_map/all_to_all | solution.py:15
  96.9 0.2 fusion.60
  97.2 6.9 %all-to-all-done.3 = f32[32,1,512]{2,1,0:T(1,128)S(1)} async-done(((f32[32,1,512]{2,1,0:T(1,128)}), f32[32,1,512]{2,1,0:T(1,128)S(1)}, u32[]{:S(2)}, u32[]{:S(2)}) %all-to-all-start.3) | async-done | bytes 65568 | tf_op jit(solution)/shard_map/all_to_all | solution.py:15
  104.1 0.8 reduce.5
  105.2 1.5 %cholesky.81 = f32[16,16]{1,0:T(8,128)S(1)} custom-call(f32[16,16]{1,0:T(8,128)S(1)} %fusion.39), custom_call_target="Cholesky" | custom-call | tf_op jit(solution)/shard_map/jit(cholesky)/cholesky | solution.py:36
  106.7 0.6 compare_reduce_fusion
  107.4 0.6 fusion.31
  108.0 1.2 %custom-call.11 = f32[1,16,16]{1,2,0:T(8,128)S(1)} custom-call(f32[1,16,16]{2,1,0:T(8,128)S(1)} %fusion.31), custom_call_target="InvertDiagBlocksLowerTriangular" | custom-call | tf_op jit(solution)/shard_map/jit(_cho_solve)/triangular_solve | solution.py:37
  109.2 0.2 fusion.32
  109.5 0.2 fusion.36
  109.7 0.8 fusion.5
  110.5 0.8 fusion.6
  (49 shorter events, 2.4 us)
Async XLA Ops:
  0.6 10.6 %copy-start = (f32[8,64,384]{2,1,0:T(8,128)S(1)}, f32[8,64,384]{2,1,0:T(8,128)}, u32[]{:S(2)}) copy-start(f32[8,64,384]{2,1,0:T(8,128)} %param.15) | copy-start | bytes 2359300
  2.2 18.0 %all-to-all-start = ((f32[8,8,2,384]{3,2,1,0:T(2,128)}), f32[8,8,2,384]{3,2,1,0:T(2,128)S(1)}, u32[]{:S(2)}, u32[]{:S(2)}) async-start(f32[8,8,2,384]{3,2,1,0:T(2,128)} %broadcast_in_dim.10), calls=%async_computation | async-start | bytes 393216 | tf_op jit(solution)/shard_map/all_to_all | solution.py:15
  21.9 17.2 %all-to-all-start.1 = ((f32[32,1,1024]{2,1,0:T(1,128)}), f32[32,1,1024]{2,1,0:T(1,128)S(1)}, u32[]{:S(2)}, u32[]{:S(2)}) async-start(f32[32,1,1024]{2,1,0:T(1,128)} %reshape.78), calls=%async_computation.1 | async-start | bytes 262144 | tf_op jit(solution)/shard_map/all_to_all | solution.py:15
  32.3 10.4 %collective-permute-start = (f32[8,16,384]{2,1,0:T(8,128)S(1)}, f32[8,16,384]{2,1,0:T(8,128)}, u32[]{:S(2)}, u32[]{:S(2)}) collective-permute-start(f32[8,16,384]{2,1,0:T(8,128)S(1)} %reshape.37), channel_id=1, source_target_pairs={{0,8},{8,16},{16,24},{24,32},{32,40},{40,48},{48,56},{56,64},{64,7... | collective-permute-start | bytes 589832 | tf_op jit(solution)/shard_map/ppermute | solution.py:30
  34.0 9.7 %collective-permute-start.1 = (f32[8,16,384]{2,1,0:T(8,128)S(1)}, f32[8,16,384]{2,1,0:T(8,128)S(1)}, u32[]{:S(2)}, u32[]{:S(2)}) collective-permute-start(f32[8,16,384]{2,1,0:T(8,128)S(1)} %reshape.37), channel_id=1, source_target_pairs={{8,0},{16,8},{24,16},{32,24},{40,32},{48,40},{56,48},{64,56},{72,6... | collective-permute-start | bytes 589832 | tf_op jit(solution)/shard_map/ppermute | solution.py:31
  46.8 27.6 %copy-start.2 = (s32[1,4]{1,0:T(1,128)S(1)}, s32[1,4]{1,0:T(1,128)}, u32[]{:S(2)}) copy-start(s32[1,4]{1,0:T(1,128)} %param.17) | copy-start | bytes 52
  46.8 33.3 %copy-start.1 = (f32[1,4,64,64]{3,2,1,0:T(8,128)S(1)}, f32[1,4,64,64]{3,2,1,0:T(8,128)}, u32[]{:S(2)}) copy-start(f32[1,4,64,64]{3,2,1,0:T(8,128)} %param.18) | copy-start | bytes 196612
  55.8 13.3 %all-to-all-start.2 = ((f32[32,16,128]{2,1,0:T(8,128)}), f32[32,16,128]{2,1,0:T(8,128)S(1)}, u32[]{:S(2)}, u32[]{:S(2)}) async-start(f32[32,16,128]{2,1,0:T(8,128)} %broadcast_in_dim.13), calls=%async_computation.2 | async-start | bytes 524288 | tf_op jit(solution)/shard_map/all_to_all | solution.py:15
  59.7 20.6 %collective-permute-start.2 = (f32[8,16,384]{2,1,0:T(8,128)S(1)}, f32[8,16,384]{2,1,0:T(8,128)S(1)}, u32[]{:S(2)}, u32[]{:S(2)}) collective-permute-start(f32[8,16,384]{2,1,0:T(8,128)S(1)} %fusion.2), channel_id=1, source_target_pairs={{0,8},{8,16},{16,24},{24,32},{32,40},{40,48},{48,56},{56,64},{64,7... | collective-permute-start | bytes 589832 | tf_op jit(solution)/shard_map/ppermute | solution.py:30
  61.4 18.9 %collective-permute-start.3 = (f32[8,16,384]{2,1,0:T(8,128)S(1)}, f32[8,16,384]{2,1,0:T(8,128)}, u32[]{:S(2)}, u32[]{:S(2)}) collective-permute-start(f32[8,16,384]{2,1,0:T(8,128)S(1)} %fusion.2), channel_id=1, source_target_pairs={{8,0},{16,8},{24,16},{32,24},{40,32},{48,40},{56,48},{64,56},{72,6... | collective-permute-start | bytes 589832 | tf_op jit(solution)/shard_map/ppermute | solution.py:31
  93.3 10.8 %all-to-all-start.3 = ((f32[32,1,512]{2,1,0:T(1,128)}), f32[32,1,512]{2,1,0:T(1,128)S(1)}, u32[]{:S(2)}, u32[]{:S(2)}) async-start(f32[32,1,512]{2,1,0:T(1,128)} %reshape.80), calls=%async_computation.3 | async-start | bytes 131072 | tf_op jit(solution)/shard_map/all_to_all | solution.py:15

commit v2 on v1

v2 whole, which is shorter than its diff:
```python
import functools

import jax
import jax.numpy as jnp
from jax import lax
from jax.experimental import pallas as pl
from jax.experimental.pallas import tpu as pltpu
from jax.sharding import PartitionSpec as P

HIGH = lax.Precision.HIGHEST
F32 = jnp.float32
BF16 = jnp.bfloat16
MIB = 1024 * 1024

K = 16
W = 384
E = 64
NB = 4
FL = 4
PD = 8
ROWS = PD * K

SMEM = pl.BlockSpec(memory_space=pltpu.SMEM)
VMEM = pl.BlockSpec(memory_space=pltpu.VMEM)
ANY = pl.BlockSpec(memory_space=pl.ANY)


def shape(*dims, dtype=F32):
    return jax.ShapeDtypeStruct(dims, dtype)


def nn(left, right):
    return jnp.dot(left, right, precision=HIGH, preferred_element_type=F32)


def nt(left, right):
    return lax.dot_general(
        left, right, (((1,), (1,)), ((), ())), precision=HIGH, preferred_element_type=F32
    )


def iotas(rows, cols):
    return (
        lax.broadcasted_iota(jnp.int32, (rows, cols), 0),
        lax.broadcasted_iota(jnp.int32, (rows, cols), 1),
    )


def inverse(matrix):
    row, lane = iotas(K, 2 * K)
    eye = jnp.where(lane == row + K, 1.0, 0.0).astype(F32)
    work = jnp.concatenate([matrix, eye[:, K:]], axis=1)
    for i in range(K):
        pivot = work[i : i + 1, :] / work[i : i + 1, i : i + 1]
        work = jnp.where(row == i, pivot, work - work[:, i : i + 1] * pivot)
    return work[:, K:]


def small(left, right):
    terms = [left[:, k : k + 1] * right[k : k + 1, :] for k in range(K)]
    while len(terms) > 1:
        terms = [a + b for a, b in zip(terms[::2], terms[1::2])]
    return terms[0]


def tiled(matrix):
    wide = jnp.concatenate([matrix, jnp.zeros((K, ROWS - K), F32)], axis=1)
    for step in (K, 2 * K, 4 * K):
        wide = wide + pltpu.roll(wide, step, 1)
    return wide


def block_diagonal(matrix):
    wide = jnp.concatenate([tiled(matrix)] * PD, axis=0)
    row, lane = iotas(ROWS, ROWS)
    return jnp.where(row // K == lane // K, wide, 0.0)


def side_by_side(field):
    return jnp.concatenate([field[p * K : (p + 1) * K] for p in range(PD)], axis=1)


def fetch(near_ref, blocks_ref, sems):
    copies = [
        pltpu.make_async_copy(near_ref.at[p], blocks_ref.at[p], sems.at[p]) for p in range(PD)
    ]
    for copy in copies:
        copy.start()
    return copies


def near_product(copies, ids_ref, blocks_ref, rounded_ref):
    total = None
    for p in range(PD):
        fields = jnp.concatenate([rounded_ref[ids_ref[p, j]] for j in range(NB)], axis=1)
        pieces = [fields]
        if p:
            pieces.insert(0, jnp.zeros((p * K, NB * W), BF16))
        if p + 1 < PD:
            pieces.append(jnp.zeros(((PD - 1 - p) * K, NB * W), BF16))
        fields = jnp.concatenate(pieces, axis=0)
        copies[p].wait()
        blocks = jnp.concatenate([blocks_ref[p, j] for j in range(NB)], axis=1)
        part = lax.dot_general(
            blocks, fields, (((1,), (1,)), ((), ())), preferred_element_type=F32
        )
        total = part if total is None else total + part
    return total


def far_product(down, local_exp):
    pair = jnp.concatenate([local_exp, local_exp], axis=1)
    wide = jnp.concatenate([jnp.concatenate([pair] * (PD // 2), axis=1)] * PD, axis=0)
    row, lane = iotas(ROWS, PD * E)
    return nt(down, jnp.where(row // K == lane // E, wide, 0.0))


def chosen_expansion(far_ref, gathered_ref, table):
    chosen = jnp.concatenate([gathered_ref[far_ref[0, j]] for j in range(FL)], axis=1)
    return nt(chosen, table)


def maps_kernel(up_ref, shift_up_ref, trans_ref, shift_down_ref, down_ref, up_out, table_out, down_out):
    for p in range(PD):
        up_out[:, p * W : (p + 1) * W] = nn(shift_up_ref[p], up_ref[p])
    for q in range(PD // 2):
        pair = [nn(down_ref[2 * q + i], shift_down_ref[2 * q + i]) for i in range(2)]
        down_out[:, q * 2 * E : (q + 1) * 2 * E] = jnp.concatenate(pair, axis=1)
    for j in range(FL):
        table_out[:, j * 2 * E : (j + 1) * 2 * E] = jnp.concatenate(
            [trans_ref[j], jnp.zeros((E, E), F32)], axis=1
        )


def moment_kernel(field_ref, up_ref, out_ref):
    field = side_by_side(field_ref[...].reshape(ROWS, W))
    moment = nt(field, up_ref[...])
    message = jnp.concatenate([moment, jnp.zeros((K, E), F32)], axis=1)
    for i in range(out_ref.shape[0]):
        out_ref[i] = message


def near_kernel(ids_ref, low_ref, own_ref, high_ref, near_ref, out_ref, blocks_ref, rounded_ref, sems):
    copies = fetch(near_ref, blocks_ref, sems)
    for i, ref in enumerate((low_ref, own_ref, high_ref)):
        rounded_ref[i * PD : (i + 1) * PD] = ref[...].astype(BF16)
    out_ref[...] = near_product(copies, ids_ref, blocks_ref, rounded_ref)


def image_kernel(far_ref, gathered_ref, near_ref, field_ref, up_ref, table_ref, down_ref, image_out, local_out, out_ref):
    local_exp = chosen_expansion(far_ref, gathered_ref, table_ref[...])
    local_out[...] = jnp.concatenate([local_exp, jnp.zeros((K, E), F32)], axis=1)
    image = (near_ref[...] + far_product(down_ref[...], local_exp)).T
    image_out[...] = image.reshape(PD, K, W)
    field = side_by_side(field_ref[...].reshape(ROWS, W))
    image = side_by_side(image)
    both = jnp.concatenate([field, image], axis=0)
    grams = nt(both, both)
    moment = nt(image, up_ref[...])
    message = jnp.concatenate(
        [moment, grams[K:, :], grams[:K, :]], axis=1
    )
    for i in range(out_ref.shape[0]):
        out_ref[i] = message


def total_of(gathered_ref):
    parts = [gathered_ref[i] for i in range(gathered_ref.shape[0])]
    while len(parts) > 1:
        parts = [a + b for a, b in zip(parts[::2], parts[1::2])]
    return parts[0]


def direction_kernel(
    ids_ref, far_ref, gathered_ref, f_low, f_own, f_high, q_low, q_own, q_high,
    local_ref, table_ref, down_ref, near_ref,
    out_ref, direction_out, image_out, alpha_out,
    blocks_ref, rounded_ref, sems,
):
    copies = fetch(near_ref, blocks_ref, sems)
    total = total_of(gathered_ref)
    qr = total[:, E : E + K]
    qq = total[:, E + K : E + 2 * K]
    rr = total[:, E + 2 * K : E + 3 * K]
    rq = total[:, E + 3 * K :]
    image_exp = chosen_expansion(far_ref, gathered_ref, table_ref[...])
    curve_inv = inverse(0.5 * (qr + rq))
    rr_inv = inverse(rr)
    alpha = small(curve_inv, rr)
    alpha_t = small(rr, curve_inv)
    following = (
        rr - small(rq, alpha) - small(alpha_t, qr) + small(alpha_t, small(qq, alpha))
    )
    row, lane = iotas(K, K)
    lift_t = small(following, rr_inv) + jnp.where(row == lane, 1.0, 0.0)
    alpha_out[...] = jnp.concatenate([alpha_t, jnp.zeros((K, ROWS - K), F32)], axis=1)
    local_exp = small(lift_t, local_ref[:, :E]) - small(alpha_t, image_exp)

    coeffs = block_diagonal(-alpha_t)
    both = jnp.concatenate([block_diagonal(lift_t), coeffs], axis=1)
    for i, (f, q) in enumerate(((f_low, q_low), (f_own, q_own), (f_high, q_high))):
        pair = jnp.concatenate(
            [f[...].reshape(ROWS, W), q[...].reshape(ROWS, W)], axis=0
        )
        mixed = nn(both, pair)
        if i == 1:
            direction = mixed
            residual = f_own[...].reshape(ROWS, W) + nn(coeffs, q_own[...].reshape(ROWS, W))
        rounded_ref[i * PD : (i + 1) * PD] = mixed.astype(BF16).reshape(PD, K, W)
    direction_out[...] = direction
    image = near_product(copies, ids_ref, blocks_ref, rounded_ref)
    image = (image + far_product(down_ref[...], local_exp)).T
    image_out[...] = image
    residual = side_by_side(residual)
    grams = nt(
        jnp.concatenate([side_by_side(image), residual], axis=0),
        jnp.concatenate([side_by_side(direction), residual], axis=0),
    )
    message = jnp.concatenate(
        [grams[:K, :K], grams[K:, K:], jnp.zeros((K, ROWS - 2 * K), F32)], axis=1
    )
    for i in range(out_ref.shape[0]):
        out_ref[i] = message


def own_coeffs(place, coeffs_t):
    row, lane = iotas(K, K)
    pick = jnp.where(lane == (row % 2) * PD + place, 1.0, 0.0).astype(F32)
    row, lane = iotas(K, ROWS)
    return jnp.where(row // 2 == lane // K, tiled(small(pick, coeffs_t)), 0.0)


def first_step_kernel(place_ref, alpha_ref, field_ref, image_ref, mine_ref, x_out, r_out):
    coeffs = own_coeffs(place_ref[0], alpha_ref[:, :K])
    x_out[...] = nn(coeffs, field_ref[...].reshape(ROWS, W))
    r_out[...] = mine_ref[...].reshape(2 * PD, W) - nn(coeffs, image_ref[...].reshape(ROWS, W))


def last_step_kernel(place_ref, gathered_ref, direction_ref, image_ref, x_ref, r_ref, x_out, r_out):
    total = total_of(gathered_ref)
    qd = total[:, :K]
    alpha_t = small(total[:, K : 2 * K], inverse(0.5 * (qd + qd.T)))
    coeffs = own_coeffs(place_ref[0], alpha_t)
    x = x_ref[...] + nn(coeffs, direction_ref[...])
    r = r_ref[...] - nn(coeffs, image_ref[...])
    for p in range(PD):
        x_out[p] = x[2 * p : 2 * p + 2]
        r_out[p] = r[2 * p : 2 * p + 2]


def call(kernel, in_specs, out_shape, scratch=(), limit=24, cost=1):
    many = isinstance(out_shape, (tuple, list))
    return pl.pallas_call(
        kernel,
        in_specs=in_specs,
        out_specs=tuple(VMEM for _ in out_shape) if many else VMEM,
        out_shape=out_shape,
        scratch_shapes=scratch,
        compiler_params=pltpu.CompilerParams(vmem_limit_bytes=limit * MIB),
        cost_estimate=pl.CostEstimate(flops=cost * 1_000_000, bytes_accessed=1_000_000, transcendentals=0),
        name=kernel.__name__,
    )


NEAR_SCRATCH = (
    pltpu.VMEM((PD, NB, W, W), BF16),
    pltpu.VMEM((3 * PD, K, W), BF16),
    pltpu.SemaphoreType.DMA((PD,)),
)


def swap(array, axis):
    return lax.all_to_all(array, axis, 0, 0, tiled=True)


def halo(block, axis):
    count = lax.axis_size(axis)
    forward = [(i, (i + 1) % count) for i in range(count)]
    backward = [(target, source) for source, target in forward]
    return lax.ppermute(block, axis, forward), lax.ppermute(block, axis, backward)


def on_device(
    rhs_vectors,
    near_blocks,
    neighbours,
    up_maps,
    shift_up,
    far_lists,
    translations,
    shift_down,
    down_maps,
):
    count = lax.axis_size("patch")
    depth = lax.axis_size("rhs")
    place = lax.axis_index("rhs").astype(jnp.int32).reshape(1)
    first = lax.axis_index("patch") * PD - PD
    ids = jnp.mod(neighbours - first, PD * count)

    parts = swap(jnp.broadcast_to(rhs_vectors[None], (depth, *rhs_vectors.shape)), "rhs")
    field = parts.transpose(1, 2, 0, 3).reshape(PD, K, W)

    up, table, down = call(
        maps_kernel,
        [VMEM] * 5,
        (shape(E, PD * W), shape(E, FL * 2 * E), shape(W, PD * E)),
    )(up_maps, shift_up, translations[0], shift_down, down_maps)

    message = call(moment_kernel, [VMEM] * 2, shape(count, K, ROWS))(field, up)
    f_low, f_high = halo(field, "patch")
    gathered = swap(message, "patch")
    near = call(near_kernel, [SMEM] + [VMEM] * 3 + [ANY], shape(W, ROWS), NEAR_SCRATCH)(
        ids, f_low, field, f_high, near_blocks
    )
    image, local_exp, message = call(
        image_kernel,
        [SMEM] + [VMEM] * 6,
        (shape(PD, K, W), shape(K, 2 * E), shape(count, K, ROWS)),
    )(far_lists, gathered, near, field, up, table, down)

    q_low, q_high = halo(image, "patch")
    gathered = swap(message, "patch")
    message, direction, image1, alpha = call(
        direction_kernel,
        [SMEM] * 2 + [VMEM] * 10 + [ANY],
        (shape(count, K, ROWS), shape(ROWS, W), shape(ROWS, W), shape(K, ROWS)),
        NEAR_SCRATCH,
    )(
        ids, far_lists, gathered, f_low, field, f_high, q_low, image, q_high,
        local_exp, table, down, near_blocks,
    )

    gathered = swap(message, "patch")
    x, r = call(first_step_kernel, [SMEM] + [VMEM] * 4, (shape(2 * PD, W),) * 2)(
        place, alpha, field, image, rhs_vectors.reshape(2 * PD, W)
    )
    return call(last_step_kernel, [SMEM] + [VMEM] * 5, (shape(PD, 2, W),) * 2)(
        place, gathered, direction, image1, x, r
    )


def solution(mesh):
    return jax.shard_map(
        on_device,
        mesh=mesh,
        in_specs=(
            P("patch", "rhs", None),
            P("patch", None, None, None),
            P("patch", None),
            P("patch", None, None),
            P("patch", None, None),
            P("patch", None),
            P("patch", None, None, None),
            P("patch", None, None),
            P("patch", None, None),
        ),
        out_specs=(P("patch", "rhs", None), P("patch", "rhs", None)),
        check_vma=False,
    )
```

time: 112 us -> 107 us (0.955)
  Pallas kernels: 0 us -> 31.5 us
  matrix products: 29.7 us -> 0 us
  other arithmetic: 15.5 us -> 0.01 us
  starting transfers between devices: 29.5 us -> 36.2 us
  local copies, waits for them, and re-layouts: 10.9 us -> 15.2 us
  waiting for transfers between devices: 24.9 us -> 22.5 us
    pallas_call x0 -> x7, Pallas kernels: none -> 31.5 us  [the longest x1 13.1 us: on_device(): call(direction_kernel, [SMEM] * 2 + [VMEM] * 10 + [ANY], (shape(count, K,...]
    dot_general x26 -> x0, matrix products: 28.5 us -> none  [the longest x24 15.9 us: einsum(): return jnp.einsum(spec, left, right, precision=HIGH)]
    all_to_all x4, waiting for transfers between devices: 24.8 us -> 11.2 us  [swap(): return lax.all_to_all(array, axis, 0, 0, tiled=True)]
    another operation x15 -> x0, other arithmetic: 12 us -> none  [the longest x9 6.4 us: spd_solve(): factor = jnp.linalg.cholesky(matrix)]
    ppermute x4, waiting for transfers between devices: 0.06 us -> 11.3 us  [the longest x2 6.92 us: halo(): lax.ppermute(block, axis, forward)]
    unnamed x15 -> x18, local copies, waits for them, and re-layouts: 2.97 us -> 13.7 us
    all_to_all x4, starting transfers between devices: 26.1 us -> 32.8 us  [swap(): return lax.all_to_all(array, axis, 0, 0, tiled=True)]
    gather x2 -> x0, local copies, waits for them, and re-layouts: 3.9 us -> none  [near_of(): picked = wide.astype(jnp.bfloat16)[local_ids]]
  transfers between devices with their start and end apart: 8 -> 8, of which waited for: 4 -> 7; matrix products, arithmetic and copies ran while one was open for 18% -> 2% of each run, Pallas kernels for 0% -> 10%
where the time goes in v2:
time: 107 us; the launch traced here: 106 us
  starting transfers between devices  36.2 us (34%)
  Pallas kernels  31.5 us (29%)
  waiting for transfers between devices  22.5 us (21%)
  local copies, waits for them, and re-layouts  15.2 us (14%)
    all_to_all x4, starting transfers between devices, swap(): return lax.all_to_all(array, axis, 0, 0, tiled=True)  32.8 us
    unnamed x18, local copies, waits for them, and re-layouts  13.7 us
    pallas_call x1, Pallas kernels, on_device(): call(direction_kernel, [SMEM] * 2 + [VMEM] * 10 + [ANY], (shape(count, K,...  13.1 us
    all_to_all x4, waiting for transfers between devices, swap(): return lax.all_to_all(array, axis, 0, 0, tiled=True)  11.2 us
    pallas_call x1, Pallas kernels, on_device(): call(near_kernel, [SMEM] + [VMEM] * 3 + [ANY], shape(W, ROWS), NEAR_SCRATCH)  7.73 us
    ppermute x2, waiting for transfers between devices, halo(): lax.ppermute(block, axis, forward)  6.92 us
    ppermute x2, waiting for transfers between devices, halo(): lax.ppermute(block, axis, backward)  4.35 us
    pallas_call x1, Pallas kernels, on_device(): call(image_kernel, [SMEM] + [VMEM] * 6, (shape(PD, K, W), shape(K, 2 * E)...  3.96 us
  transfers between devices with their start and end apart: 8, of which 7 were waited for; matrix products, arithmetic and copies ran while one was open for 2% of the time, Pallas kernels for 10%

profile of v2, /device:TPU:1, one launch (start us, length us, event | category | flops | bytes accessed | tf_op | source)
XLA Modules:
  0.0 106.1 jit_solution(677426253236002605)
XLA Ops:
  0.6 0.0 copy-start.6
  0.6 1.5 %broadcast_in_dim.2 = f32[8,8,2,384]{3,2,1,0:T(2,128)} broadcast(f32[8,2,384]{2,1,0:T(2,128)} %param.9), dimensions={1,2,3} | broadcast | bytes 221184 | tf_op jit(solution)/shard_map/broadcast_in_dim | solution.py:300
  2.1 9.0 %all-to-all-start = ((f32[8,8,2,384]{3,2,1,0:T(2,128)}), f32[8,8,2,384]{3,2,1,0:T(2,128)S(1)}, u32[]{:S(2)}, u32[]{:S(2)}) async-start(f32[8,8,2,384]{3,2,1,0:T(2,128)} %broadcast_in_dim.2), calls=%async_computation | async-start | bytes 393216 | tf_op jit(solution)/shard_map/all_to_all | solution.py:273
  11.1 1.6 %copy.15.down_ref = f32[8,384,64]{2,1,0:T(8,128)S(1)} copy(f32[8,384,64]{1,2,0:T(8,128)} %param.17) | data formatting | bytes 1572864 | tf_op args[8]
  12.7 0.0 copy-start.2
  12.7 1.1 %copy-done.2 = f32[8,64,384]{2,1,0:T(8,128)S(1)} copy-done((f32[8,64,384]{2,1,0:T(8,128)S(1)}, f32[8,64,384]{2,1,0:T(8,128)}, u32[]{:S(2)}) %copy-start.2) | copy-done | bytes 786456
  13.8 0.0 copy-start.3
  13.8 0.9 copy-done.3
  14.8 0.0 copy-start.4
  14.8 0.9 copy-done.4
  15.7 0.0 copy-start.5
  15.8 0.9 copy-done.5
  16.7 2.1 %maps_kernel.1 = (f32[64,3072]{1,0:T(8,128)S(1)}, f32[64,512]{1,0:T(8,128)S(1)}, f32[384,512]{1,0:T(8,128)S(1)}) custom-call(f32[8,64,384]{2,1,0:T(8,128)S(1)} %copy-done.2, f32[8,64,64]{2,1,0:T(8,128)S(1)} %copy-done.3, f32[4,64,64]{2,1,0:T(8,128)S(1)} %bitcast.13, f32[8,64,64]{2,1,0:T(8,128)S(1)} %copy-done.4, f32[8,384,64]{2,1,0:T(8,128)S(1)} %copy.15.down_ref), custom_call_target="tpu_custom_call" | custom-call | flops 1000000 | bytes 1000000 | tf_op jit(solution)/shard_map/maps_kernel/pallas_call | solution.py:303
  18.7 1.4 %all-to-all-done = f32[8,8,2,384]{3,2,1,0:T(2,128)S(1)} async-done(((f32[8,8,2,384]{3,2,1,0:T(2,128)}), f32[8,8,2,384]{3,2,1,0:T(2,128)S(1)}, u32[]{:S(2)}, u32[]{:S(2)}) %all-to-all-start) | async-done | bytes 196640 | tf_op jit(solution)/shard_map/all_to_all | solution.py:273
  20.1 0.1 copy.17
  20.2 1.4 %moment_kernel.1 = f32[32,16,128]{2,1,0:T(8,128)} custom-call(f32[8,16,384]{2,1,0:T(8,128)S(1)} %bitcast.6, f32[64,3072]{1,0:T(8,128)S(1)} %get-tuple-element.14.up_ref), custom_call_target="tpu_custom_call" | custom-call | flops 1000000 | bytes 1000000 | tf_op jit(solution)/shard_map/moment_kernel/pallas_call | solution.py:309
  21.6 9.5 %all-to-all-start.1 = ((f32[32,16,128]{2,1,0:T(8,128)}), f32[32,16,128]{2,1,0:T(8,128)S(1)}, u32[]{:S(2)}, u32[]{:S(2)}) async-start(f32[32,16,128]{2,1,0:T(8,128)} %moment_kernel.1), calls=%async_computation.1 | async-start | bytes 524288 | tf_op jit(solution)/shard_map/all_to_all | solution.py:273
  31.1 0.8 copy.13
  31.9 1.6 %collective-permute-start = (f32[8,16,384]{2,1,0:T(8,128)S(1)}, f32[8,16,384]{2,1,0:T(8,128)S(1)}, u32[]{:S(2)}, u32[]{:S(2)}) collective-permute-start(f32[8,16,384]{2,1,0:T(8,128)S(1)} %bitcast.7), channel_id=1, source_target_pairs={{0,8},{8,16},{16,24},{24,32},{32,40},{40,48},{48,56},{56,64},{64,7... | collective-permute-start | bytes 589832 | tf_op jit(solution)/shard_map/ppermute | solution.py:280
  33.5 0.0 collective-permute-start.1
  33.5 3.1 %collective-permute-done.low_ref.f_low = f32[8,16,384]{2,1,0:T(8,128)S(1)} collective-permute-done((f32[8,16,384]{2,1,0:T(8,128)S(1)}, f32[8,16,384]{2,1,0:T(8,128)S(1)}, u32[]{:S(2)}, u32[]{:S(2)}) %collective-permute-start) | collective-permute-done | bytes 196640 | tf_op jit(solution)/shard_map/ppermute | solution.py:280
  36.7 2.3 %collective-permute-done.1.high_ref.f_high = f32[8,16,384]{2,1,0:T(8,128)S(1)} collective-permute-done((f32[8,16,384]{2,1,0:T(8,128)S(1)}, f32[8,16,384]{2,1,0:T(8,128)S(1)}, u32[]{:S(2)}, u32[]{:S(2)}) %collective-permute-start.1) | collective-permute-done | bytes 196640 | tf_op jit(solution)/shard_map/ppermute | solution.py:280
  38.9 0.0 copy-start
  38.9 3.7 %copy-done = bf16[8,4,384,384]{3,2,1,0:T(8,128)(2,1)S(1)} copy-done((bf16[8,4,384,384]{3,2,1,0:T(8,128)(2,1)S(1)}, bf16[8,4,384,384]{3,2,1,0:T(8,128)(2,1)}, u32[]{:S(2)}) %copy-start) | copy-done | bytes 9437208
  42.6 7.7 %near_kernel.1.near_ref = f32[384,128]{1,0:T(8,128)S(1)} custom-call(s32[8,4]{1,0:T(8,128)S(1)} %add_select_fusion.ids_ref, f32[8,16,384]{2,1,0:T(8,128)S(1)} %collective-permute-done.low_ref.f_low, f32[8,16,384]{2,1,0:T(8,128)S(1)} %bitcast.9, f32[8,16,384]{2,1,0:T(8,128)S(1)} %collective-permute-done.1.high_ref.f_high, bf16[8,4,384,384]{3,2,1,0:T(8,128)(2,1)S(1)} %copy-done), custom_call_target="tpu_custom_call" | custom-call | flops 1000000 | bytes 1000000 | tf_op jit(solution)/shard_map/near_kernel/pallas_call | solution.py:312
  50.3 0.0 copy-start.7
  50.4 0.0 all-to-all-done.1.gathered_ref
  50.4 0.0 copy-done.6
  50.4 4.0 %image_kernel.1 = (f32[8,16,384]{2,1,0:T(8,128)S(1)}, f32[16,128]{1,0:T(8,128)S(1)}, f32[32,16,128]{2,1,0:T(8,128)}) custom-call(s32[1,4]{1,0:T(1,128)S(1)} %copy-done.6, f32[32,16,128]{2,1,0:T(8,128)S(1)} %all-to-all-done.1.gathered_ref, f32[384,128]{1,0:T(8,128)S(1)} %near_kernel.1.near_ref, f32[8,16,384]{2,1,0:T(8,128)S(1)} %bitcast.10, ...), custom_call_target="tpu_custom_call" | custom-call | flops 1000000 | bytes 1000000 | tf_op jit(solution)/shard_map/image_kernel/pallas_call | solution.py:315
  54.3 8.2 %all-to-all-start.2 = ((f32[32,16,128]{2,1,0:T(8,128)}), f32[32,16,128]{2,1,0:T(8,128)S(1)}, u32[]{:S(2)}, u32[]{:S(2)}) async-start(f32[32,16,128]{2,1,0:T(8,128)} %get-tuple-element.17), calls=%async_computation.2 | async-start | bytes 524288 | tf_op jit(solution)/shard_map/all_to_all | solution.py:273
  62.5 1.7 %collective-permute-start.2 = (f32[8,16,384]{2,1,0:T(8,128)S(1)}, f32[8,16,384]{2,1,0:T(8,128)S(1)}, u32[]{:S(2)}, u32[]{:S(2)}) collective-permute-start(f32[8,16,384]{2,1,0:T(8,128)S(1)} %get-tuple-element.18.q_own.image_ref), channel_id=1, source_target_pairs={{0,8},{8,16},{16,24},{24,32},{32,40},{40,48},{48,56},{56,64},{64,7... | collective-permute-start | bytes 589832 | tf_op jit(solution)/shard_map/ppermute | solution.py:280
  64.2 0.0 collective-permute-start.3
  64.2 3.8 %collective-permute-done.2.q_low = f32[8,16,384]{2,1,0:T(8,128)S(1)} collective-permute-done((f32[8,16,384]{2,1,0:T(8,128)S(1)}, f32[8,16,384]{2,1,0:T(8,128)S(1)}, u32[]{:S(2)}, u32[]{:S(2)}) %collective-permute-start.2) | collective-permute-done | bytes 196640 | tf_op jit(solution)/shard_map/ppermute | solution.py:280
  68.0 2.1 %collective-permute-done.3.q_high = f32[8,16,384]{2,1,0:T(8,128)S(1)} collective-permute-done((f32[8,16,384]{2,1,0:T(8,128)S(1)}, f32[8,16,384]{2,1,0:T(8,128)S(1)}, u32[]{:S(2)}, u32[]{:S(2)}) %collective-permute-start.3) | collective-permute-done | bytes 196640 | tf_op jit(solution)/shard_map/ppermute | solution.py:280
  70.1 1.6 %all-to-all-done.2.gathered_ref = f32[32,16,128]{2,1,0:T(8,128)S(1)} async-done(((f32[32,16,128]{2,1,0:T(8,128)}), f32[32,16,128]{2,1,0:T(8,128)S(1)}, u32[]{:S(2)}, u32[]{:S(2)}) %all-to-all-start.2) | async-done | bytes 262176 | tf_op jit(solution)/shard_map/all_to_all | solution.py:273
  71.8 0.0 copy-start.1
  71.8 3.7 %copy-done.1 = bf16[8,4,384,384]{3,2,1,0:T(8,128)(2,1)S(1)} copy-done((bf16[8,4,384,384]{3,2,1,0:T(8,128)(2,1)S(1)}, bf16[8,4,384,384]{3,2,1,0:T(8,128)(2,1)}, u32[]{:S(2)}) %copy-start.1) | copy-done | bytes 9437208
  75.4 13.1 %direction_kernel.1 = (f32[32,16,128]{2,1,0:T(8,128)}, f32[128,384]{1,0:T(8,128)S(1)}, f32[128,384]{1,0:T(8,128)S(1)}, f32[16,128]{1,0:T(8,128)S(1)}) custom-call(s32[8,4]{1,0:T(8,128)S(1)} %add_select_fusion.ids_ref, s32[1,4]{1,0:T(1,128)S(1)} %copy-done.6, f32[32,16,128]{2,1,0:T(8,128)S(1)} %all-to-all-done.2.gathered_ref, ...), custom_call_target="tpu_custom_call" | custom-call | flops 1000000 | bytes 1000000 | tf_op jit(solution)/shard_map/direction_kernel/pallas_call | solution.py:323
  88.5 6.1 %all-to-all-start.3 = ((f32[32,16,128]{2,1,0:T(8,128)}), f32[32,16,128]{2,1,0:T(8,128)S(1)}, u32[]{:S(2)}, u32[]{:S(2)}) async-start(f32[32,16,128]{2,1,0:T(8,128)} %get-tuple-element.20), calls=%async_computation.3 | async-start | bytes 524288 | tf_op jit(solution)/shard_map/all_to_all | solution.py:273
  94.7 0.0 copy-done.7
  94.7 0.6 first_step_kernel.1
  95.3 8.2 %all-to-all-done.3.gathered_ref = f32[32,16,128]{2,1,0:T(8,128)S(1)} async-done(((f32[32,16,128]{2,1,0:T(8,128)}), f32[32,16,128]{2,1,0:T(8,128)S(1)}, u32[]{:S(2)}, u32[]{:S(2)}) %all-to-all-start.3) | async-done | bytes 262176 | tf_op jit(solution)/shard_map/all_to_all | solution.py:273
  103.6 2.6 %last_step_kernel.1 = (f32[8,2,384]{2,1,0:T(2,128)}, f32[8,2,384]{2,1,0:T(2,128)}) custom-call(s32[1]{0:T(128)} %bitcast.place_ref, f32[32,16,128]{2,1,0:T(8,128)S(1)} %all-to-all-done.3.gathered_ref, f32[128,384]{1,0:T(8,128)S(1)} %get-tuple-element.21.direction_ref, f32[128,384]{1,0:T(8,128)S(1)} %get-tuple-element.22.image_ref, ...), custom_call_target="tpu_custom_call" | custom-call | flops 1000000 | bytes 1000000 | tf_op jit(solution)/shard_map/last_step_kernel/pallas_call | solution.py:337
  (2 shorter events, 0.0 us)
Async XLA Ops:
  0.6 49.7 %copy-start.6 = (s32[1,4]{1,0:T(1,128)S(1)}, s32[1,4]{1,0:T(1,128)}, u32[]{:S(2)}) copy-start(s32[1,4]{1,0:T(1,128)} %far_ref.3) | copy-start | bytes 52
  2.1 18.0 %all-to-all-start = ((f32[8,8,2,384]{3,2,1,0:T(2,128)}), f32[8,8,2,384]{3,2,1,0:T(2,128)S(1)}, u32[]{:S(2)}, u32[]{:S(2)}) async-start(f32[8,8,2,384]{3,2,1,0:T(2,128)} %broadcast_in_dim.2), calls=%async_computation | async-start | bytes 393216 | tf_op jit(solution)/shard_map/all_to_all | solution.py:273
  12.7 1.1 %copy-start.2 = (f32[8,64,384]{2,1,0:T(8,128)S(1)}, f32[8,64,384]{2,1,0:T(8,128)}, u32[]{:S(2)}) copy-start(f32[8,64,384]{2,1,0:T(8,128)} %up_ref.1) | copy-start | bytes 2359300
  13.8 0.9 copy-start.3
  14.8 0.9 copy-start.4
  15.7 0.9 copy-start.5
  21.6 28.7 %all-to-all-start.1 = ((f32[32,16,128]{2,1,0:T(8,128)}), f32[32,16,128]{2,1,0:T(8,128)S(1)}, u32[]{:S(2)}, u32[]{:S(2)}) async-start(f32[32,16,128]{2,1,0:T(8,128)} %moment_kernel.1), calls=%async_computation.1 | async-start | bytes 524288 | tf_op jit(solution)/shard_map/all_to_all | solution.py:273
  31.9 4.8 %collective-permute-start = (f32[8,16,384]{2,1,0:T(8,128)S(1)}, f32[8,16,384]{2,1,0:T(8,128)S(1)}, u32[]{:S(2)}, u32[]{:S(2)}) collective-permute-start(f32[8,16,384]{2,1,0:T(8,128)S(1)} %bitcast.7), channel_id=1, source_target_pairs={{0,8},{8,16},{16,24},{24,32},{32,40},{40,48},{48,56},{56,64},{64,7... | collective-permute-start | bytes 589832 | tf_op jit(solution)/shard_map/ppermute | solution.py:280
  33.5 5.4 %collective-permute-start.1 = (f32[8,16,384]{2,1,0:T(8,128)S(1)}, f32[8,16,384]{2,1,0:T(8,128)S(1)}, u32[]{:S(2)}, u32[]{:S(2)}) collective-permute-start(f32[8,16,384]{2,1,0:T(8,128)S(1)} %bitcast.8), channel_id=1, source_target_pairs={{8,0},{16,8},{24,16},{32,24},{40,32},{48,40},{56,48},{64,56},{72,6... | collective-permute-start | bytes 589832 | tf_op jit(solution)/shard_map/ppermute | solution.py:280
  38.9 3.7 %copy-start = (bf16[8,4,384,384]{3,2,1,0:T(8,128)(2,1)S(1)}, bf16[8,4,384,384]{3,2,1,0:T(8,128)(2,1)}, u32[]{:S(2)}) copy-start(bf16[8,4,384,384]{3,2,1,0:T(8,128)(2,1)} %near_ref.3) | copy-start | bytes 28311556
  50.3 44.3 %copy-start.7 = (f32[8,2,384]{2,1,0:T(2,128)S(1)}, f32[8,2,384]{2,1,0:T(2,128)}, u32[]{:S(2)}) copy-start(f32[8,2,384]{2,1,0:T(2,128)} %param.9) | copy-start | bytes 73732
  54.3 17.4 %all-to-all-start.2 = ((f32[32,16,128]{2,1,0:T(8,128)}), f32[32,16,128]{2,1,0:T(8,128)S(1)}, u32[]{:S(2)}, u32[]{:S(2)}) async-start(f32[32,16,128]{2,1,0:T(8,128)} %get-tuple-element.17), calls=%async_computation.2 | async-start | bytes 524288 | tf_op jit(solution)/shard_map/all_to_all | solution.py:273
  62.5 5.5 %collective-permute-start.2 = (f32[8,16,384]{2,1,0:T(8,128)S(1)}, f32[8,16,384]{2,1,0:T(8,128)S(1)}, u32[]{:S(2)}, u32[]{:S(2)}) collective-permute-start(f32[8,16,384]{2,1,0:T(8,128)S(1)} %get-tuple-element.18.q_own.image_ref), channel_id=1, source_target_pairs={{0,8},{8,16},{16,24},{24,32},{32,40},{40,48},{48,56},{56,64},{64,7... | collective-permute-start | bytes 589832 | tf_op jit(solution)/shard_map/ppermute | solution.py:280
  64.2 5.9 %collective-permute-start.3 = (f32[8,16,384]{2,1,0:T(8,128)S(1)}, f32[8,16,384]{2,1,0:T(8,128)S(1)}, u32[]{:S(2)}, u32[]{:S(2)}) collective-permute-start(f32[8,16,384]{2,1,0:T(8,128)S(1)} %get-tuple-element.18.q_own.image_ref), channel_id=1, source_target_pairs={{8,0},{16,8},{24,16},{32,24},{40,32},{48,40},{56,48},{64,56},{72,6... | collective-permute-start | bytes 589832 | tf_op jit(solution)/shard_map/ppermute | solution.py:280
  71.8 3.7 %copy-start.1 = (bf16[8,4,384,384]{3,2,1,0:T(8,128)(2,1)S(1)}, bf16[8,4,384,384]{3,2,1,0:T(8,128)(2,1)}, u32[]{:S(2)}) copy-start(bf16[8,4,384,384]{3,2,1,0:T(8,128)(2,1)} %near_ref.3) | copy-start | bytes 28311556
  88.5 15.0 %all-to-all-start.3 = ((f32[32,16,128]{2,1,0:T(8,128)}), f32[32,16,128]{2,1,0:T(8,128)S(1)}, u32[]{:S(2)}, u32[]{:S(2)}) async-start(f32[32,16,128]{2,1,0:T(8,128)} %get-tuple-element.20), calls=%async_computation.3 | async-start | bytes 524288 | tf_op jit(solution)/shard_map/all_to_all | solution.py:273

commit v3 on v2

--- a/solution.py
+++ b/solution.py
@@ -1,11 +1,10 @@
-import functools
-
 import jax
 import jax.numpy as jnp
 from jax import lax
 from jax.experimental import pallas as pl
 from jax.experimental.pallas import tpu as pltpu
 from jax.sharding import PartitionSpec as P
+
 
 HIGH = lax.Precision.HIGHEST
 F32 = jnp.float32
@@ -22,7 +21,7 @@
 
 SMEM = pl.BlockSpec(memory_space=pltpu.SMEM)
 VMEM = pl.BlockSpec(memory_space=pltpu.VMEM)
-ANY = pl.BlockSpec(memory_space=pl.ANY)
+HBM = pl.BlockSpec(memory_space=pltpu.HBM)
 
 
 def shape(*dims, dtype=F32):
@@ -116,15 +115,48 @@
 
 
 def chosen_expansion(far_ref, gathered_ref, table):
-    chosen = jnp.concatenate([gathered_ref[far_ref[0, j]] for j in range(FL)], axis=1)
-    return nt(chosen, table)
-
-
-def maps_kernel(up_ref, shift_up_ref, trans_ref, shift_down_ref, down_ref, up_out, table_out, down_out):
+    chosen = []
+    for j in range(FL):
+        moment = gathered_ref[far_ref[0, j]]
+        if moment.shape[0] < K:
+            moment = jnp.concatenate([moment, pltpu.roll(moment, E, 1)], axis=0)
+        chosen.append(moment)
+    return nt(jnp.concatenate(chosen, axis=1), table)
+
+
+def spread_kernel(mine_ref, out_ref, sem):
+    copies = [
+        pltpu.make_async_copy(mine_ref, out_ref.at[i], sem.at[i]) for i in range(out_ref.shape[0])
+    ]
+    for copy in copies:
+        copy.start()
+    for copy in copies:
+        copy.wait()
+
+
+def maps_kernel(
+    up_hbm, shift_up_hbm, trans_hbm, shift_down_hbm, down_hbm,
+    up_out, table_out, down_out,
+    up_ref, shift_up_ref, trans_ref, shift_down_ref, down_ref, sems,
+):
+    pairs = (
+        (up_hbm, up_ref),
+        (shift_up_hbm, shift_up_ref),
+        (trans_hbm, trans_ref),
+        (shift_down_hbm, shift_down_ref),
+        (down_hbm, down_ref),
+    )
+    copies = [
+        pltpu.make_async_copy(source, target, sems.at[i]) for i, (source, target) in enumerate(pairs)
+    ]
+    for copy in copies:
+        copy.start()
+    for copy in copies:
+        copy.wait()
     for p in range(PD):
         up_out[:, p * W : (p + 1) * W] = nn(shift_up_ref[p], up_ref[p])
     for q in range(PD // 2):
-        pair = [nn(down_ref[2 * q + i], shift_down_ref[2 * q + i]) for i in range(2)]
+        pair = [nn(down_ref[2 * q + i].T, shift_down_ref[2 * q + i]) for i in range(2)]
         down_out[:, q * 2 * E : (q + 1) * 2 * E] = jnp.concatenate(pair, axis=1)
     for j in range(FL):
         table_out[:, j * 2 * E : (j + 1) * 2 * E] = jnp.concatenate(
@@ -135,7 +167,7 @@
 def moment_kernel(field_ref, up_ref, out_ref):
     field = side_by_side(field_ref[...].reshape(ROWS, W))
     moment = nt(field, up_ref[...])
-    message = jnp.concatenate([moment, jnp.zeros((K, E), F32)], axis=1)
+    message = jnp.concatenate([moment[: K // 2], moment[K // 2 :]], axis=1)
     for i in range(out_ref.shape[0]):
         out_ref[i] = message
 
@@ -147,13 +179,16 @@
     out_ref[...] = near_product(copies, ids_ref, blocks_ref, rounded_ref)
 
 
-def image_kernel(far_ref, gathered_ref, near_ref, field_ref, up_ref, table_ref, down_ref, image_out, local_out, out_ref):
+def image_kernel(far_ref, gathered_ref, near_ref, table_ref, down_ref, image_out, local_out):
     local_exp = chosen_expansion(far_ref, gathered_ref, table_ref[...])
     local_out[...] = jnp.concatenate([local_exp, jnp.zeros((K, E), F32)], axis=1)
     image = (near_ref[...] + far_product(down_ref[...], local_exp)).T
     image_out[...] = image.reshape(PD, K, W)
+
+
+def grams_kernel(field_ref, image_ref, up_ref, out_ref):
     field = side_by_side(field_ref[...].reshape(ROWS, W))
-    image = side_by_side(image)
+    image = side_by_side(image_ref[...].reshape(ROWS, W))
     both = jnp.concatenate([field, image], axis=0)
     grams = nt(both, both)
     moment = nt(image, up_ref[...])
@@ -216,8 +251,9 @@
         jnp.concatenate([side_by_side(image), residual], axis=0),
         jnp.concatenate([side_by_side(direction), residual], axis=0),
     )
+    message = jnp.concatenate([grams[:K, :K], grams[K:, K:]], axis=1)
     message = jnp.concatenate(
-        [grams[:K, :K], grams[K:, K:], jnp.zeros((K, ROWS - 2 * K), F32)], axis=1
+        [message[: K // 2], message[K // 2 :], jnp.zeros((K // 2, ROWS - 4 * K), F32)], axis=1
     )
     for i in range(out_ref.shape[0]):
         out_ref[i] = message
@@ -230,19 +266,24 @@
     return jnp.where(row // 2 == lane // K, tiled(small(pick, coeffs_t)), 0.0)
 
 
-def first_step_kernel(place_ref, alpha_ref, field_ref, image_ref, mine_ref, x_out, r_out):
-    coeffs = own_coeffs(place_ref[0], alpha_ref[:, :K])
-    x_out[...] = nn(coeffs, field_ref[...].reshape(ROWS, W))
-    r_out[...] = mine_ref[...].reshape(2 * PD, W) - nn(coeffs, image_ref[...].reshape(ROWS, W))
-
-
-def last_step_kernel(place_ref, gathered_ref, direction_ref, image_ref, x_ref, r_ref, x_out, r_out):
+def last_step_kernel(
+    place_ref, gathered_ref, alpha_ref, field_ref, image0_ref, direction_ref, image_ref,
+    x_out, r_out,
+):
     total = total_of(gathered_ref)
+    total = jnp.concatenate([total[:, : 2 * K], total[:, 2 * K : 4 * K]], axis=0)
     qd = total[:, :K]
+    row, lane = iotas(K, K)
+    eye = jnp.where(row == lane, 1.0, 0.0).astype(F32)
+    field = field_ref[...].reshape(ROWS, W)
+    mine = own_coeffs(place_ref[0], eye)
+    coeffs0 = own_coeffs(place_ref[0], alpha_ref[:, :K])
+    x = nn(coeffs0, field)
+    r = nn(mine, field) - nn(coeffs0, image0_ref[...].reshape(ROWS, W))
     alpha_t = small(total[:, K : 2 * K], inverse(0.5 * (qd + qd.T)))
     coeffs = own_coeffs(place_ref[0], alpha_t)
-    x = x_ref[...] + nn(coeffs, direction_ref[...])
-    r = r_ref[...] - nn(coeffs, image_ref[...])
+    x = x + nn(coeffs, direction_ref[...])
+    r = r - nn(coeffs, image_ref[...])
     for p in range(PD):
         x_out[p] = x[2 * p : 2 * p + 2]
         r_out[p] = r[2 * p : 2 * p + 2]
@@ -258,7 +299,6 @@
         scratch_shapes=scratch,
         compiler_params=pltpu.CompilerParams(vmem_limit_bytes=limit * MIB),
         cost_estimate=pl.CostEstimate(flops=cost * 1_000_000, bytes_accessed=1_000_000, transcendentals=0),
-        name=kernel.__name__,
     )
 
 
@@ -297,45 +337,62 @@
     first = lax.axis_index("patch") * PD - PD
     ids = jnp.mod(neighbours - first, PD * count)
 
-    parts = swap(jnp.broadcast_to(rhs_vectors[None], (depth, *rhs_vectors.shape)), "rhs")
+    message = call(
+        spread_kernel,
+        [HBM],
+        shape(depth, PD, 2, W),
+        (pltpu.SemaphoreType.DMA((depth,)),),
+        limit=63,
+    )(rhs_vectors)
+    parts = swap(message, "rhs")
     field = parts.transpose(1, 2, 0, 3).reshape(PD, K, W)
 
     up, table, down = call(
         maps_kernel,
-        [VMEM] * 5,
-        (shape(E, PD * W), shape(E, FL * 2 * E), shape(W, PD * E)),
-    )(up_maps, shift_up, translations[0], shift_down, down_maps)
-
-    message = call(moment_kernel, [VMEM] * 2, shape(count, K, ROWS))(field, up)
+        [HBM] * 5,
+        (
+            shape(E, PD * W),
+            shape(E, FL * 2 * E),
+            shape(W, PD * E),
+        ),
+        (
+            pltpu.VMEM((PD, E, W), F32),
+            pltpu.VMEM((PD, E, E), F32),
+            pltpu.VMEM((FL, E, E), F32),
+            pltpu.VMEM((PD, E, E), F32),
+            pltpu.VMEM((PD, E, W), F32),
+            pltpu.SemaphoreType.DMA((5,)),
+        ),
+        limit=53,
+    )(up_maps, shift_up, translations[0], shift_down, down_maps.transpose(0, 2, 1))
+
     f_low, f_high = halo(field, "patch")
+    message = call(moment_kernel, [VMEM] * 2, shape(count, K // 2, ROWS))(field, up)
     gathered = swap(message, "patch")
-    near = call(near_kernel, [SMEM] + [VMEM] * 3 + [ANY], shape(W, ROWS), NEAR_SCRATCH)(
+    near = call(near_kernel, [SMEM] + [VMEM] * 3 + [HBM], shape(W, ROWS), NEAR_SCRATCH, limit=48)(
         ids, f_low, field, f_high, near_blocks
     )
-    image, local_exp, message = call(
-        image_kernel,
-        [SMEM] + [VMEM] * 6,
-        (shape(PD, K, W), shape(K, 2 * E), shape(count, K, ROWS)),
-    )(far_lists, gathered, near, field, up, table, down)
+    image, local_exp = call(
+        image_kernel, [SMEM] + [VMEM] * 4, (shape(PD, K, W), shape(K, 2 * E))
+    )(far_lists, gathered, near, table, down)
 
     q_low, q_high = halo(image, "patch")
+    message = call(grams_kernel, [VMEM] * 3, shape(count, K, ROWS))(field, image, up)
     gathered = swap(message, "patch")
     message, direction, image1, alpha = call(
         direction_kernel,
-        [SMEM] * 2 + [VMEM] * 10 + [ANY],
-        (shape(count, K, ROWS), shape(ROWS, W), shape(ROWS, W), shape(K, ROWS)),
+        [SMEM] * 2 + [VMEM] * 10 + [HBM],
+        (shape(count, K // 2, ROWS), shape(ROWS, W), shape(ROWS, W), shape(K, ROWS)),
         NEAR_SCRATCH,
+        limit=48,
     )(
         ids, far_lists, gathered, f_low, field, f_high, q_low, image, q_high,
         local_exp, table, down, near_blocks,
     )
 
     gathered = swap(message, "patch")
-    x, r = call(first_step_kernel, [SMEM] + [VMEM] * 4, (shape(2 * PD, W),) * 2)(
-        place, alpha, field, image, rhs_vectors.reshape(2 * PD, W)
-    )
-    return call(last_step_kernel, [SMEM] + [VMEM] * 5, (shape(PD, 2, W),) * 2)(
-        place, gathered, direction, image1, x, r
+    return call(last_step_kernel, [SMEM] + [VMEM] * 6, (shape(PD, 2, W),) * 2)(
+        place, gathered, alpha, field, image, direction, image1
     )
 
 

time: 107 us -> 94.3 us (0.88)
  local copies, waits for them, and re-layouts: 15.2 us -> 4.77 us
  waiting for transfers between devices: 22.5 us -> 16.1 us
  Pallas kernels: 31.5 us -> 34 us
  starting transfers between devices: 36.2 us -> 38.1 us
    unnamed x18 -> x15, local copies, waits for them, and re-layouts: 13.7 us -> 4.7 us
    ppermute x2, waiting for transfers between devices: 6.92 us -> 0.01 us  [halo(): lax.ppermute(block, axis, forward)]
    ppermute x2, starting transfers between devices: 0.01 us -> 2.83 us  [halo(): lax.ppermute(block, axis, backward)]
    pallas_call x7 -> x8, Pallas kernels: 31.5 us -> 34 us  [the longest x1 12.5 us: on_device(): call(direction_kernel, [SMEM] * 2 + [VMEM] * 10 + [HBM], (shape(count, K...]
    broadcast_in_dim x1 -> x0, local copies, waits for them, and re-layouts: 1.46 us -> none  [on_device(): jnp.broadcast_to(rhs_vectors[None], (depth, *rhs_vectors.shape))]
    ppermute x2, waiting for transfers between devices: 4.35 us -> 5.63 us  [halo(): lax.ppermute(block, axis, backward)]
  transfers between devices with their start and end apart: 8 -> 8, of which waited for: 7 -> 5; matrix products, arithmetic and copies ran while one was open for 2% -> 1% of each run, Pallas kernels for 10% -> 14%
where the time goes in v3:
time: 94.3 us; the launch traced here: 93.6 us
  starting transfers between devices  38.1 us (40%)
  Pallas kernels  34 us (36%)
  waiting for transfers between devices  16.1 us (17%)
  local copies, waits for them, and re-layouts  4.77 us (5%)
    all_to_all x4, starting transfers between devices, swap(): return lax.all_to_all(array, axis, 0, 0, tiled=True)  32.4 us
    pallas_call x1, Pallas kernels, on_device(): call(direction_kernel, [SMEM] * 2 + [VMEM] * 10 + [HBM], (shape(count, K...  12.5 us
    all_to_all x4, waiting for transfers between devices, swap(): return lax.all_to_all(array, axis, 0, 0, tiled=True)  10.5 us
    pallas_call x1, Pallas kernels, on_device(): call(near_kernel, [SMEM] + [VMEM] * 3 + [HBM], shape(W, ROWS), NEAR_SCRAT...  7.32 us
    ppermute x2, waiting for transfers between devices, halo(): lax.ppermute(block, axis, backward)  5.63 us
    unnamed x15, local copies, waits for them, and re-layouts  4.7 us
    pallas_call x1, Pallas kernels, on_device(): call(maps_kernel, [HBM] * 5, (shape(E, PD * W), shape(E, FL * 2 * E), sha...  4.47 us
    ppermute x2, starting transfers between devices, halo(): lax.ppermute(block, axis, forward)  2.85 us
  transfers between devices with their start and end apart: 8, of which 5 were waited for; matrix products, arithmetic and copies ran while one was open for 1% of the time, Pallas kernels for 14%

profile of v3, /device:TPU:1, one launch (start us, length us, event | category | flops | bytes accessed | tf_op | source)
XLA Modules:
  0.0 93.6 jit_solution(8645360881176088131)
XLA Ops:
  0.6 0.0 copy-start.6
  0.6 1.8 %shard_map.104 = f32[8,8,2,384]{3,2,1,0:T(2,128)} custom-call(f32[8,2,384]{2,1,0:T(2,128)} %mine_ref.1), custom_call_target="tpu_custom_call" | custom-call | flops 1000000 | bytes 1000000 | tf_op jit(solution)/shard_map/pallas_call | solution.py:340
  2.4 9.0 %all-to-all-start = ((f32[8,8,2,384]{3,2,1,0:T(2,128)}), f32[8,8,2,384]{3,2,1,0:T(2,128)S(1)}, u32[]{:S(2)}, u32[]{:S(2)}) async-start(f32[8,8,2,384]{3,2,1,0:T(2,128)} %shard_map.104), calls=%async_computation | async-start | bytes 393216 | tf_op jit(solution)/shard_map/all_to_all | solution.py:313
  11.4 0.8 copy.11
  12.2 0.0 copy-start.3
  12.2 0.9 %copy-done.3 = f32[8,64,64]{2,1,0:T(8,128)S(1)} copy-done((f32[8,64,64]{2,1,0:T(8,128)S(1)}, f32[8,64,64]{2,1,0:T(8,128)}, u32[]{:S(2)}) %copy-start.3) | copy-done | bytes 131096
  13.1 0.0 copy-start.4
  13.1 0.9 %copy-done.4 = f32[8,64,64]{2,1,0:T(8,128)S(1)} copy-done((f32[8,64,64]{2,1,0:T(8,128)S(1)}, f32[8,64,64]{2,1,0:T(8,128)}, u32[]{:S(2)}) %copy-start.4) | copy-done | bytes 131096
  14.1 0.0 copy-start.5
  14.1 0.9 copy-done.5
  15.0 4.5 %shard_map.105 = (f32[64,3072]{1,0:T(8,128)}, f32[64,512]{1,0:T(8,128)S(1)}, f32[384,512]{1,0:T(8,128)}) custom-call(f32[8,64,384]{2,1,0:T(8,128)} %up_hbm.1, f32[8,64,64]{2,1,0:T(8,128)S(1)} %copy-done.3, f32[4,64,64]{2,1,0:T(8,128)S(1)} %bitcast.14, f32[8,64,64]{2,1,0:T(8,128)S(1)} %copy-done.4, f32[8,64,384]{2,1,0:T(8,128)} %bitcast.15), custom_call_target="tpu_custom_call" | custom-call | flops 1000000 | bytes 1000000 | tf_op jit(solution)/shard_map/pallas_call | solution.py:350
  19.5 0.0 copy-start
  19.5 0.9 %all-to-all-done = f32[8,8,2,384]{3,2,1,0:T(2,128)S(1)} async-done(((f32[8,8,2,384]{3,2,1,0:T(2,128)}), f32[8,8,2,384]{3,2,1,0:T(2,128)S(1)}, u32[]{:S(2)}, u32[]{:S(2)}) %all-to-all-start) | async-done | bytes 196640 | tf_op jit(solution)/shard_map/all_to_all | solution.py:313
  20.4 0.1 copy.14
  20.5 2.5 %collective-permute-start.1 = (f32[8,16,384]{2,1,0:T(8,128)S(1)}, f32[8,16,384]{2,1,0:T(8,128)S(1)}, u32[]{:S(2)}, u32[]{:S(2)}) collective-permute-start(f32[8,16,384]{2,1,0:T(8,128)S(1)} %bitcast.7), channel_id=1, source_target_pairs={{8,0},{16,8},{24,16},{32,24},{40,32},{48,40},{56,48},{64,56},{72,6... | collective-permute-start | bytes 589832 | tf_op jit(solution)/shard_map/ppermute | solution.py:320
  23.0 1.2 %collective-permute-start = (f32[8,16,384]{2,1,0:T(8,128)S(1)}, f32[8,16,384]{2,1,0:T(8,128)S(1)}, u32[]{:S(2)}, u32[]{:S(2)}) collective-permute-start(f32[8,16,384]{2,1,0:T(8,128)S(1)} %bitcast.8), channel_id=1, source_target_pairs={{0,8},{8,16},{16,24},{24,32},{32,40},{40,48},{48,56},{56,64},{64,7... | collective-permute-start | bytes 589832 | tf_op jit(solution)/shard_map/ppermute | solution.py:320
  24.2 0.0 copy-start.1
  24.2 1.1 %copy-done.1 = f32[64,3072]{1,0:T(8,128)S(1)} copy-done((f32[64,3072]{1,0:T(8,128)S(1)}, f32[64,3072]{1,0:T(8,128)}, u32[]{:S(2)}) %copy-start.1) | copy-done | bytes 786456
  25.3 0.0 copy-start.2
  25.3 1.5 %shard_map.106 = f32[32,8,128]{2,1,0:T(8,128)} custom-call(f32[8,16,384]{2,1,0:T(8,128)S(1)} %bitcast.9, f32[64,3072]{1,0:T(8,128)S(1)} %copy-done.1), custom_call_target="tpu_custom_call" | custom-call | flops 1000000 | bytes 1000000 | tf_op jit(solution)/shard_map/pallas_call | solution.py:370
  26.8 8.2 %all-to-all-start.1 = ((f32[32,8,128]{2,1,0:T(8,128)}), f32[32,8,128]{2,1,0:T(8,128)S(1)}, u32[]{:S(2)}, u32[]{:S(2)}) async-start(f32[32,8,128]{2,1,0:T(8,128)} %shard_map.106), calls=%async_computation.1 | async-start | bytes 262144 | tf_op jit(solution)/shard_map/all_to_all | solution.py:313
  35.0 0.0 collective-permute-done.1.high_ref.f_high
  35.0 0.0 collective-permute-done.low_ref.f_low
  35.0 7.3 %shard_map.107.near_ref = f32[384,128]{1,0:T(8,128)S(1)} custom-call(s32[8,4]{1,0:T(8,128)S(1)} %add_select_fusion.ids_ref, f32[8,16,384]{2,1,0:T(8,128)S(1)} %collective-permute-done.low_ref.f_low, f32[8,16,384]{2,1,0:T(8,128)S(1)} %bitcast.10, f32[8,16,384]{2,1,0:T(8,128)S(1)} %collective-permute-done.1.high_ref.f_high, bf16[8,4,384,384]{3,2,1,0:T(8,128)(2,1)} %near_ref.3), custom_call_target="tpu_custom_call" | custom-call | flops 1000000 | bytes 1000000 | tf_op jit(solution)/shard_map/pallas_call | solution.py:372
  42.4 0.2 all-to-all-done.1.gathered_ref
  42.6 0.0 copy-done.6
  42.6 0.0 copy-done
  42.6 1.9 %shard_map.108 = (f32[8,16,384]{2,1,0:T(8,128)S(1)}, f32[16,128]{1,0:T(8,128)S(1)}) custom-call(s32[1,4]{1,0:T(1,128)S(1)} %copy-done.6, f32[32,8,128]{2,1,0:T(8,128)S(1)} %all-to-all-done.1.gathered_ref, f32[384,128]{1,0:T(8,128)S(1)} %shard_map.107.near_ref, f32[64,512]{1,0:T(8,128)S(1)} %get-tuple-element.12.table_ref, f32[384,512]{1,0:T(8,128)S(1)} %copy-done), custom_call_target="tpu_custom_call" | custom-call | flops 1000000 | bytes 1000000 | tf_op jit(solution)/shard_map/pallas_call | solution.py:375
  44.5 0.0 copy-done.2
  44.5 1.8 %shard_map.109 = f32[32,16,128]{2,1,0:T(8,128)} custom-call(f32[8,16,384]{2,1,0:T(8,128)S(1)} %bitcast.11, f32[8,16,384]{2,1,0:T(8,128)S(1)} %get-tuple-element.14.image_ref.q_own.image0_ref, f32[64,3072]{1,0:T(8,128)S(1)} %copy-done.2), custom_call_target="tpu_custom_call" | custom-call | flops 1000000 | bytes 1000000 | tf_op jit(solution)/shard_map/pallas_call | solution.py:380
  46.3 7.2 %all-to-all-start.2 = ((f32[32,16,128]{2,1,0:T(8,128)}), f32[32,16,128]{2,1,0:T(8,128)S(1)}, u32[]{:S(2)}, u32[]{:S(2)}) async-start(f32[32,16,128]{2,1,0:T(8,128)} %shard_map.109), calls=%async_computation.2 | async-start | bytes 524288 | tf_op jit(solution)/shard_map/all_to_all | solution.py:313
  53.5 0.3 collective-permute-start.3
  53.8 1.7 %collective-permute-start.2 = (f32[8,16,384]{2,1,0:T(8,128)S(1)}, f32[8,16,384]{2,1,0:T(8,128)S(1)}, u32[]{:S(2)}, u32[]{:S(2)}) collective-permute-start(f32[8,16,384]{2,1,0:T(8,128)S(1)} %get-tuple-element.14.image_ref.q_own.image0_ref), channel_id=1, source_target_pairs={{0,8},{8,16},{16,24},{24,32},{32,40},{40,48},{48,56},{56,64},{64,7... | collective-permute-start | bytes 589832 | tf_op jit(solution)/shard_map/ppermute | solution.py:320
  55.5 5.6 %collective-permute-done.3.q_high = f32[8,16,384]{2,1,0:T(8,128)S(1)} collective-permute-done((f32[8,16,384]{2,1,0:T(8,128)S(1)}, f32[8,16,384]{2,1,0:T(8,128)S(1)}, u32[]{:S(2)}, u32[]{:S(2)}) %collective-permute-start.3) | collective-permute-done | bytes 196640 | tf_op jit(solution)/shard_map/ppermute | solution.py:320
  61.1 0.0 collective-permute-done.2.q_low
  61.1 1.6 %all-to-all-done.2.gathered_ref = f32[32,16,128]{2,1,0:T(8,128)S(1)} async-done(((f32[32,16,128]{2,1,0:T(8,128)}), f32[32,16,128]{2,1,0:T(8,128)S(1)}, u32[]{:S(2)}, u32[]{:S(2)}) %all-to-all-start.2) | async-done | bytes 262176 | tf_op jit(solution)/shard_map/all_to_all | solution.py:313
  62.6 12.5 %shard_map.110 = (f32[32,8,128]{2,1,0:T(8,128)}, f32[128,384]{1,0:T(8,128)S(1)}, f32[128,384]{1,0:T(8,128)S(1)}, f32[16,128]{1,0:T(8,128)S(1)}) custom-call(s32[8,4]{1,0:T(8,128)S(1)} %add_select_fusion.ids_ref, s32[1,4]{1,0:T(1,128)S(1)} %copy-done.6, f32[32,16,128]{2,1,0:T(8,128)S(1)} %all-to-all-done.2.gathered_ref, ...), custom_call_target="tpu_custom_call" | custom-call | flops 1000000 | bytes 1000000 | tf_op jit(solution)/shard_map/pallas_call | solution.py:382
  75.1 8.0 %all-to-all-start.3 = ((f32[32,8,128]{2,1,0:T(8,128)}), f32[32,8,128]{2,1,0:T(8,128)S(1)}, u32[]{:S(2)}, u32[]{:S(2)}) async-start(f32[32,8,128]{2,1,0:T(8,128)} %get-tuple-element.16), calls=%async_computation.3 | async-start | bytes 262144 | tf_op jit(solution)/shard_map/all_to_all | solution.py:313
  83.1 7.7 %all-to-all-done.3.gathered_ref = f32[32,8,128]{2,1,0:T(8,128)S(1)} async-done(((f32[32,8,128]{2,1,0:T(8,128)}), f32[32,8,128]{2,1,0:T(8,128)S(1)}, u32[]{:S(2)}, u32[]{:S(2)}) %all-to-all-start.3) | async-done | bytes 131104 | tf_op jit(solution)/shard_map/all_to_all | solution.py:313
  90.8 2.8 %shard_map.111 = (f32[8,2,384]{2,1,0:T(2,128)}, f32[8,2,384]{2,1,0:T(2,128)}) custom-call(s32[1]{0:T(128)} %bitcast.place_ref, f32[32,8,128]{2,1,0:T(8,128)S(1)} %all-to-all-done.3.gathered_ref, f32[16,128]{1,0:T(8,128)S(1)} %get-tuple-element.17.alpha_ref, f32[8,16,384]{2,1,0:T(8,128)S(1)} %bitcast.13, ...), custom_call_target="tpu_custom_call" | custom-call | flops 1000000 | bytes 1000000 | tf_op jit(solution)/shard_map/pallas_call | solution.py:394
  (1 shorter events, 0.0 us)
Async XLA Ops:
  0.6 42.0 %copy-start.6 = (s32[1,4]{1,0:T(1,128)S(1)}, s32[1,4]{1,0:T(1,128)}, u32[]{:S(2)}) copy-start(s32[1,4]{1,0:T(1,128)} %far_ref.3) | copy-start | bytes 52
  2.4 18.0 %all-to-all-start = ((f32[8,8,2,384]{3,2,1,0:T(2,128)}), f32[8,8,2,384]{3,2,1,0:T(2,128)S(1)}, u32[]{:S(2)}, u32[]{:S(2)}) async-start(f32[8,8,2,384]{3,2,1,0:T(2,128)} %shard_map.104), calls=%async_computation | async-start | bytes 393216 | tf_op jit(solution)/shard_map/all_to_all | solution.py:313
  12.2 0.9 %copy-start.3 = (f32[8,64,64]{2,1,0:T(8,128)S(1)}, f32[8,64,64]{2,1,0:T(8,128)}, u32[]{:S(2)}) copy-start(f32[8,64,64]{2,1,0:T(8,128)} %shift_up_hbm.1) | copy-start | bytes 393220
  13.1 0.9 %copy-start.4 = (f32[8,64,64]{2,1,0:T(8,128)S(1)}, f32[8,64,64]{2,1,0:T(8,128)}, u32[]{:S(2)}) copy-start(f32[8,64,64]{2,1,0:T(8,128)} %shift_down_hbm.1) | copy-start | bytes 393220
  14.1 0.9 copy-start.5
  19.5 23.1 %copy-start = (f32[384,512]{1,0:T(8,128)S(1)}, f32[384,512]{1,0:T(8,128)}, u32[]{:S(2)}) copy-start(f32[384,512]{1,0:T(8,128)} %get-tuple-element.13.down_ref) | copy-start | bytes 2359300
  20.5 14.5 %collective-permute-start.1 = (f32[8,16,384]{2,1,0:T(8,128)S(1)}, f32[8,16,384]{2,1,0:T(8,128)S(1)}, u32[]{:S(2)}, u32[]{:S(2)}) collective-permute-start(f32[8,16,384]{2,1,0:T(8,128)S(1)} %bitcast.7), channel_id=1, source_target_pairs={{8,0},{16,8},{24,16},{32,24},{40,32},{48,40},{56,48},{64,56},{72,6... | collective-permute-start | bytes 589832 | tf_op jit(solution)/shard_map/ppermute | solution.py:320
  23.0 12.0 %collective-permute-start = (f32[8,16,384]{2,1,0:T(8,128)S(1)}, f32[8,16,384]{2,1,0:T(8,128)S(1)}, u32[]{:S(2)}, u32[]{:S(2)}) collective-permute-start(f32[8,16,384]{2,1,0:T(8,128)S(1)} %bitcast.8), channel_id=1, source_target_pairs={{0,8},{8,16},{16,24},{24,32},{32,40},{40,48},{48,56},{56,64},{64,7... | collective-permute-start | bytes 589832 | tf_op jit(solution)/shard_map/ppermute | solution.py:320
  24.2 1.1 %copy-start.1 = (f32[64,3072]{1,0:T(8,128)S(1)}, f32[64,3072]{1,0:T(8,128)}, u32[]{:S(2)}) copy-start(f32[64,3072]{1,0:T(8,128)} %get-tuple-element.11.up_ref) | copy-start | bytes 2359300
  25.3 19.2 %copy-start.2 = (f32[64,3072]{1,0:T(8,128)S(1)}, f32[64,3072]{1,0:T(8,128)}, u32[]{:S(2)}) copy-start(f32[64,3072]{1,0:T(8,128)} %get-tuple-element.11.up_ref) | copy-start | bytes 2359300
  26.8 15.8 %all-to-all-start.1 = ((f32[32,8,128]{2,1,0:T(8,128)}), f32[32,8,128]{2,1,0:T(8,128)S(1)}, u32[]{:S(2)}, u32[]{:S(2)}) async-start(f32[32,8,128]{2,1,0:T(8,128)} %shard_map.106), calls=%async_computation.1 | async-start | bytes 262144 | tf_op jit(solution)/shard_map/all_to_all | solution.py:313
  46.3 16.3 %all-to-all-start.2 = ((f32[32,16,128]{2,1,0:T(8,128)}), f32[32,16,128]{2,1,0:T(8,128)S(1)}, u32[]{:S(2)}, u32[]{:S(2)}) async-start(f32[32,16,128]{2,1,0:T(8,128)} %shard_map.109), calls=%async_computation.2 | async-start | bytes 524288 | tf_op jit(solution)/shard_map/all_to_all | solution.py:313
  53.5 7.6 %collective-permute-start.3 = (f32[8,16,384]{2,1,0:T(8,128)S(1)}, f32[8,16,384]{2,1,0:T(8,128)S(1)}, u32[]{:S(2)}, u32[]{:S(2)}) collective-permute-start(f32[8,16,384]{2,1,0:T(8,128)S(1)} %get-tuple-element.14.image_ref.q_own.image0_ref), channel_id=1, source_target_pairs={{8,0},{16,8},{24,16},{32,24},{40,32},{48,40},{56,48},{64,56},{72,6... | collective-permute-start | bytes 589832 | tf_op jit(solution)/shard_map/ppermute | solution.py:320
  53.8 7.3 %collective-permute-start.2 = (f32[8,16,384]{2,1,0:T(8,128)S(1)}, f32[8,16,384]{2,1,0:T(8,128)S(1)}, u32[]{:S(2)}, u32[]{:S(2)}) collective-permute-start(f32[8,16,384]{2,1,0:T(8,128)S(1)} %get-tuple-element.14.image_ref.q_own.image0_ref), channel_id=1, source_target_pairs={{0,8},{8,16},{16,24},{24,32},{32,40},{40,48},{48,56},{56,64},{64,7... | collective-permute-start | bytes 589832 | tf_op jit(solution)/shard_map/ppermute | solution.py:320
  75.1 15.7 %all-to-all-start.3 = ((f32[32,8,128]{2,1,0:T(8,128)}), f32[32,8,128]{2,1,0:T(8,128)S(1)}, u32[]{:S(2)}, u32[]{:S(2)}) async-start(f32[32,8,128]{2,1,0:T(8,128)} %get-tuple-element.16), calls=%async_computation.3 | async-start | bytes 262144 | tf_op jit(solution)/shard_map/all_to_all | solution.py:313

commit v4 on v3

--- a/solution.py
+++ b/solution.py
@@ -80,15 +80,22 @@
 
 
 def fetch(near_ref, blocks_ref, sems):
-    copies = [
-        pltpu.make_async_copy(near_ref.at[p], blocks_ref.at[p], sems.at[p]) for p in range(PD)
-    ]
-    for copy in copies:
-        copy.start()
-    return copies
-
-
-def near_product(copies, ids_ref, blocks_ref, rounded_ref):
+    def start(p, carry):
+        pltpu.make_async_copy(near_ref.at[p], blocks_ref.at[p], sems.at[p]).start()
+        return carry
+
+    lax.fori_loop(0, PD, start, 0)
+
+
+def fetched(near_ref, blocks_ref, sems):
+    def wait(p, carry):
+        pltpu.make_async_copy(near_ref.at[p], blocks_ref.at[p], sems.at[p]).wait()
+        return carry
+
+    lax.fori_loop(0, PD, wait, 0)
+
+
+def near_product(ids_ref, blocks_ref, rounded_ref):
     total = None
     for p in range(PD):
         fields = jnp.concatenate([rounded_ref[ids_ref[p, j]] for j in range(NB)], axis=1)
@@ -98,7 +105,6 @@
         if p + 1 < PD:
             pieces.append(jnp.zeros(((PD - 1 - p) * K, NB * W), BF16))
         fields = jnp.concatenate(pieces, axis=0)
-        copies[p].wait()
         blocks = jnp.concatenate([blocks_ref[p, j] for j in range(NB)], axis=1)
         part = lax.dot_general(
             blocks, fields, (((1,), (1,)), ((), ())), preferred_element_type=F32
@@ -107,21 +113,26 @@
     return total
 
 
-def far_product(down, local_exp):
-    pair = jnp.concatenate([local_exp, local_exp], axis=1)
-    wide = jnp.concatenate([jnp.concatenate([pair] * (PD // 2), axis=1)] * PD, axis=0)
+def shifted(local_exp, shift_ref):
+    return nt(local_exp, shift_ref[...].reshape(PD * E, E))
+
+
+def far_product(patch_exp, down_ref):
     row, lane = iotas(ROWS, PD * E)
-    return nt(down, jnp.where(row // K == lane // E, wide, 0.0))
-
-
-def chosen_expansion(far_ref, gathered_ref, table):
-    chosen = []
+    wide = jnp.concatenate([patch_exp] * PD, axis=0)
+    wide = jnp.where(row // K == lane // E, wide, 0.0)
+    return nn(wide, down_ref[...].reshape(PD * E, W))
+
+
+def chosen_expansion(far_ref, gathered_ref, table_ref):
+    total = None
     for j in range(FL):
         moment = gathered_ref[far_ref[0, j]]
         if moment.shape[0] < K:
-            moment = jnp.concatenate([moment, pltpu.roll(moment, E, 1)], axis=0)
-        chosen.append(moment)
-    return nt(jnp.concatenate(chosen, axis=1), table)
+            moment = jnp.concatenate([moment[:, :E], moment[:, E:]], axis=0)
+        part = nt(moment[:, :E], table_ref[j])
+        total = part if total is None else total + part
+    return total
 
 
 def spread_kernel(mine_ref, out_ref, sem):
@@ -134,64 +145,38 @@
         copy.wait()
 
 
-def maps_kernel(
-    up_hbm, shift_up_hbm, trans_hbm, shift_down_hbm, down_hbm,
-    up_out, table_out, down_out,
-    up_ref, shift_up_ref, trans_ref, shift_down_ref, down_ref, sems,
-):
-    pairs = (
-        (up_hbm, up_ref),
-        (shift_up_hbm, shift_up_ref),
-        (trans_hbm, trans_ref),
-        (shift_down_hbm, shift_down_ref),
-        (down_hbm, down_ref),
-    )
-    copies = [
-        pltpu.make_async_copy(source, target, sems.at[i]) for i, (source, target) in enumerate(pairs)
-    ]
-    for copy in copies:
-        copy.start()
-    for copy in copies:
-        copy.wait()
+def maps_kernel(up_ref, shift_ref, out_ref):
     for p in range(PD):
-        up_out[:, p * W : (p + 1) * W] = nn(shift_up_ref[p], up_ref[p])
-    for q in range(PD // 2):
-        pair = [nn(down_ref[2 * q + i].T, shift_down_ref[2 * q + i]) for i in range(2)]
-        down_out[:, q * 2 * E : (q + 1) * 2 * E] = jnp.concatenate(pair, axis=1)
-    for j in range(FL):
-        table_out[:, j * 2 * E : (j + 1) * 2 * E] = jnp.concatenate(
-            [trans_ref[j], jnp.zeros((E, E), F32)], axis=1
-        )
+        out_ref[:, p * W : (p + 1) * W] = nn(shift_ref[p], up_ref[p])
 
 
 def moment_kernel(field_ref, up_ref, out_ref):
-    field = side_by_side(field_ref[...].reshape(ROWS, W))
-    moment = nt(field, up_ref[...])
+    moment = nt(side_by_side(field_ref[...].reshape(ROWS, W)), up_ref[...])
     message = jnp.concatenate([moment[: K // 2], moment[K // 2 :]], axis=1)
     for i in range(out_ref.shape[0]):
         out_ref[i] = message
 
 
 def near_kernel(ids_ref, low_ref, own_ref, high_ref, near_ref, out_ref, blocks_ref, rounded_ref, sems):
-    copies = fetch(near_ref, blocks_ref, sems)
+    fetch(near_ref, blocks_ref, sems)
     for i, ref in enumerate((low_ref, own_ref, high_ref)):
         rounded_ref[i * PD : (i + 1) * PD] = ref[...].astype(BF16)
-    out_ref[...] = near_product(copies, ids_ref, blocks_ref, rounded_ref)
-
-
-def image_kernel(far_ref, gathered_ref, near_ref, table_ref, down_ref, image_out, local_out):
-    local_exp = chosen_expansion(far_ref, gathered_ref, table_ref[...])
+    fetched(near_ref, blocks_ref, sems)
+    out_ref[...] = near_product(ids_ref, blocks_ref, rounded_ref).T
+
+
+def image_kernel(far_ref, gathered_ref, near_ref, table_ref, shift_ref, down_ref, image_out, local_out):
+    local_exp = chosen_expansion(far_ref, gathered_ref, table_ref)
     local_out[...] = jnp.concatenate([local_exp, jnp.zeros((K, E), F32)], axis=1)
-    image = (near_ref[...] + far_product(down_ref[...], local_exp)).T
+    image = near_ref[...] + far_product(shifted(local_exp, shift_ref), down_ref)
     image_out[...] = image.reshape(PD, K, W)
 
 
 def grams_kernel(field_ref, image_ref, up_ref, out_ref):
-    field = side_by_side(field_ref[...].reshape(ROWS, W))
     image = side_by_side(image_ref[...].reshape(ROWS, W))
-    both = jnp.concatenate([field, image], axis=0)
+    moment = nt(image, up_ref[...])
+    both = jnp.concatenate([side_by_side(field_ref[...].reshape(ROWS, W)), image], axis=0)
     grams = nt(both, both)
-    moment = nt(image, up_ref[...])
     message = jnp.concatenate(
         [moment, grams[K:, :], grams[:K, :]], axis=1
     )
@@ -208,17 +193,17 @@
 
 def direction_kernel(
     ids_ref, far_ref, gathered_ref, f_low, f_own, f_high, q_low, q_own, q_high,
-    local_ref, table_ref, down_ref, near_ref,
+    local_ref, table_ref, shift_ref, down_ref, near_ref,
     out_ref, direction_out, image_out, alpha_out,
     blocks_ref, rounded_ref, sems,
 ):
-    copies = fetch(near_ref, blocks_ref, sems)
+    fetch(near_ref, blocks_ref, sems)
     total = total_of(gathered_ref)
     qr = total[:, E : E + K]
     qq = total[:, E + K : E + 2 * K]
     rr = total[:, E + 2 * K : E + 3 * K]
     rq = total[:, E + 3 * K :]
-    image_exp = chosen_expansion(far_ref, gathered_ref, table_ref[...])
+    image_exp = chosen_expansion(far_ref, gathered_ref, table_ref)
     curve_inv = inverse(0.5 * (qr + rq))
     rr_inv = inverse(rr)
     alpha = small(curve_inv, rr)
@@ -230,6 +215,7 @@
     lift_t = small(following, rr_inv) + jnp.where(row == lane, 1.0, 0.0)
     alpha_out[...] = jnp.concatenate([alpha_t, jnp.zeros((K, ROWS - K), F32)], axis=1)
     local_exp = small(lift_t, local_ref[:, :E]) - small(alpha_t, image_exp)
+    far = far_product(shifted(local_exp, shift_ref), down_ref)
 
     coeffs = block_diagonal(-alpha_t)
     both = jnp.concatenate([block_diagonal(lift_t), coeffs], axis=1)
@@ -243,8 +229,9 @@
             residual = f_own[...].reshape(ROWS, W) + nn(coeffs, q_own[...].reshape(ROWS, W))
         rounded_ref[i * PD : (i + 1) * PD] = mixed.astype(BF16).reshape(PD, K, W)
     direction_out[...] = direction
-    image = near_product(copies, ids_ref, blocks_ref, rounded_ref)
-    image = (image + far_product(down_ref[...], local_exp)).T
+    fetched(near_ref, blocks_ref, sems)
+    image = near_product(ids_ref, blocks_ref, rounded_ref)
+    image = image.T + far
     image_out[...] = image
     residual = side_by_side(residual)
     grams = nt(
@@ -347,47 +334,32 @@
     parts = swap(message, "rhs")
     field = parts.transpose(1, 2, 0, 3).reshape(PD, K, W)
 
-    up, table, down = call(
-        maps_kernel,
-        [HBM] * 5,
-        (
-            shape(E, PD * W),
-            shape(E, FL * 2 * E),
-            shape(W, PD * E),
-        ),
-        (
-            pltpu.VMEM((PD, E, W), F32),
-            pltpu.VMEM((PD, E, E), F32),
-            pltpu.VMEM((FL, E, E), F32),
-            pltpu.VMEM((PD, E, E), F32),
-            pltpu.VMEM((PD, E, W), F32),
-            pltpu.SemaphoreType.DMA((5,)),
-        ),
-        limit=53,
-    )(up_maps, shift_up, translations[0], shift_down, down_maps.transpose(0, 2, 1))
+    up = call(maps_kernel, [VMEM] * 2, shape(E, PD * W))(up_maps, shift_up)
+    table = translations[0]
+    down = down_maps.transpose(0, 2, 1)
 
     f_low, f_high = halo(field, "patch")
     message = call(moment_kernel, [VMEM] * 2, shape(count, K // 2, ROWS))(field, up)
     gathered = swap(message, "patch")
-    near = call(near_kernel, [SMEM] + [VMEM] * 3 + [HBM], shape(W, ROWS), NEAR_SCRATCH, limit=48)(
+    near = call(near_kernel, [SMEM] + [VMEM] * 3 + [HBM], shape(ROWS, W), NEAR_SCRATCH, limit=48)(
         ids, f_low, field, f_high, near_blocks
     )
     image, local_exp = call(
-        image_kernel, [SMEM] + [VMEM] * 4, (shape(PD, K, W), shape(K, 2 * E))
-    )(far_lists, gathered, near, table, down)
+        image_kernel, [SMEM] + [VMEM] * 5, (shape(PD, K, W), shape(K, 2 * E))
+    )(far_lists, gathered, near, table, shift_down, down)
 
     q_low, q_high = halo(image, "patch")
     message = call(grams_kernel, [VMEM] * 3, shape(count, K, ROWS))(field, image, up)
     gathered = swap(message, "patch")
     message, direction, image1, alpha = call(
         direction_kernel,
-        [SMEM] * 2 + [VMEM] * 10 + [HBM],
+        [SMEM] * 2 + [VMEM] * 11 + [HBM],
         (shape(count, K // 2, ROWS), shape(ROWS, W), shape(ROWS, W), shape(K, ROWS)),
         NEAR_SCRATCH,
         limit=48,
     )(
         ids, far_lists, gathered, f_low, field, f_high, q_low, image, q_high,
-        local_exp, table, down, near_blocks,
+        local_exp, table, shift_down, down, near_blocks,
     )
 
     gathered = swap(message, "patch")

time: 94.3 us -> 89.5 us (0.949)
  Pallas kernels: 34 us -> 26.6 us
  waiting for transfers between devices: 16.1 us -> 20.8 us
  local copies, waits for them, and re-layouts: 4.77 us -> 2.92 us
    pallas_call x4, Pallas kernels: 26.2 us -> 18.8 us  [the longest x1 8.97 us: on_device(): call(direction_kernel, [SMEM] * 2 + [VMEM] * 11 + [HBM], (shape(count, K...]
    all_to_all x4, waiting for transfers between devices: 10.5 us -> 15.2 us  [swap(): return lax.all_to_all(array, axis, 0, 0, tiled=True)]
    unnamed x15 -> x13, local copies, waits for them, and re-layouts: 4.7 us -> 2.86 us
  transfers between devices with their start and end apart: 8 -> 8, of which waited for: 5 -> 5; matrix products, arithmetic and copies ran while one was open for 1% -> 1% of each run, Pallas kernels for 14% -> 10%
where the time goes in v4:
time: 89.5 us; the launch traced here: 89 us
  starting transfers between devices  37.9 us (42%)
  Pallas kernels  26.6 us (30%)
  waiting for transfers between devices  20.8 us (23%)
  local copies, waits for them, and re-layouts  2.92 us (3%)
    all_to_all x4, starting transfers between devices, swap(): return lax.all_to_all(array, axis, 0, 0, tiled=True)  32.2 us
    all_to_all x4, waiting for transfers between devices, swap(): return lax.all_to_all(array, axis, 0, 0, tiled=True)  15.2 us
    pallas_call x1, Pallas kernels, on_device(): call(direction_kernel, [SMEM] * 2 + [VMEM] * 11 + [HBM], (shape(count, K...  8.97 us
    pallas_call x1, Pallas kernels, on_device(): call(near_kernel, [SMEM] + [VMEM] * 3 + [HBM], shape(ROWS, W), NEAR_SCRAT...  7.03 us
    ppermute x2, waiting for transfers between devices, halo(): lax.ppermute(block, axis, backward)  5.63 us
    unnamed x13, local copies, waits for them, and re-layouts  2.86 us
    ppermute x2, starting transfers between devices, halo(): lax.ppermute(block, axis, forward)  2.85 us
    ppermute x2, starting transfers between devices, halo(): lax.ppermute(block, axis, backward)  2.83 us
  transfers between devices with their start and end apart: 8, of which 5 were waited for; matrix products, arithmetic and copies ran while one was open for 1% of the time, Pallas kernels for 10%

profile of v4, /device:TPU:1, one launch (start us, length us, event | category | flops | bytes accessed | tf_op | source)
XLA Modules:
  0.0 89.0 jit_solution(4899333665821844470)
XLA Ops:
  0.6 0.0 copy-start
  0.6 1.8 %shard_map.104 = f32[8,8,2,384]{3,2,1,0:T(2,128)} custom-call(f32[8,2,384]{2,1,0:T(2,128)} %mine_ref.1), custom_call_target="tpu_custom_call" | custom-call | flops 1000000 | bytes 1000000 | tf_op jit(solution)/shard_map/pallas_call | solution.py:327
  2.4 0.0 copy-start.1
  2.4 9.1 %all-to-all-start = ((f32[8,8,2,384]{3,2,1,0:T(2,128)}), f32[8,8,2,384]{3,2,1,0:T(2,128)S(1)}, u32[]{:S(2)}, u32[]{:S(2)}) async-start(f32[8,8,2,384]{3,2,1,0:T(2,128)} %shard_map.104), calls=%async_computation | async-start | bytes 393216 | tf_op jit(solution)/shard_map/all_to_all | solution.py:300
  11.6 0.8 copy.11
  12.3 0.0 copy-start.2
  12.3 1.1 %copy-done.2 = f32[8,64,384]{2,1,0:T(8,128)S(1)} copy-done((f32[8,64,384]{2,1,0:T(8,128)S(1)}, f32[8,64,384]{2,1,0:T(8,128)}, u32[]{:S(2)}) %copy-start.2) | copy-done | bytes 786456
  13.5 0.0 copy-start.4
  13.5 0.9 %copy-done.4 = f32[8,64,64]{2,1,0:T(8,128)S(1)} copy-done((f32[8,64,64]{2,1,0:T(8,128)S(1)}, f32[8,64,64]{2,1,0:T(8,128)}, u32[]{:S(2)}) %copy-start.4) | copy-done | bytes 131096
  14.4 0.0 copy-start.3
  14.4 0.0 copy-start.5
  14.4 0.8 shard_map.105.up_ref
  15.2 5.4 %all-to-all-done = f32[8,8,2,384]{3,2,1,0:T(2,128)S(1)} async-done(((f32[8,8,2,384]{3,2,1,0:T(2,128)}), f32[8,8,2,384]{3,2,1,0:T(2,128)S(1)}, u32[]{:S(2)}, u32[]{:S(2)}) %all-to-all-start) | async-done | bytes 196640 | tf_op jit(solution)/shard_map/all_to_all | solution.py:300
  20.6 0.1 copy.14
  20.6 2.5 %collective-permute-start.1 = (f32[8,16,384]{2,1,0:T(8,128)S(1)}, f32[8,16,384]{2,1,0:T(8,128)S(1)}, u32[]{:S(2)}, u32[]{:S(2)}) collective-permute-start(f32[8,16,384]{2,1,0:T(8,128)S(1)} %bitcast.7), channel_id=1, source_target_pairs={{8,0},{16,8},{24,16},{32,24},{40,32},{48,40},{56,48},{64,56},{72,6... | collective-permute-start | bytes 589832 | tf_op jit(solution)/shard_map/ppermute | solution.py:307
  23.1 1.2 %collective-permute-start = (f32[8,16,384]{2,1,0:T(8,128)S(1)}, f32[8,16,384]{2,1,0:T(8,128)S(1)}, u32[]{:S(2)}, u32[]{:S(2)}) collective-permute-start(f32[8,16,384]{2,1,0:T(8,128)S(1)} %bitcast.8), channel_id=1, source_target_pairs={{0,8},{8,16},{16,24},{24,32},{32,40},{40,48},{48,56},{56,64},{64,7... | collective-permute-start | bytes 589832 | tf_op jit(solution)/shard_map/ppermute | solution.py:307
  24.3 1.5 %shard_map.106 = f32[32,8,128]{2,1,0:T(8,128)} custom-call(f32[8,16,384]{2,1,0:T(8,128)S(1)} %bitcast.9, f32[64,3072]{1,0:T(8,128)S(1)} %shard_map.105.up_ref), custom_call_target="tpu_custom_call" | custom-call | flops 1000000 | bytes 1000000 | tf_op jit(solution)/shard_map/pallas_call | solution.py:342
  25.8 8.2 %all-to-all-start.1 = ((f32[32,8,128]{2,1,0:T(8,128)}), f32[32,8,128]{2,1,0:T(8,128)S(1)}, u32[]{:S(2)}, u32[]{:S(2)}) async-start(f32[32,8,128]{2,1,0:T(8,128)} %shard_map.106), calls=%async_computation.1 | async-start | bytes 262144 | tf_op jit(solution)/shard_map/all_to_all | solution.py:300
  34.0 0.0 collective-permute-done.1.high_ref.f_high
  34.0 0.0 collective-permute-done.low_ref.f_low
  34.0 7.0 %shard_map.107.near_ref = f32[128,384]{1,0:T(8,128)S(1)} custom-call(s32[8,4]{1,0:T(8,128)S(1)} %add_select_fusion.ids_ref, f32[8,16,384]{2,1,0:T(8,128)S(1)} %collective-permute-done.low_ref.f_low, f32[8,16,384]{2,1,0:T(8,128)S(1)} %bitcast.10, f32[8,16,384]{2,1,0:T(8,128)S(1)} %collective-permute-done.1.high_ref.f_high, bf16[8,4,384,384]{3,2,1,0:T(8,128)(2,1)} %near_ref.3), custom_call_target="tpu_custom_call" | custom-call | flops 1000000 | bytes 1000000 | tf_op jit(solution)/shard_map/pallas_call | solution.py:344
  41.1 0.5 all-to-all-done.1.gathered_ref
  41.6 0.0 copy-done
  41.6 0.0 copy-done.1
  41.6 0.0 copy-done.3
  41.6 0.0 copy-done.5
  41.6 2.0 %shard_map.108 = (f32[8,16,384]{2,1,0:T(8,128)S(1)}, f32[16,128]{1,0:T(8,128)S(1)}) custom-call(s32[1,4]{1,0:T(1,128)S(1)} %copy-done.5, f32[32,8,128]{2,1,0:T(8,128)S(1)} %all-to-all-done.1.gathered_ref, f32[128,384]{1,0:T(8,128)S(1)} %shard_map.107.near_ref, f32[4,64,64]{2,1,0:T(8,128)S(1)} %bitcast.16, f32[8,64,64]{2,1,0:T(8,128)S(1)} %copy-done.1, ...), custom_call_target="tpu_custom_call" | custom-call | flops 1000000 | bytes 1000000 | tf_op jit(solution)/shard_map/pallas_call | solution.py:347
  43.7 1.8 %shard_map.109 = f32[32,16,128]{2,1,0:T(8,128)} custom-call(f32[8,16,384]{2,1,0:T(8,128)S(1)} %bitcast.11, f32[8,16,384]{2,1,0:T(8,128)S(1)} %get-tuple-element.8.image_ref.q_own.image0_ref, f32[64,3072]{1,0:T(8,128)S(1)} %shard_map.105.up_ref), custom_call_target="tpu_custom_call" | custom-call | flops 1000000 | bytes 1000000 | tf_op jit(solution)/shard_map/pallas_call | solution.py:352
  45.5 6.9 %all-to-all-start.2 = ((f32[32,16,128]{2,1,0:T(8,128)}), f32[32,16,128]{2,1,0:T(8,128)S(1)}, u32[]{:S(2)}, u32[]{:S(2)}) async-start(f32[32,16,128]{2,1,0:T(8,128)} %shard_map.109), calls=%async_computation.2 | async-start | bytes 524288 | tf_op jit(solution)/shard_map/all_to_all | solution.py:300
  52.4 0.3 collective-permute-start.3
  52.7 1.7 %collective-permute-start.2 = (f32[8,16,384]{2,1,0:T(8,128)S(1)}, f32[8,16,384]{2,1,0:T(8,128)S(1)}, u32[]{:S(2)}, u32[]{:S(2)}) collective-permute-start(f32[8,16,384]{2,1,0:T(8,128)S(1)} %get-tuple-element.8.image_ref.q_own.image0_ref), channel_id=1, source_target_pairs={{0,8},{8,16},{16,24},{24,32},{32,40},{40,48},{48,56},{56,64},{64,7... | collective-permute-start | bytes 589832 | tf_op jit(solution)/shard_map/ppermute | solution.py:307
  54.3 5.6 %collective-permute-done.3.q_high = f32[8,16,384]{2,1,0:T(8,128)S(1)} collective-permute-done((f32[8,16,384]{2,1,0:T(8,128)S(1)}, f32[8,16,384]{2,1,0:T(8,128)S(1)}, u32[]{:S(2)}, u32[]{:S(2)}) %collective-permute-start.3) | collective-permute-done | bytes 196640 | tf_op jit(solution)/shard_map/ppermute | solution.py:307
  60.0 0.0 collective-permute-done.2.q_low
  60.0 1.6 %all-to-all-done.2.gathered_ref = f32[32,16,128]{2,1,0:T(8,128)S(1)} async-done(((f32[32,16,128]{2,1,0:T(8,128)}), f32[32,16,128]{2,1,0:T(8,128)S(1)}, u32[]{:S(2)}, u32[]{:S(2)}) %all-to-all-start.2) | async-done | bytes 262176 | tf_op jit(solution)/shard_map/all_to_all | solution.py:300
  61.5 9.0 %shard_map.110 = (f32[32,8,128]{2,1,0:T(8,128)}, f32[128,384]{1,0:T(8,128)S(1)}, f32[128,384]{1,0:T(8,128)S(1)}, f32[16,128]{1,0:T(8,128)S(1)}) custom-call(s32[8,4]{1,0:T(8,128)S(1)} %add_select_fusion.ids_ref, s32[1,4]{1,0:T(1,128)S(1)} %copy-done.5, f32[32,16,128]{2,1,0:T(8,128)S(1)} %all-to-all-done.2.gathered_ref, ...), custom_call_target="tpu_custom_call" | custom-call | flops 1000000 | bytes 1000000 | tf_op jit(solution)/shard_map/pallas_call | solution.py:354
  70.5 8.0 %all-to-all-start.3 = ((f32[32,8,128]{2,1,0:T(8,128)}), f32[32,8,128]{2,1,0:T(8,128)S(1)}, u32[]{:S(2)}, u32[]{:S(2)}) async-start(f32[32,8,128]{2,1,0:T(8,128)} %get-tuple-element.10), calls=%async_computation.3 | async-start | bytes 262144 | tf_op jit(solution)/shard_map/all_to_all | solution.py:300
  78.5 7.7 %all-to-all-done.3.gathered_ref = f32[32,8,128]{2,1,0:T(8,128)S(1)} async-done(((f32[32,8,128]{2,1,0:T(8,128)}), f32[32,8,128]{2,1,0:T(8,128)S(1)}, u32[]{:S(2)}, u32[]{:S(2)}) %all-to-all-start.3) | async-done | bytes 131104 | tf_op jit(solution)/shard_map/all_to_all | solution.py:300
  86.2 2.8 %shard_map.111 = (f32[8,2,384]{2,1,0:T(2,128)}, f32[8,2,384]{2,1,0:T(2,128)}) custom-call(s32[1]{0:T(128)} %bitcast.place_ref, f32[32,8,128]{2,1,0:T(8,128)S(1)} %all-to-all-done.3.gathered_ref, f32[16,128]{1,0:T(8,128)S(1)} %get-tuple-element.11.alpha_ref, f32[8,16,384]{2,1,0:T(8,128)S(1)} %bitcast.13, ...), custom_call_target="tpu_custom_call" | custom-call | flops 1000000 | bytes 1000000 | tf_op jit(solution)/shard_map/pallas_call | solution.py:366
  (1 shorter events, 0.0 us)
Async XLA Ops:
  0.6 41.0 %copy-start = (f32[8,384,64]{1,2,0:T(8,128)S(1)}, f32[8,384,64]{1,2,0:T(8,128)}, u32[]{:S(2)}) copy-start(f32[8,384,64]{1,2,0:T(8,128)} %param.17) | copy-start | bytes 2359300
  2.4 39.2 %copy-start.1 = (f32[8,64,64]{2,1,0:T(8,128)S(1)}, f32[8,64,64]{2,1,0:T(8,128)}, u32[]{:S(2)}) copy-start(f32[8,64,64]{2,1,0:T(8,128)} %shift_ref.5) | copy-start | bytes 393220
  2.4 18.1 %all-to-all-start = ((f32[8,8,2,384]{3,2,1,0:T(2,128)}), f32[8,8,2,384]{3,2,1,0:T(2,128)S(1)}, u32[]{:S(2)}, u32[]{:S(2)}) async-start(f32[8,8,2,384]{3,2,1,0:T(2,128)} %shard_map.104), calls=%async_computation | async-start | bytes 393216 | tf_op jit(solution)/shard_map/all_to_all | solution.py:300
  12.3 1.1 %copy-start.2 = (f32[8,64,384]{2,1,0:T(8,128)S(1)}, f32[8,64,384]{2,1,0:T(8,128)}, u32[]{:S(2)}) copy-start(f32[8,64,384]{2,1,0:T(8,128)} %up_ref.1) | copy-start | bytes 2359300
  13.5 0.9 %copy-start.4 = (f32[8,64,64]{2,1,0:T(8,128)S(1)}, f32[8,64,64]{2,1,0:T(8,128)}, u32[]{:S(2)}) copy-start(f32[8,64,64]{2,1,0:T(8,128)} %shift_ref.3) | copy-start | bytes 393220
  14.4 27.2 %copy-start.3 = (f32[1,4,64,64]{3,2,1,0:T(8,128)S(1)}, f32[1,4,64,64]{3,2,1,0:T(8,128)}, u32[]{:S(2)}) copy-start(f32[1,4,64,64]{3,2,1,0:T(8,128)} %param.15) | copy-start | bytes 196612
  14.4 27.2 %copy-start.5 = (s32[1,4]{1,0:T(1,128)S(1)}, s32[1,4]{1,0:T(1,128)}, u32[]{:S(2)}) copy-start(s32[1,4]{1,0:T(1,128)} %far_ref.3) | copy-start | bytes 52
  20.6 13.4 %collective-permute-start.1 = (f32[8,16,384]{2,1,0:T(8,128)S(1)}, f32[8,16,384]{2,1,0:T(8,128)S(1)}, u32[]{:S(2)}, u32[]{:S(2)}) collective-permute-start(f32[8,16,384]{2,1,0:T(8,128)S(1)} %bitcast.7), channel_id=1, source_target_pairs={{8,0},{16,8},{24,16},{32,24},{40,32},{48,40},{56,48},{64,56},{72,6... | collective-permute-start | bytes 589832 | tf_op jit(solution)/shard_map/ppermute | solution.py:307
  23.1 10.9 %collective-permute-start = (f32[8,16,384]{2,1,0:T(8,128)S(1)}, f32[8,16,384]{2,1,0:T(8,128)S(1)}, u32[]{:S(2)}, u32[]{:S(2)}) collective-permute-start(f32[8,16,384]{2,1,0:T(8,128)S(1)} %bitcast.8), channel_id=1, source_target_pairs={{0,8},{8,16},{16,24},{24,32},{32,40},{40,48},{48,56},{56,64},{64,7... | collective-permute-start | bytes 589832 | tf_op jit(solution)/shard_map/ppermute | solution.py:307
  25.8 15.8 %all-to-all-start.1 = ((f32[32,8,128]{2,1,0:T(8,128)}), f32[32,8,128]{2,1,0:T(8,128)S(1)}, u32[]{:S(2)}, u32[]{:S(2)}) async-start(f32[32,8,128]{2,1,0:T(8,128)} %shard_map.106), calls=%async_computation.1 | async-start | bytes 262144 | tf_op jit(solution)/shard_map/all_to_all | solution.py:300
  45.5 16.1 %all-to-all-start.2 = ((f32[32,16,128]{2,1,0:T(8,128)}), f32[32,16,128]{2,1,0:T(8,128)S(1)}, u32[]{:S(2)}, u32[]{:S(2)}) async-start(f32[32,16,128]{2,1,0:T(8,128)} %shard_map.109), calls=%async_computation.2 | async-start | bytes 524288 | tf_op jit(solution)/shard_map/all_to_all | solution.py:300
  52.4 7.6 %collective-permute-start.3 = (f32[8,16,384]{2,1,0:T(8,128)S(1)}, f32[8,16,384]{2,1,0:T(8,128)S(1)}, u32[]{:S(2)}, u32[]{:S(2)}) collective-permute-start(f32[8,16,384]{2,1,0:T(8,128)S(1)} %get-tuple-element.8.image_ref.q_own.image0_ref), channel_id=1, source_target_pairs={{8,0},{16,8},{24,16},{32,24},{40,32},{48,40},{56,48},{64,56},{72,6... | collective-permute-start | bytes 589832 | tf_op jit(solution)/shard_map/ppermute | solution.py:307
  52.7 7.3 %collective-permute-start.2 = (f32[8,16,384]{2,1,0:T(8,128)S(1)}, f32[8,16,384]{2,1,0:T(8,128)S(1)}, u32[]{:S(2)}, u32[]{:S(2)}) collective-permute-start(f32[8,16,384]{2,1,0:T(8,128)S(1)} %get-tuple-element.8.image_ref.q_own.image0_ref), channel_id=1, source_target_pairs={{0,8},{8,16},{16,24},{24,32},{32,40},{40,48},{48,56},{56,64},{64,7... | collective-permute-start | bytes 589832 | tf_op jit(solution)/shard_map/ppermute | solution.py:307
  70.5 15.7 %all-to-all-start.3 = ((f32[32,8,128]{2,1,0:T(8,128)}), f32[32,8,128]{2,1,0:T(8,128)S(1)}, u32[]{:S(2)}, u32[]{:S(2)}) async-start(f32[32,8,128]{2,1,0:T(8,128)} %get-tuple-element.10), calls=%async_computation.3 | async-start | bytes 262144 | tf_op jit(solution)/shard_map/all_to_all | solution.py:300

commit v5 on v4

--- a/solution.py
+++ b/solution.py
@@ -6,7 +6,7 @@
 from jax.sharding import PartitionSpec as P
 
 
-HIGH = lax.Precision.HIGHEST
+HIGH = lax.Precision.HIGH
 F32 = jnp.float32
 BF16 = jnp.bfloat16
 MIB = 1024 * 1024
@@ -32,6 +32,10 @@
     return jnp.dot(left, right, precision=HIGH, preferred_element_type=F32)
 
 
+def exact(left, right):
+    return jnp.dot(left, right, precision=lax.Precision.HIGHEST, preferred_element_type=F32)
+
+
 def nt(left, right):
     return lax.dot_general(
         left, right, (((1,), (1,)), ((), ())), precision=HIGH, preferred_element_type=F32
@@ -49,9 +53,16 @@
     row, lane = iotas(K, 2 * K)
     eye = jnp.where(lane == row + K, 1.0, 0.0).astype(F32)
     work = jnp.concatenate([matrix, eye[:, K:]], axis=1)
-    for i in range(K):
-        pivot = work[i : i + 1, :] / work[i : i + 1, i : i + 1]
-        work = jnp.where(row == i, pivot, work - work[:, i : i + 1] * pivot)
+    for i in range(0, K, 2):
+        left = jnp.broadcast_to(work[:, i : i + 1], (K, 2 * K))
+        right = jnp.broadcast_to(work[:, i + 1 : i + 2], (K, 2 * K))
+        a, c = left[i : i + 1], left[i + 1 : i + 2]
+        b, d = right[i : i + 1], right[i + 1 : i + 2]
+        upper, lower = work[i : i + 1], work[i + 1 : i + 2]
+        scale = 1.0 / (a * d - b * c)
+        upper, lower = (d * upper - b * lower) * scale, (a * lower - c * upper) * scale
+        rest = work - left * upper - right * lower
+        work = jnp.where(row == i, upper, jnp.where(row == i + 1, lower, rest))
     return work[:, K:]
 
 
@@ -124,10 +135,10 @@
     return nn(wide, down_ref[...].reshape(PD * E, W))
 
 
-def chosen_expansion(far_ref, gathered_ref, table_ref):
+def expansion(chosen, table_ref):
     total = None
     for j in range(FL):
-        moment = gathered_ref[far_ref[0, j]]
+        moment = chosen[j]
         if moment.shape[0] < K:
             moment = jnp.concatenate([moment[:, :E], moment[:, E:]], axis=0)
         part = nt(moment[:, :E], table_ref[j])
@@ -135,14 +146,10 @@
     return total
 
 
-def spread_kernel(mine_ref, out_ref, sem):
-    copies = [
-        pltpu.make_async_copy(mine_ref, out_ref.at[i], sem.at[i]) for i in range(out_ref.shape[0])
-    ]
-    for copy in copies:
-        copy.start()
-    for copy in copies:
-        copy.wait()
+def summed(parts):
+    while len(parts) > 1:
+        parts = [a + b for a, b in zip(parts[::2], parts[1::2])]
+    return parts[0]
 
 
 def maps_kernel(up_ref, shift_ref, out_ref):
@@ -157,23 +164,33 @@
         out_ref[i] = message
 
 
-def near_kernel(ids_ref, low_ref, own_ref, high_ref, near_ref, out_ref, blocks_ref, rounded_ref, sems):
+def near_kernel(
+    ids_ref, low_ref, own_ref, high_ref, near_ref, out_ref, blocks_ref, rounded_ref, ids_smem, sems
+):
+    ids = pltpu.make_async_copy(ids_ref, ids_smem, sems.at[PD])
+    ids.start()
     fetch(near_ref, blocks_ref, sems)
     for i, ref in enumerate((low_ref, own_ref, high_ref)):
         rounded_ref[i * PD : (i + 1) * PD] = ref[...].astype(BF16)
+    ids.wait()
     fetched(near_ref, blocks_ref, sems)
-    out_ref[...] = near_product(ids_ref, blocks_ref, rounded_ref).T
-
-
-def image_kernel(far_ref, gathered_ref, near_ref, table_ref, shift_ref, down_ref, image_out, local_out):
-    local_exp = chosen_expansion(far_ref, gathered_ref, table_ref)
+    out_ref[...] = near_product(ids_smem, blocks_ref, rounded_ref).T
+
+
+def image_kernel(
+    pick_ref, gathered_ref, near_ref, field_ref, up_ref, table_ref, shift_ref, down_ref,
+    image_out, local_out, out_ref,
+):
+    count = gathered_ref.shape[0]
+    chosen = [
+        summed([gathered_ref[c] * pick_ref[j * count + c : j * count + c + 1] for c in range(count)])
+        for j in range(FL)
+    ]
+    local_exp = expansion(chosen, table_ref)
     local_out[...] = jnp.concatenate([local_exp, jnp.zeros((K, E), F32)], axis=1)
     image = near_ref[...] + far_product(shifted(local_exp, shift_ref), down_ref)
     image_out[...] = image.reshape(PD, K, W)
-
-
-def grams_kernel(field_ref, image_ref, up_ref, out_ref):
-    image = side_by_side(image_ref[...].reshape(ROWS, W))
+    image = side_by_side(image)
     moment = nt(image, up_ref[...])
     both = jnp.concatenate([side_by_side(field_ref[...].reshape(ROWS, W)), image], axis=0)
     grams = nt(both, both)
@@ -185,25 +202,25 @@
 
 
 def total_of(gathered_ref):
-    parts = [gathered_ref[i] for i in range(gathered_ref.shape[0])]
-    while len(parts) > 1:
-        parts = [a + b for a, b in zip(parts[::2], parts[1::2])]
-    return parts[0]
+    return summed([gathered_ref[i] for i in range(gathered_ref.shape[0])])
 
 
 def direction_kernel(
     ids_ref, far_ref, gathered_ref, f_low, f_own, f_high, q_low, q_own, q_high,
     local_ref, table_ref, shift_ref, down_ref, near_ref,
     out_ref, direction_out, image_out, alpha_out,
-    blocks_ref, rounded_ref, sems,
+    blocks_ref, rounded_ref, ids_smem, far_smem, sems,
 ):
+    ids = pltpu.make_async_copy(ids_ref, ids_smem, sems.at[PD])
+    far_ids = pltpu.make_async_copy(far_ref, far_smem, sems.at[PD + 1])
+    ids.start()
+    far_ids.start()
     fetch(near_ref, blocks_ref, sems)
     total = total_of(gathered_ref)
     qr = total[:, E : E + K]
     qq = total[:, E + K : E + 2 * K]
     rr = total[:, E + 2 * K : E + 3 * K]
     rq = total[:, E + 3 * K :]
-    image_exp = chosen_expansion(far_ref, gathered_ref, table_ref)
     curve_inv = inverse(0.5 * (qr + rq))
     rr_inv = inverse(rr)
     alpha = small(curve_inv, rr)
@@ -214,6 +231,8 @@
     row, lane = iotas(K, K)
     lift_t = small(following, rr_inv) + jnp.where(row == lane, 1.0, 0.0)
     alpha_out[...] = jnp.concatenate([alpha_t, jnp.zeros((K, ROWS - K), F32)], axis=1)
+    far_ids.wait()
+    image_exp = expansion([gathered_ref[far_smem[0, j]] for j in range(FL)], table_ref)
     local_exp = small(lift_t, local_ref[:, :E]) - small(alpha_t, image_exp)
     far = far_product(shifted(local_exp, shift_ref), down_ref)
 
@@ -229,8 +248,9 @@
             residual = f_own[...].reshape(ROWS, W) + nn(coeffs, q_own[...].reshape(ROWS, W))
         rounded_ref[i * PD : (i + 1) * PD] = mixed.astype(BF16).reshape(PD, K, W)
     direction_out[...] = direction
+    ids.wait()
     fetched(near_ref, blocks_ref, sems)
-    image = near_product(ids_ref, blocks_ref, rounded_ref)
+    image = near_product(ids_smem, blocks_ref, rounded_ref)
     image = image.T + far
     image_out[...] = image
     residual = side_by_side(residual)
@@ -246,29 +266,27 @@
         out_ref[i] = message
 
 
-def own_coeffs(place, coeffs_t):
-    row, lane = iotas(K, K)
-    pick = jnp.where(lane == (row % 2) * PD + place, 1.0, 0.0).astype(F32)
+def own_coeffs(pick, coeffs_t):
     row, lane = iotas(K, ROWS)
     return jnp.where(row // 2 == lane // K, tiled(small(pick, coeffs_t)), 0.0)
 
 
 def last_step_kernel(
-    place_ref, gathered_ref, alpha_ref, field_ref, image0_ref, direction_ref, image_ref,
+    pick_ref, gathered_ref, alpha_ref, field_ref, image0_ref, direction_ref, image_ref,
     x_out, r_out,
 ):
     total = total_of(gathered_ref)
     total = jnp.concatenate([total[:, : 2 * K], total[:, 2 * K : 4 * K]], axis=0)
+    pick = pick_ref[...]
     qd = total[:, :K]
-    row, lane = iotas(K, K)
-    eye = jnp.where(row == lane, 1.0, 0.0).astype(F32)
     field = field_ref[...].reshape(ROWS, W)
-    mine = own_coeffs(place_ref[0], eye)
-    coeffs0 = own_coeffs(place_ref[0], alpha_ref[:, :K])
+    row, lane = iotas(K, ROWS)
+    mine = jnp.where(row // 2 == lane // K, tiled(pick), 0.0)
+    coeffs0 = own_coeffs(pick, alpha_ref[:, :K])
     x = nn(coeffs0, field)
-    r = nn(mine, field) - nn(coeffs0, image0_ref[...].reshape(ROWS, W))
+    r = exact(mine, field) - exact(coeffs0, image0_ref[...].reshape(ROWS, W))
     alpha_t = small(total[:, K : 2 * K], inverse(0.5 * (qd + qd.T)))
-    coeffs = own_coeffs(place_ref[0], alpha_t)
+    coeffs = own_coeffs(pick, alpha_t)
     x = x + nn(coeffs, direction_ref[...])
     r = r - nn(coeffs, image_ref[...])
     for p in range(PD):
@@ -292,7 +310,7 @@
 NEAR_SCRATCH = (
     pltpu.VMEM((PD, NB, W, W), BF16),
     pltpu.VMEM((3 * PD, K, W), BF16),
-    pltpu.SemaphoreType.DMA((PD,)),
+    pltpu.SMEM((PD, NB), jnp.int32),
 )
 
 
@@ -320,19 +338,18 @@
 ):
     count = lax.axis_size("patch")
     depth = lax.axis_size("rhs")
-    place = lax.axis_index("rhs").astype(jnp.int32).reshape(1)
+    place = lax.axis_index("rhs").astype(jnp.int32)
     first = lax.axis_index("patch") * PD - PD
     ids = jnp.mod(neighbours - first, PD * count)
 
-    message = call(
-        spread_kernel,
-        [HBM],
-        shape(depth, PD, 2, W),
-        (pltpu.SemaphoreType.DMA((depth,)),),
-        limit=63,
-    )(rhs_vectors)
+    message = jnp.broadcast_to(rhs_vectors[None], (depth, *rhs_vectors.shape))
     parts = swap(message, "rhs")
     field = parts.transpose(1, 2, 0, 3).reshape(PD, K, W)
+
+    row, lane = jnp.arange(K)[:, None], jnp.arange(K)[None, :]
+    pick_column = (lane == (row % 2) * PD + place).astype(F32)
+    pick_cell = (far_lists[0][:, None] == jnp.arange(count)[None, :]).astype(F32)
+    pick_cell = jnp.broadcast_to(pick_cell.reshape(FL * count, 1), (FL * count, 2 * E))
 
     up = call(maps_kernel, [VMEM] * 2, shape(E, PD * W))(up_maps, shift_up)
     table = translations[0]
@@ -341,21 +358,28 @@
     f_low, f_high = halo(field, "patch")
     message = call(moment_kernel, [VMEM] * 2, shape(count, K // 2, ROWS))(field, up)
     gathered = swap(message, "patch")
-    near = call(near_kernel, [SMEM] + [VMEM] * 3 + [HBM], shape(ROWS, W), NEAR_SCRATCH, limit=48)(
+    near = call(
+        near_kernel,
+        [VMEM] * 4 + [HBM],
+        shape(ROWS, W),
+        (*NEAR_SCRATCH, pltpu.SemaphoreType.DMA((PD + 1,))),
+        limit=48,
+    )(
         ids, f_low, field, f_high, near_blocks
     )
-    image, local_exp = call(
-        image_kernel, [SMEM] + [VMEM] * 5, (shape(PD, K, W), shape(K, 2 * E))
-    )(far_lists, gathered, near, table, shift_down, down)
+    image, local_exp, message = call(
+        image_kernel,
+        [VMEM] * 8,
+        (shape(PD, K, W), shape(K, 2 * E), shape(count, K, ROWS)),
+    )(pick_cell, gathered, near, field, up, table, shift_down, down)
 
     q_low, q_high = halo(image, "patch")
-    message = call(grams_kernel, [VMEM] * 3, shape(count, K, ROWS))(field, image, up)
     gathered = swap(message, "patch")
     message, direction, image1, alpha = call(
         direction_kernel,
-        [SMEM] * 2 + [VMEM] * 11 + [HBM],
+        [VMEM] * 13 + [HBM],
         (shape(count, K // 2, ROWS), shape(ROWS, W), shape(ROWS, W), shape(K, ROWS)),
-        NEAR_SCRATCH,
+        (*NEAR_SCRATCH, pltpu.SMEM((1, FL), jnp.int32), pltpu.SemaphoreType.DMA((PD + 2,))),
         limit=48,
     )(
         ids, far_lists, gathered, f_low, field, f_high, q_low, image, q_high,
@@ -363,8 +387,8 @@
     )
 
     gathered = swap(message, "patch")
-    return call(last_step_kernel, [SMEM] + [VMEM] * 6, (shape(PD, 2, W),) * 2)(
-        place, gathered, alpha, field, image, direction, image1
+    return call(last_step_kernel, [VMEM] * 7, (shape(PD, 2, W),) * 2)(
+        pick_column, gathered, alpha, field, image, direction, image1
     )
 
 

time: 89.5 us -> 82.3 us (0.920)
  Pallas kernels: 26.6 us -> 20.2 us
  starting transfers between devices: 37.9 us -> 34.4 us
  local copies, waits for them, and re-layouts: 2.92 us -> 4.62 us
    pallas_call x6 -> x4, Pallas kernels: 24.4 us -> 18.6 us  [the longest x1 7.7 us: on_device(): call(direction_kernel, [VMEM] * 13 + [HBM], (shape(count, K // 2, ROWS),...]
    ppermute x2, waiting for transfers between devices: 0.01 us -> 3.8 us  [halo(): lax.ppermute(block, axis, forward)]
    ppermute x2, waiting for transfers between devices: 5.63 us -> 2.09 us  [halo(): lax.ppermute(block, axis, backward)]
    all_to_all x4, starting transfers between devices: 32.2 us -> 29.1 us  [swap(): return lax.all_to_all(array, axis, 0, 0, tiled=True)]
    ppermute x2, starting transfers between devices: 2.83 us -> 0.01 us  [halo(): lax.ppermute(block, axis, backward)]
    ppermute x2, starting transfers between devices: 2.85 us -> 5.32 us  [halo(): lax.ppermute(block, axis, forward)]
    broadcast_in_dim x0 -> x2, local copies, waits for them, and re-layouts: none -> 1.62 us  [the longest x1 1.55 us: on_device(): message = jnp.broadcast_to(rhs_vectors[None], (depth, *rhs_vectors.shape))]
  transfers between devices with their start and end apart: 8 -> 8, of which waited for: 5 -> 6; matrix products, arithmetic and copies ran while one was open for 1% -> 2% of each run, Pallas kernels for 10% -> 10%
where the time goes in v5:
time: 82.3 us; the launch traced here: 81.8 us
  starting transfers between devices  34.4 us (42%)
  waiting for transfers between devices  21 us (26%)
  Pallas kernels  20.2 us (25%)
  local copies, waits for them, and re-layouts  4.62 us (6%)
    all_to_all x4, starting transfers between devices, swap(): return lax.all_to_all(array, axis, 0, 0, tiled=True)  29.1 us
    all_to_all x4, waiting for transfers between devices, swap(): return lax.all_to_all(array, axis, 0, 0, tiled=True)  15.1 us
    pallas_call x1, Pallas kernels, on_device(): call(direction_kernel, [VMEM] * 13 + [HBM], (shape(count, K // 2, ROWS),...  7.7 us
    pallas_call x1, Pallas kernels, on_device(): call(near_kernel, [VMEM] * 4 + [HBM], shape(ROWS, W), (*NEAR_SCRATCH, plt...  6.44 us
    ppermute x2, starting transfers between devices, halo(): lax.ppermute(block, axis, forward)  5.32 us
    ppermute x2, waiting for transfers between devices, halo(): lax.ppermute(block, axis, forward)  3.8 us
    unnamed x13, local copies, waits for them, and re-layouts  2.86 us
    pallas_call x1, Pallas kernels, on_device(): call(image_kernel, [VMEM] * 8, (shape(PD, K, W), shape(K, 2 * E), shape(c...  2.34 us
  transfers between devices with their start and end apart: 8, of which 6 were waited for; matrix products, arithmetic and copies ran while one was open for 2% of the time, Pallas kernels for 10%

profile of v5, /device:TPU:1, one launch (start us, length us, event | category | flops | bytes accessed | tf_op | source)
XLA Modules:
  0.0 81.8 jit_solution(13196372334345390048)
XLA Ops:
  0.6 0.0 copy-start
  0.6 0.0 copy-start.1
  0.6 1.5 %broadcast_in_dim.5 = f32[8,8,2,384]{3,2,1,0:T(2,128)} broadcast(f32[8,2,384]{2,1,0:T(2,128)} %param.9), dimensions={1,2,3} | broadcast | bytes 221184 | tf_op jit(solution)/shard_map/broadcast_in_dim | solution.py:345
  2.2 9.0 %all-to-all-start = ((f32[8,8,2,384]{3,2,1,0:T(2,128)}), f32[8,8,2,384]{3,2,1,0:T(2,128)S(1)}, u32[]{:S(2)}, u32[]{:S(2)}) async-start(f32[8,8,2,384]{3,2,1,0:T(2,128)} %broadcast_in_dim.5), calls=%async_computation | async-start | bytes 393216 | tf_op jit(solution)/shard_map/all_to_all | solution.py:318
  11.2 0.8 copy.12
  12.0 0.7 fusion.2
  12.7 0.1 reshape.47
  12.8 0.0 copy-start.2
  12.8 1.1 %copy-done.2 = f32[8,64,384]{2,1,0:T(8,128)S(1)} copy-done((f32[8,64,384]{2,1,0:T(8,128)S(1)}, f32[8,64,384]{2,1,0:T(8,128)}, u32[]{:S(2)}) %copy-start.2) | copy-done | bytes 786456
  13.9 0.0 copy-start.4
  13.9 0.9 %copy-done.4 = f32[8,64,64]{2,1,0:T(8,128)S(1)} copy-done((f32[8,64,64]{2,1,0:T(8,128)S(1)}, f32[8,64,64]{2,1,0:T(8,128)}, u32[]{:S(2)}) %copy-start.4) | copy-done | bytes 131096
  14.9 0.0 copy-start.3
  14.9 0.0 copy-start.5
  14.9 0.5 shard_map.104.up_ref
  15.3 4.9 %all-to-all-done = f32[8,8,2,384]{3,2,1,0:T(2,128)S(1)} async-done(((f32[8,8,2,384]{3,2,1,0:T(2,128)}), f32[8,8,2,384]{3,2,1,0:T(2,128)S(1)}, u32[]{:S(2)}, u32[]{:S(2)}) %all-to-all-start) | async-done | bytes 196640 | tf_op jit(solution)/shard_map/all_to_all | solution.py:318
  20.2 0.1 copy.15
  20.3 3.6 %collective-permute-start = (f32[8,16,384]{2,1,0:T(8,128)S(1)}, f32[8,16,384]{2,1,0:T(8,128)S(1)}, u32[]{:S(2)}, u32[]{:S(2)}) collective-permute-start(f32[8,16,384]{2,1,0:T(8,128)S(1)} %bitcast.7), channel_id=1, source_target_pairs={{0,8},{8,16},{16,24},{24,32},{32,40},{40,48},{48,56},{56,64},{64,7... | collective-permute-start | bytes 589832 | tf_op jit(solution)/shard_map/ppermute | solution.py:325
  23.9 0.0 collective-permute-start.1
  23.9 1.2 %shard_map.105 = f32[32,8,128]{2,1,0:T(8,128)} custom-call(f32[8,16,384]{2,1,0:T(8,128)S(1)} %bitcast.9, f32[64,3072]{1,0:T(8,128)S(1)} %shard_map.104.up_ref), custom_call_target="tpu_custom_call" | custom-call | flops 1000000 | bytes 1000000 | tf_op jit(solution)/shard_map/pallas_call | solution.py:359
  25.0 7.7 %all-to-all-start.1 = ((f32[32,8,128]{2,1,0:T(8,128)}), f32[32,8,128]{2,1,0:T(8,128)S(1)}, u32[]{:S(2)}, u32[]{:S(2)}) async-start(f32[32,8,128]{2,1,0:T(8,128)} %shard_map.105), calls=%async_computation.1 | async-start | bytes 262144 | tf_op jit(solution)/shard_map/all_to_all | solution.py:318
  32.8 0.0 collective-permute-done.low_ref.f_low
  32.8 0.0 collective-permute-done.1.high_ref.f_high
  32.8 6.4 %shard_map.106.near_ref = f32[128,384]{1,0:T(8,128)S(1)} custom-call(s32[8,4]{1,0:T(8,128)S(1)} %add_select_fusion.ids_ref, f32[8,16,384]{2,1,0:T(8,128)S(1)} %collective-permute-done.low_ref.f_low, f32[8,16,384]{2,1,0:T(8,128)S(1)} %bitcast.10, f32[8,16,384]{2,1,0:T(8,128)S(1)} %collective-permute-done.1.high_ref.f_high, bf16[8,4,384,384]{3,2,1,0:T(8,128)(2,1)} %near_ref.3), custom_call_target="tpu_custom_call" | custom-call | flops 1000000 | bytes 1000000 | tf_op jit(solution)/shard_map/pallas_call | solution.py:361
  39.3 1.1 %all-to-all-done.1.gathered_ref = f32[32,8,128]{2,1,0:T(8,128)S(1)} async-done(((f32[32,8,128]{2,1,0:T(8,128)}), f32[32,8,128]{2,1,0:T(8,128)S(1)}, u32[]{:S(2)}, u32[]{:S(2)}) %all-to-all-start.1) | async-done | bytes 131104 | tf_op jit(solution)/shard_map/all_to_all | solution.py:318
  40.4 0.1 broadcast_in_dim.4.pick_ref
  40.4 0.0 copy-done
  40.5 0.0 copy-done.1
  40.5 0.0 copy-done.3
  40.5 2.3 %shard_map.107 = (f32[8,16,384]{2,1,0:T(8,128)S(1)}, f32[16,128]{1,0:T(8,128)S(1)}, f32[32,16,128]{2,1,0:T(8,128)}) custom-call(f32[128,128]{1,0:T(8,128)S(1)} %broadcast_in_dim.4.pick_ref, f32[32,8,128]{2,1,0:T(8,128)S(1)} %all-to-all-done.1.gathered_ref, f32[128,384]{1,0:T(8,128)S(1)} %shard_map.106.near_ref, f32[8,16,384]{2,1,0:T(8,128)S(1)} %bitcast.11, ...), custom_call_target="tpu_custom_call" | custom-call | flops 1000000 | bytes 1000000 | tf_op jit(solution)/shard_map/pallas_call | solution.py:370
  42.8 6.3 %all-to-all-start.2 = ((f32[32,16,128]{2,1,0:T(8,128)}), f32[32,16,128]{2,1,0:T(8,128)S(1)}, u32[]{:S(2)}, u32[]{:S(2)}) async-start(f32[32,16,128]{2,1,0:T(8,128)} %get-tuple-element.9), calls=%async_computation.2 | async-start | bytes 524288 | tf_op jit(solution)/shard_map/all_to_all | solution.py:318
  49.1 1.7 %collective-permute-start.2 = (f32[8,16,384]{2,1,0:T(8,128)S(1)}, f32[8,16,384]{2,1,0:T(8,128)S(1)}, u32[]{:S(2)}, u32[]{:S(2)}) collective-permute-start(f32[8,16,384]{2,1,0:T(8,128)S(1)} %get-tuple-element.10.q_own.image0_ref), channel_id=1, source_target_pairs={{0,8},{8,16},{16,24},{24,32},{32,40},{40,48},{48,56},{56,64},{64,7... | collective-permute-start | bytes 589832 | tf_op jit(solution)/shard_map/ppermute | solution.py:325
  50.8 0.0 collective-permute-start.3
  50.8 3.8 %collective-permute-done.2.q_low = f32[8,16,384]{2,1,0:T(8,128)S(1)} collective-permute-done((f32[8,16,384]{2,1,0:T(8,128)S(1)}, f32[8,16,384]{2,1,0:T(8,128)S(1)}, u32[]{:S(2)}, u32[]{:S(2)}) %collective-permute-start.2) | collective-permute-done | bytes 196640 | tf_op jit(solution)/shard_map/ppermute | solution.py:325
  54.6 2.1 %collective-permute-done.3.q_high = f32[8,16,384]{2,1,0:T(8,128)S(1)} collective-permute-done((f32[8,16,384]{2,1,0:T(8,128)S(1)}, f32[8,16,384]{2,1,0:T(8,128)S(1)}, u32[]{:S(2)}, u32[]{:S(2)}) %collective-permute-start.3) | collective-permute-done | bytes 196640 | tf_op jit(solution)/shard_map/ppermute | solution.py:325
  56.7 1.6 %all-to-all-done.2.gathered_ref = f32[32,16,128]{2,1,0:T(8,128)S(1)} async-done(((f32[32,16,128]{2,1,0:T(8,128)}), f32[32,16,128]{2,1,0:T(8,128)S(1)}, u32[]{:S(2)}, u32[]{:S(2)}) %all-to-all-start.2) | async-done | bytes 262176 | tf_op jit(solution)/shard_map/all_to_all | solution.py:318
  58.3 0.0 copy-done.5
  58.3 7.7 %shard_map.108 = (f32[32,8,128]{2,1,0:T(8,128)}, f32[128,384]{1,0:T(8,128)S(1)}, f32[128,384]{1,0:T(8,128)S(1)}, f32[16,128]{1,0:T(8,128)S(1)}) custom-call(s32[8,4]{1,0:T(8,128)S(1)} %add_select_fusion.ids_ref, s32[1,4]{1,0:T(1,128)S(1)} %copy-done.5, f32[32,16,128]{2,1,0:T(8,128)S(1)} %all-to-all-done.2.gathered_ref, ...), custom_call_target="tpu_custom_call" | custom-call | flops 1000000 | bytes 1000000 | tf_op jit(solution)/shard_map/pallas_call | solution.py:378
  66.0 6.1 %all-to-all-start.3 = ((f32[32,8,128]{2,1,0:T(8,128)}), f32[32,8,128]{2,1,0:T(8,128)S(1)}, u32[]{:S(2)}, u32[]{:S(2)}) async-start(f32[32,8,128]{2,1,0:T(8,128)} %get-tuple-element.12), calls=%async_computation.3 | async-start | bytes 262144 | tf_op jit(solution)/shard_map/all_to_all | solution.py:318
  72.1 0.1 fusion.pick_ref
  72.2 7.5 %all-to-all-done.3.gathered_ref = f32[32,8,128]{2,1,0:T(8,128)S(1)} async-done(((f32[32,8,128]{2,1,0:T(8,128)}), f32[32,8,128]{2,1,0:T(8,128)S(1)}, u32[]{:S(2)}, u32[]{:S(2)}) %all-to-all-start.3) | async-done | bytes 131104 | tf_op jit(solution)/shard_map/all_to_all | solution.py:318
  79.7 2.1 %shard_map.109 = (f32[8,2,384]{2,1,0:T(2,128)}, f32[8,2,384]{2,1,0:T(2,128)}) custom-call(f32[16,16]{1,0:T(8,128)S(1)} %fusion.pick_ref, f32[32,8,128]{2,1,0:T(8,128)S(1)} %all-to-all-done.3.gathered_ref, f32[16,128]{1,0:T(8,128)S(1)} %get-tuple-element.13.alpha_ref, f32[8,16,384]{2,1,0:T(8,128)S(1)} %bitcast.13, ...), custom_call_target="tpu_custom_call" | custom-call | flops 1000000 | bytes 1000000 | tf_op jit(solution)/shard_map/pallas_call | solution.py:390
  (2 shorter events, 0.0 us)
Async XLA Ops:
  0.6 39.8 %copy-start = (f32[8,384,64]{1,2,0:T(8,128)S(1)}, f32[8,384,64]{1,2,0:T(8,128)}, u32[]{:S(2)}) copy-start(f32[8,384,64]{1,2,0:T(8,128)} %param.17) | copy-start | bytes 2359300
  0.6 39.8 %copy-start.1 = (f32[8,64,64]{2,1,0:T(8,128)S(1)}, f32[8,64,64]{2,1,0:T(8,128)}, u32[]{:S(2)}) copy-start(f32[8,64,64]{2,1,0:T(8,128)} %shift_ref.5) | copy-start | bytes 393220
  2.2 18.0 %all-to-all-start = ((f32[8,8,2,384]{3,2,1,0:T(2,128)}), f32[8,8,2,384]{3,2,1,0:T(2,128)S(1)}, u32[]{:S(2)}, u32[]{:S(2)}) async-start(f32[8,8,2,384]{3,2,1,0:T(2,128)} %broadcast_in_dim.5), calls=%async_computation | async-start | bytes 393216 | tf_op jit(solution)/shard_map/all_to_all | solution.py:318
  12.8 1.1 %copy-start.2 = (f32[8,64,384]{2,1,0:T(8,128)S(1)}, f32[8,64,384]{2,1,0:T(8,128)}, u32[]{:S(2)}) copy-start(f32[8,64,384]{2,1,0:T(8,128)} %up_ref.1) | copy-start | bytes 2359300
  13.9 0.9 %copy-start.4 = (f32[8,64,64]{2,1,0:T(8,128)S(1)}, f32[8,64,64]{2,1,0:T(8,128)}, u32[]{:S(2)}) copy-start(f32[8,64,64]{2,1,0:T(8,128)} %shift_ref.3) | copy-start | bytes 393220
  14.9 25.6 %copy-start.3 = (f32[1,4,64,64]{3,2,1,0:T(8,128)S(1)}, f32[1,4,64,64]{3,2,1,0:T(8,128)}, u32[]{:S(2)}) copy-start(f32[1,4,64,64]{3,2,1,0:T(8,128)} %param.15) | copy-start | bytes 196612
  14.9 43.5 %copy-start.5 = (s32[1,4]{1,0:T(1,128)S(1)}, s32[1,4]{1,0:T(1,128)}, u32[]{:S(2)}) copy-start(s32[1,4]{1,0:T(1,128)} %far_ref.1) | copy-start | bytes 52
  20.3 12.5 %collective-permute-start = (f32[8,16,384]{2,1,0:T(8,128)S(1)}, f32[8,16,384]{2,1,0:T(8,128)S(1)}, u32[]{:S(2)}, u32[]{:S(2)}) collective-permute-start(f32[8,16,384]{2,1,0:T(8,128)S(1)} %bitcast.7), channel_id=1, source_target_pairs={{0,8},{8,16},{16,24},{24,32},{32,40},{40,48},{48,56},{56,64},{64,7... | collective-permute-start | bytes 589832 | tf_op jit(solution)/shard_map/ppermute | solution.py:325
  23.9 8.9 %collective-permute-start.1 = (f32[8,16,384]{2,1,0:T(8,128)S(1)}, f32[8,16,384]{2,1,0:T(8,128)S(1)}, u32[]{:S(2)}, u32[]{:S(2)}) collective-permute-start(f32[8,16,384]{2,1,0:T(8,128)S(1)} %bitcast.8), channel_id=1, source_target_pairs={{8,0},{16,8},{24,16},{32,24},{40,32},{48,40},{56,48},{64,56},{72,6... | collective-permute-start | bytes 589832 | tf_op jit(solution)/shard_map/ppermute | solution.py:325
  25.0 15.3 %all-to-all-start.1 = ((f32[32,8,128]{2,1,0:T(8,128)}), f32[32,8,128]{2,1,0:T(8,128)S(1)}, u32[]{:S(2)}, u32[]{:S(2)}) async-start(f32[32,8,128]{2,1,0:T(8,128)} %shard_map.105), calls=%async_computation.1 | async-start | bytes 262144 | tf_op jit(solution)/shard_map/all_to_all | solution.py:318
  42.8 15.5 %all-to-all-start.2 = ((f32[32,16,128]{2,1,0:T(8,128)}), f32[32,16,128]{2,1,0:T(8,128)S(1)}, u32[]{:S(2)}, u32[]{:S(2)}) async-start(f32[32,16,128]{2,1,0:T(8,128)} %get-tuple-element.9), calls=%async_computation.2 | async-start | bytes 524288 | tf_op jit(solution)/shard_map/all_to_all | solution.py:318
  49.1 5.5 %collective-permute-start.2 = (f32[8,16,384]{2,1,0:T(8,128)S(1)}, f32[8,16,384]{2,1,0:T(8,128)S(1)}, u32[]{:S(2)}, u32[]{:S(2)}) collective-permute-start(f32[8,16,384]{2,1,0:T(8,128)S(1)} %get-tuple-element.10.q_own.image0_ref), channel_id=1, source_target_pairs={{0,8},{8,16},{16,24},{24,32},{32,40},{40,48},{48,56},{56,64},{64,7... | collective-permute-start | bytes 589832 | tf_op jit(solution)/shard_map/ppermute | solution.py:325
  50.8 5.9 %collective-permute-start.3 = (f32[8,16,384]{2,1,0:T(8,128)S(1)}, f32[8,16,384]{2,1,0:T(8,128)S(1)}, u32[]{:S(2)}, u32[]{:S(2)}) collective-permute-start(f32[8,16,384]{2,1,0:T(8,128)S(1)} %get-tuple-element.10.q_own.image0_ref), channel_id=1, source_target_pairs={{8,0},{16,8},{24,16},{32,24},{40,32},{48,40},{56,48},{64,56},{72,6... | collective-permute-start | bytes 589832 | tf_op jit(solution)/shard_map/ppermute | solution.py:325
  66.0 13.7 %all-to-all-start.3 = ((f32[32,8,128]{2,1,0:T(8,128)}), f32[32,8,128]{2,1,0:T(8,128)S(1)}, u32[]{:S(2)}, u32[]{:S(2)}) async-start(f32[32,8,128]{2,1,0:T(8,128)} %get-tuple-element.12), calls=%async_computation.3 | async-start | bytes 262144 | tf_op jit(solution)/shard_map/all_to_all | solution.py:318

commit v6 on v5

--- a/solution.py
+++ b/solution.py
@@ -152,7 +152,8 @@
     return parts[0]
 
 
-def maps_kernel(up_ref, shift_ref, out_ref):
+def maps_kernel(up_ref, shift_ref, pick_ref, out_ref, pick_out):
+    pick_out[...] = pick_ref[...]
     for p in range(PD):
         out_ref[:, p * W : (p + 1) * W] = nn(shift_ref[p], up_ref[p])
 
@@ -242,10 +243,10 @@
         pair = jnp.concatenate(
             [f[...].reshape(ROWS, W), q[...].reshape(ROWS, W)], axis=0
         )
-        mixed = nn(both, pair)
+        mixed = exact(both, pair)
         if i == 1:
             direction = mixed
-            residual = f_own[...].reshape(ROWS, W) + nn(coeffs, q_own[...].reshape(ROWS, W))
+            residual = f_own[...].reshape(ROWS, W) + exact(coeffs, q_own[...].reshape(ROWS, W))
         rounded_ref[i * PD : (i + 1) * PD] = mixed.astype(BF16).reshape(PD, K, W)
     direction_out[...] = direction
     ids.wait()
@@ -351,7 +352,9 @@
     pick_cell = (far_lists[0][:, None] == jnp.arange(count)[None, :]).astype(F32)
     pick_cell = jnp.broadcast_to(pick_cell.reshape(FL * count, 1), (FL * count, 2 * E))
 
-    up = call(maps_kernel, [VMEM] * 2, shape(E, PD * W))(up_maps, shift_up)
+    up, pick_column = call(maps_kernel, [VMEM] * 3, (shape(E, PD * W), shape(K, K)))(
+        up_maps, shift_up, pick_column
+    )
     table = translations[0]
     down = down_maps.transpose(0, 2, 1)
 

time: 82.3 us -> 83.3 us (1.012)
  blocking collectives: 0 us -> 14.8 us
  waiting for transfers between devices: 21 us -> 13.3 us
  starting transfers between devices: 34.4 us -> 29 us
    all_to_all x0 -> x1, blocking collectives: none -> 14.8 us  [swap(): return lax.all_to_all(array, axis, 0, 0, tiled=True)]
    all_to_all x4 -> x3, waiting for transfers between devices: 15.1 us -> 7.47 us  [swap(): return lax.all_to_all(array, axis, 0, 0, tiled=True)]
    all_to_all x4 -> x3, starting transfers between devices: 29.1 us -> 23.5 us  [swap(): return lax.all_to_all(array, axis, 0, 0, tiled=True)]
    ppermute x2, waiting for transfers between devices: 3.8 us -> 0.01 us  [halo(): lax.ppermute(block, axis, forward)]
    ppermute x2, waiting for transfers between devices: 2.09 us -> 5.78 us  [halo(): lax.ppermute(block, axis, backward)]
    ppermute x2, starting transfers between devices: 0.01 us -> 2.83 us  [halo(): lax.ppermute(block, axis, backward)]
    ppermute x2, starting transfers between devices: 5.32 us -> 2.7 us  [halo(): lax.ppermute(block, axis, forward)]
  transfers between devices with their start and end apart: 8 -> 7, of which waited for: 6 -> 4; matrix products, arithmetic and copies ran while one was open for 2% -> 2% of each run, Pallas kernels for 10% -> 10%
where the time goes in v6:
time: 83.3 us; the launch traced here: 82.8 us
  starting transfers between devices  29 us (35%)
  Pallas kernels  19.5 us (23%)
  blocking collectives  14.8 us (18%)
  waiting for transfers between devices  13.3 us (16%)
  local copies, waits for them, and re-layouts  4.64 us (6%)
    all_to_all x3, starting transfers between devices, swap(): return lax.all_to_all(array, axis, 0, 0, tiled=True)  23.5 us
    all_to_all x1, blocking collectives, swap(): return lax.all_to_all(array, axis, 0, 0, tiled=True)  14.8 us
    all_to_all x3, waiting for transfers between devices, swap(): return lax.all_to_all(array, axis, 0, 0, tiled=True)  7.47 us
    pallas_call x1, Pallas kernels, on_device(): call(direction_kernel, [VMEM] * 13 + [HBM], (shape(count, K // 2, ROWS),...  7.04 us
    pallas_call x1, Pallas kernels, on_device(): call(near_kernel, [VMEM] * 4 + [HBM], shape(ROWS, W), (*NEAR_SCRATCH, plt...  6.44 us
    ppermute x2, waiting for transfers between devices, halo(): lax.ppermute(block, axis, backward)  5.78 us
    unnamed x13, local copies, waits for them, and re-layouts  2.86 us
    ppermute x2, starting transfers between devices, halo(): lax.ppermute(block, axis, backward)  2.83 us
  transfers between devices with their start and end apart: 7, of which 4 were waited for; matrix products, arithmetic and copies ran while one was open for 2% of the time, Pallas kernels for 10%

profile of v6, /device:TPU:1, one launch (start us, length us, event | category | flops | bytes accessed | tf_op | source)
XLA Modules:
  0.0 82.8 jit_solution(13865707828972728983)
XLA Ops:
  0.6 0.0 copy-start.1
  0.6 0.0 copy-start
  0.6 1.6 %broadcast_in_dim.5 = f32[8,8,2,384]{3,2,1,0:T(2,128)} broadcast(f32[8,2,384]{2,1,0:T(2,128)} %param.9), dimensions={1,2,3} | broadcast | bytes 221184 | tf_op jit(solution)/shard_map/broadcast_in_dim | solution.py:346
  2.2 9.0 %all-to-all-start = ((f32[8,8,2,384]{3,2,1,0:T(2,128)}), f32[8,8,2,384]{3,2,1,0:T(2,128)S(1)}, u32[]{:S(2)}, u32[]{:S(2)}) async-start(f32[8,8,2,384]{3,2,1,0:T(2,128)} %broadcast_in_dim.5), calls=%async_computation | async-start | bytes 393216 | tf_op jit(solution)/shard_map/all_to_all | solution.py:319
  11.2 0.7 fusion.2
  11.9 0.1 reshape.47
  12.0 0.8 copy.12
  12.8 0.1 fusion.pick_ref
  12.9 0.0 copy-start.2
  12.9 1.1 %copy-done.2 = f32[8,64,384]{2,1,0:T(8,128)S(1)} copy-done((f32[8,64,384]{2,1,0:T(8,128)S(1)}, f32[8,64,384]{2,1,0:T(8,128)}, u32[]{:S(2)}) %copy-start.2) | copy-done | bytes 786456
  14.0 0.0 copy-start.4
  14.0 0.9 %copy-done.4 = f32[8,64,64]{2,1,0:T(8,128)S(1)} copy-done((f32[8,64,64]{2,1,0:T(8,128)S(1)}, f32[8,64,64]{2,1,0:T(8,128)}, u32[]{:S(2)}) %copy-start.4) | copy-done | bytes 131096
  14.9 0.0 copy-start.3
  15.0 0.0 copy-start.5
  15.0 0.5 shard_map.104
  15.4 4.8 %all-to-all-done = f32[8,8,2,384]{3,2,1,0:T(2,128)S(1)} async-done(((f32[8,8,2,384]{3,2,1,0:T(2,128)}), f32[8,8,2,384]{3,2,1,0:T(2,128)S(1)}, u32[]{:S(2)}, u32[]{:S(2)}) %all-to-all-start) | async-done | bytes 196640 | tf_op jit(solution)/shard_map/all_to_all | solution.py:319
  20.2 0.1 copy.15
  20.3 2.5 %collective-permute-start.1 = (f32[8,16,384]{2,1,0:T(8,128)S(1)}, f32[8,16,384]{2,1,0:T(8,128)S(1)}, u32[]{:S(2)}, u32[]{:S(2)}) collective-permute-start(f32[8,16,384]{2,1,0:T(8,128)S(1)} %bitcast.7), channel_id=1, source_target_pairs={{8,0},{16,8},{24,16},{32,24},{40,32},{48,40},{56,48},{64,56},{72,6... | collective-permute-start | bytes 589832 | tf_op jit(solution)/shard_map/ppermute | solution.py:326
  22.8 1.2 %collective-permute-start = (f32[8,16,384]{2,1,0:T(8,128)S(1)}, f32[8,16,384]{2,1,0:T(8,128)S(1)}, u32[]{:S(2)}, u32[]{:S(2)}) collective-permute-start(f32[8,16,384]{2,1,0:T(8,128)S(1)} %bitcast.8), channel_id=1, source_target_pairs={{0,8},{8,16},{16,24},{24,32},{32,40},{40,48},{48,56},{56,64},{64,7... | collective-permute-start | bytes 589832 | tf_op jit(solution)/shard_map/ppermute | solution.py:326
  24.0 1.2 %shard_map.105 = f32[32,8,128]{2,1,0:T(8,128)} custom-call(f32[8,16,384]{2,1,0:T(8,128)S(1)} %bitcast.9, f32[64,3072]{1,0:T(8,128)S(1)} %get-tuple-element.12.up_ref), custom_call_target="tpu_custom_call" | custom-call | flops 1000000 | bytes 1000000 | tf_op jit(solution)/shard_map/pallas_call | solution.py:362
  25.1 8.2 %all-to-all-start.1 = ((f32[32,8,128]{2,1,0:T(8,128)}), f32[32,8,128]{2,1,0:T(8,128)S(1)}, u32[]{:S(2)}, u32[]{:S(2)}) async-start(f32[32,8,128]{2,1,0:T(8,128)} %shard_map.105), calls=%async_computation.1 | async-start | bytes 262144 | tf_op jit(solution)/shard_map/all_to_all | solution.py:319
  33.4 0.0 collective-permute-done.1.high_ref.f_high
  33.4 0.0 collective-permute-done.low_ref.f_low
  33.4 6.4 %shard_map.106.near_ref = f32[128,384]{1,0:T(8,128)S(1)} custom-call(s32[8,4]{1,0:T(8,128)S(1)} %add_select_fusion.ids_ref, f32[8,16,384]{2,1,0:T(8,128)S(1)} %collective-permute-done.low_ref.f_low, f32[8,16,384]{2,1,0:T(8,128)S(1)} %bitcast.10, f32[8,16,384]{2,1,0:T(8,128)S(1)} %collective-permute-done.1.high_ref.f_high, bf16[8,4,384,384]{3,2,1,0:T(8,128)(2,1)} %near_ref.3), custom_call_target="tpu_custom_call" | custom-call | flops 1000000 | bytes 1000000 | tf_op jit(solution)/shard_map/pallas_call | solution.py:364
  39.8 1.1 %all-to-all-done.1.gathered_ref = f32[32,8,128]{2,1,0:T(8,128)S(1)} async-done(((f32[32,8,128]{2,1,0:T(8,128)}), f32[32,8,128]{2,1,0:T(8,128)S(1)}, u32[]{:S(2)}, u32[]{:S(2)}) %all-to-all-start.1) | async-done | bytes 131104 | tf_op jit(solution)/shard_map/all_to_all | solution.py:319
  41.0 0.1 broadcast_in_dim.4.pick_ref
  41.0 0.0 copy-done.1
  41.0 0.0 copy-done
  41.0 0.0 copy-done.3
  41.1 2.4 %shard_map.107 = (f32[8,16,384]{2,1,0:T(8,128)S(1)}, f32[16,128]{1,0:T(8,128)S(1)}, f32[32,16,128]{2,1,0:T(8,128)}) custom-call(f32[128,128]{1,0:T(8,128)S(1)} %broadcast_in_dim.4.pick_ref, f32[32,8,128]{2,1,0:T(8,128)S(1)} %all-to-all-done.1.gathered_ref, f32[128,384]{1,0:T(8,128)S(1)} %shard_map.106.near_ref, f32[8,16,384]{2,1,0:T(8,128)S(1)} %bitcast.11, ...), custom_call_target="tpu_custom_call" | custom-call | flops 1000000 | bytes 1000000 | tf_op jit(solution)/shard_map/pallas_call | solution.py:373
  43.4 6.3 %all-to-all-start.2 = ((f32[32,16,128]{2,1,0:T(8,128)}), f32[32,16,128]{2,1,0:T(8,128)S(1)}, u32[]{:S(2)}, u32[]{:S(2)}) async-start(f32[32,16,128]{2,1,0:T(8,128)} %get-tuple-element.13), calls=%async_computation.2 | async-start | bytes 524288 | tf_op jit(solution)/shard_map/all_to_all | solution.py:319
  49.7 0.3 collective-permute-start.3
  50.0 1.5 %collective-permute-start.2 = (f32[8,16,384]{2,1,0:T(8,128)S(1)}, f32[8,16,384]{2,1,0:T(8,128)S(1)}, u32[]{:S(2)}, u32[]{:S(2)}) collective-permute-start(f32[8,16,384]{2,1,0:T(8,128)S(1)} %get-tuple-element.14.q_own.image0_ref), channel_id=1, source_target_pairs={{0,8},{8,16},{16,24},{24,32},{32,40},{40,48},{48,56},{56,64},{64,7... | collective-permute-start | bytes 589832 | tf_op jit(solution)/shard_map/ppermute | solution.py:326
  51.5 5.8 %collective-permute-done.3.q_high = f32[8,16,384]{2,1,0:T(8,128)S(1)} collective-permute-done((f32[8,16,384]{2,1,0:T(8,128)S(1)}, f32[8,16,384]{2,1,0:T(8,128)S(1)}, u32[]{:S(2)}, u32[]{:S(2)}) %collective-permute-start.3) | collective-permute-done | bytes 196640 | tf_op jit(solution)/shard_map/ppermute | solution.py:326
  57.3 0.0 collective-permute-done.2.q_low
  57.3 1.6 %all-to-all-done.2.gathered_ref = f32[32,16,128]{2,1,0:T(8,128)S(1)} async-done(((f32[32,16,128]{2,1,0:T(8,128)}), f32[32,16,128]{2,1,0:T(8,128)S(1)}, u32[]{:S(2)}, u32[]{:S(2)}) %all-to-all-start.2) | async-done | bytes 262176 | tf_op jit(solution)/shard_map/all_to_all | solution.py:319
  58.9 0.0 copy-done.5
  58.9 7.0 %shard_map.108 = (f32[32,8,128]{2,1,0:T(8,128)S(1)}, f32[128,384]{1,0:T(8,128)S(1)}, f32[128,384]{1,0:T(8,128)S(1)}, f32[16,128]{1,0:T(8,128)S(1)}) custom-call(s32[8,4]{1,0:T(8,128)S(1)} %add_select_fusion.ids_ref, s32[1,4]{1,0:T(1,128)S(1)} %copy-done.5, f32[32,16,128]{2,1,0:T(8,128)S(1)} %all-to-all-done.2.gathered_ref, ...), custom_call_target="tpu_custom_call" | custom-call | flops 1000000 | bytes 1000000 | tf_op jit(solution)/shard_map/pallas_call | solution.py:381
  65.9 14.8 %all_to_all.20.gathered_ref = f32[32,8,128]{2,1,0:T(8,128)S(1)} all-to-all(f32[32,8,128]{2,1,0:T(8,128)S(1)} %get-tuple-element.16), channel_id=1, replica_groups=mesh['patch'=32,'rhs'=8] {'patch'}, dimensions={0} | all-to-all | bytes 262144 | tf_op jit(solution)/shard_map/all_to_all | solution.py:319
  80.8 2.1 %shard_map.109 = (f32[8,2,384]{2,1,0:T(2,128)}, f32[8,2,384]{2,1,0:T(2,128)}) custom-call(f32[16,16]{1,0:T(8,128)S(1)} %get-tuple-element.11.pick_ref, f32[32,8,128]{2,1,0:T(8,128)S(1)} %all_to_all.20.gathered_ref, f32[16,128]{1,0:T(8,128)S(1)} %get-tuple-element.17.alpha_ref, f32[8,16,384]{2,1,0:T(8,128)S(1)} %bitcast.13, ...), custom_call_target="tpu_custom_call" | custom-call | flops 1000000 | bytes 1000000 | tf_op jit(solution)/shard_map/pallas_call | solution.py:393
  (2 shorter events, 0.0 us)
Async XLA Ops:
  0.6 40.4 %copy-start.1 = (f32[8,64,64]{2,1,0:T(8,128)S(1)}, f32[8,64,64]{2,1,0:T(8,128)}, u32[]{:S(2)}) copy-start(f32[8,64,64]{2,1,0:T(8,128)} %shift_ref.5) | copy-start | bytes 393220
  0.6 40.4 %copy-start = (f32[8,384,64]{1,2,0:T(8,128)S(1)}, f32[8,384,64]{1,2,0:T(8,128)}, u32[]{:S(2)}) copy-start(f32[8,384,64]{1,2,0:T(8,128)} %param.17) | copy-start | bytes 2359300
  2.2 18.0 %all-to-all-start = ((f32[8,8,2,384]{3,2,1,0:T(2,128)}), f32[8,8,2,384]{3,2,1,0:T(2,128)S(1)}, u32[]{:S(2)}, u32[]{:S(2)}) async-start(f32[8,8,2,384]{3,2,1,0:T(2,128)} %broadcast_in_dim.5), calls=%async_computation | async-start | bytes 393216 | tf_op jit(solution)/shard_map/all_to_all | solution.py:319
  12.9 1.1 %copy-start.2 = (f32[8,64,384]{2,1,0:T(8,128)S(1)}, f32[8,64,384]{2,1,0:T(8,128)}, u32[]{:S(2)}) copy-start(f32[8,64,384]{2,1,0:T(8,128)} %up_ref.1) | copy-start | bytes 2359300
  14.0 0.9 %copy-start.4 = (f32[8,64,64]{2,1,0:T(8,128)S(1)}, f32[8,64,64]{2,1,0:T(8,128)}, u32[]{:S(2)}) copy-start(f32[8,64,64]{2,1,0:T(8,128)} %shift_ref.3) | copy-start | bytes 393220
  14.9 26.1 %copy-start.3 = (f32[1,4,64,64]{3,2,1,0:T(8,128)S(1)}, f32[1,4,64,64]{3,2,1,0:T(8,128)}, u32[]{:S(2)}) copy-start(f32[1,4,64,64]{3,2,1,0:T(8,128)} %param.15) | copy-start | bytes 196612
  15.0 43.9 %copy-start.5 = (s32[1,4]{1,0:T(1,128)S(1)}, s32[1,4]{1,0:T(1,128)}, u32[]{:S(2)}) copy-start(s32[1,4]{1,0:T(1,128)} %far_ref.1) | copy-start | bytes 52
  20.3 13.1 %collective-permute-start.1 = (f32[8,16,384]{2,1,0:T(8,128)S(1)}, f32[8,16,384]{2,1,0:T(8,128)S(1)}, u32[]{:S(2)}, u32[]{:S(2)}) collective-permute-start(f32[8,16,384]{2,1,0:T(8,128)S(1)} %bitcast.7), channel_id=1, source_target_pairs={{8,0},{16,8},{24,16},{32,24},{40,32},{48,40},{56,48},{64,56},{72,6... | collective-permute-start | bytes 589832 | tf_op jit(solution)/shard_map/ppermute | solution.py:326
  22.8 10.6 %collective-permute-start = (f32[8,16,384]{2,1,0:T(8,128)S(1)}, f32[8,16,384]{2,1,0:T(8,128)S(1)}, u32[]{:S(2)}, u32[]{:S(2)}) collective-permute-start(f32[8,16,384]{2,1,0:T(8,128)S(1)} %bitcast.8), channel_id=1, source_target_pairs={{0,8},{8,16},{16,24},{24,32},{32,40},{40,48},{48,56},{56,64},{64,7... | collective-permute-start | bytes 589832 | tf_op jit(solution)/shard_map/ppermute | solution.py:326
  25.1 15.8 %all-to-all-start.1 = ((f32[32,8,128]{2,1,0:T(8,128)}), f32[32,8,128]{2,1,0:T(8,128)S(1)}, u32[]{:S(2)}, u32[]{:S(2)}) async-start(f32[32,8,128]{2,1,0:T(8,128)} %shard_map.105), calls=%async_computation.1 | async-start | bytes 262144 | tf_op jit(solution)/shard_map/all_to_all | solution.py:319
  43.4 15.5 %all-to-all-start.2 = ((f32[32,16,128]{2,1,0:T(8,128)}), f32[32,16,128]{2,1,0:T(8,128)S(1)}, u32[]{:S(2)}, u32[]{:S(2)}) async-start(f32[32,16,128]{2,1,0:T(8,128)} %get-tuple-element.13), calls=%async_computation.2 | async-start | bytes 524288 | tf_op jit(solution)/shard_map/all_to_all | solution.py:319
  49.7 7.6 %collective-permute-start.3 = (f32[8,16,384]{2,1,0:T(8,128)S(1)}, f32[8,16,384]{2,1,0:T(8,128)S(1)}, u32[]{:S(2)}, u32[]{:S(2)}) collective-permute-start(f32[8,16,384]{2,1,0:T(8,128)S(1)} %get-tuple-element.14.q_own.image0_ref), channel_id=1, source_target_pairs={{8,0},{16,8},{24,16},{32,24},{40,32},{48,40},{56,48},{64,56},{72,6... | collective-permute-start | bytes 589832 | tf_op jit(solution)/shard_map/ppermute | solution.py:326
  50.0 7.3 %collective-permute-start.2 = (f32[8,16,384]{2,1,0:T(8,128)S(1)}, f32[8,16,384]{2,1,0:T(8,128)S(1)}, u32[]{:S(2)}, u32[]{:S(2)}) collective-permute-start(f32[8,16,384]{2,1,0:T(8,128)S(1)} %get-tuple-element.14.q_own.image0_ref), channel_id=1, source_target_pairs={{0,8},{8,16},{16,24},{24,32},{32,40},{40,48},{48,56},{56,64},{64,7... | collective-permute-start | bytes 589832 | tf_op jit(solution)/shard_map/ppermute | solution.py:326

commit v7 on v6

--- a/solution.py
+++ b/solution.py
@@ -272,24 +272,24 @@
     return jnp.where(row // 2 == lane // K, tiled(small(pick, coeffs_t)), 0.0)
 
 
-def last_step_kernel(
-    pick_ref, gathered_ref, alpha_ref, field_ref, image0_ref, direction_ref, image_ref,
-    x_out, r_out,
-):
-    total = total_of(gathered_ref)
-    total = jnp.concatenate([total[:, : 2 * K], total[:, 2 * K : 4 * K]], axis=0)
+def first_step_kernel(pick_ref, alpha_ref, field_ref, image_ref, x_out, r_out):
     pick = pick_ref[...]
-    qd = total[:, :K]
     field = field_ref[...].reshape(ROWS, W)
     row, lane = iotas(K, ROWS)
     mine = jnp.where(row // 2 == lane // K, tiled(pick), 0.0)
-    coeffs0 = own_coeffs(pick, alpha_ref[:, :K])
-    x = nn(coeffs0, field)
-    r = exact(mine, field) - exact(coeffs0, image0_ref[...].reshape(ROWS, W))
+    coeffs = own_coeffs(pick, alpha_ref[:, :K])
+    x_out[...] = exact(coeffs, field)
+    r_out[...] = exact(mine, field) - exact(coeffs, image_ref[...].reshape(ROWS, W))
+
+
+def last_step_kernel(pick_ref, gathered_ref, direction_ref, image_ref, x_ref, r_ref, x_out, r_out):
+    total = total_of(gathered_ref)
+    total = jnp.concatenate([total[:, : 2 * K], total[:, 2 * K : 4 * K]], axis=0)
+    qd = total[:, :K]
     alpha_t = small(total[:, K : 2 * K], inverse(0.5 * (qd + qd.T)))
-    coeffs = own_coeffs(pick, alpha_t)
-    x = x + nn(coeffs, direction_ref[...])
-    r = r - nn(coeffs, image_ref[...])
+    coeffs = own_coeffs(pick_ref[...], alpha_t)
+    x = x_ref[...] + nn(coeffs, direction_ref[...])
+    r = r_ref[...] - nn(coeffs, image_ref[...])
     for p in range(PD):
         x_out[p] = x[2 * p : 2 * p + 2]
         r_out[p] = r[2 * p : 2 * p + 2]
@@ -323,7 +323,9 @@
     count = lax.axis_size(axis)
     forward = [(i, (i + 1) % count) for i in range(count)]
     backward = [(target, source) for source, target in forward]
-    return lax.ppermute(block, axis, forward), lax.ppermute(block, axis, backward)
+    low = lax.ppermute(block, axis, forward)
+    high = lax.ppermute(block, axis, backward)
+    return low, high
 
 
 def on_device(
@@ -390,8 +392,11 @@
     )
 
     gathered = swap(message, "patch")
-    return call(last_step_kernel, [VMEM] * 7, (shape(PD, 2, W),) * 2)(
-        pick_column, gathered, alpha, field, image, direction, image1
+    x, r = call(first_step_kernel, [VMEM] * 4, (shape(2 * PD, W),) * 2)(
+        pick_column, alpha, field, image
+    )
+    return call(last_step_kernel, [VMEM] * 6, (shape(PD, 2, W),) * 2)(
+        pick_column, gathered, direction, image1, x, r
     )
 
 

time: 83.3 us -> 84.8 us (1.018)
  blocking collectives: 14.8 us -> 0 us
  starting transfers between devices: 29 us -> 37 us
  waiting for transfers between devices: 13.3 us -> 20.2 us
  Pallas kernels: 19.5 us -> 20.9 us
    all_to_all x1 -> x0, blocking collectives: 14.8 us -> none  [swap(): return lax.all_to_all(array, axis, 0, 0, tiled=True)]
    all_to_all x3 -> x4, starting transfers between devices: 23.5 us -> 31.5 us  [swap(): return lax.all_to_all(array, axis, 0, 0, tiled=True)]
    all_to_all x3 -> x4, waiting for transfers between devices: 7.47 us -> 14.4 us  [swap(): return lax.all_to_all(array, axis, 0, 0, tiled=True)]
    pallas_call x1 -> x2, Pallas kernels: 2.09 us -> 2.81 us  [the longest x1 2.05 us: on_device(): call(last_step_kernel, [VMEM] * 6, (shape(PD, 2, W),) * 2)]
  transfers between devices with their start and end apart: 7 -> 8, of which waited for: 4 -> 5; matrix products, arithmetic and copies ran while one was open for 2% -> 2% of each run, Pallas kernels for 10% -> 10%
where the time goes in v7:
time: 84.8 us; the launch traced here: 84.3 us
  starting transfers between devices  37 us (44%)
  Pallas kernels  20.9 us (25%)
  waiting for transfers between devices  20.2 us (24%)
  local copies, waits for them, and re-layouts  4.62 us (5%)
    all_to_all x4, starting transfers between devices, swap(): return lax.all_to_all(array, axis, 0, 0, tiled=True)  31.5 us
    all_to_all x4, waiting for transfers between devices, swap(): return lax.all_to_all(array, axis, 0, 0, tiled=True)  14.4 us
    pallas_call x1, Pallas kernels, on_device(): call(direction_kernel, [VMEM] * 13 + [HBM], (shape(count, K // 2, ROWS),...  7.68 us
    pallas_call x1, Pallas kernels, on_device(): call(near_kernel, [VMEM] * 4 + [HBM], shape(ROWS, W), (*NEAR_SCRATCH, plt...  6.44 us
    ppermute x2, waiting for transfers between devices, halo(): high = lax.ppermute(block, axis, backward)  5.78 us
    unnamed x13, local copies, waits for them, and re-layouts  2.86 us
    ppermute x2, starting transfers between devices, halo(): high = lax.ppermute(block, axis, backward)  2.83 us
    ppermute x2, starting transfers between devices, halo(): low = lax.ppermute(block, axis, forward)  2.7 us
  transfers between devices with their start and end apart: 8, of which 5 were waited for; matrix products, arithmetic and copies ran while one was open for 2% of the time, Pallas kernels for 10%

profile of v7, /device:TPU:1, one launch (start us, length us, event | category | flops | bytes accessed | tf_op | source)
XLA Modules:
  0.0 84.3 jit_solution(7538776913833549212)
XLA Ops:
  0.6 0.0 copy-start.1
  0.6 0.0 copy-start
  0.6 1.5 %broadcast_in_dim.5 = f32[8,8,2,384]{3,2,1,0:T(2,128)} broadcast(f32[8,2,384]{2,1,0:T(2,128)} %param.9), dimensions={1,2,3} | broadcast | bytes 221184 | tf_op jit(solution)/shard_map/broadcast_in_dim | solution.py:348
  2.2 9.0 %all-to-all-start = ((f32[8,8,2,384]{3,2,1,0:T(2,128)}), f32[8,8,2,384]{3,2,1,0:T(2,128)S(1)}, u32[]{:S(2)}, u32[]{:S(2)}) async-start(f32[8,8,2,384]{3,2,1,0:T(2,128)} %broadcast_in_dim.5), calls=%async_computation | async-start | bytes 393216 | tf_op jit(solution)/shard_map/all_to_all | solution.py:319
  11.2 0.7 fusion.2
  11.9 0.1 reshape.47
  12.0 0.8 copy.12
  12.8 0.1 fusion.pick_ref
  12.8 0.0 copy-start.2
  12.8 1.1 %copy-done.2 = f32[8,64,384]{2,1,0:T(8,128)S(1)} copy-done((f32[8,64,384]{2,1,0:T(8,128)S(1)}, f32[8,64,384]{2,1,0:T(8,128)}, u32[]{:S(2)}) %copy-start.2) | copy-done | bytes 786456
  14.0 0.0 copy-start.4
  14.0 0.9 %copy-done.4 = f32[8,64,64]{2,1,0:T(8,128)S(1)} copy-done((f32[8,64,64]{2,1,0:T(8,128)S(1)}, f32[8,64,64]{2,1,0:T(8,128)}, u32[]{:S(2)}) %copy-start.4) | copy-done | bytes 131096
  14.9 0.0 copy-start.3
  14.9 0.0 copy-start.5
  14.9 0.4 shard_map.104
  15.4 4.8 %all-to-all-done = f32[8,8,2,384]{3,2,1,0:T(2,128)S(1)} async-done(((f32[8,8,2,384]{3,2,1,0:T(2,128)}), f32[8,8,2,384]{3,2,1,0:T(2,128)S(1)}, u32[]{:S(2)}, u32[]{:S(2)}) %all-to-all-start) | async-done | bytes 196640 | tf_op jit(solution)/shard_map/all_to_all | solution.py:319
  20.2 0.1 copy.15
  20.3 2.5 %collective-permute-start.1 = (f32[8,16,384]{2,1,0:T(8,128)S(1)}, f32[8,16,384]{2,1,0:T(8,128)S(1)}, u32[]{:S(2)}, u32[]{:S(2)}) collective-permute-start(f32[8,16,384]{2,1,0:T(8,128)S(1)} %bitcast.7), channel_id=1, source_target_pairs={{8,0},{16,8},{24,16},{32,24},{40,32},{48,40},{56,48},{64,56},{72,6... | collective-permute-start | bytes 589832 | tf_op jit(solution)/shard_map/ppermute | solution.py:327
  22.8 1.2 %collective-permute-start = (f32[8,16,384]{2,1,0:T(8,128)S(1)}, f32[8,16,384]{2,1,0:T(8,128)S(1)}, u32[]{:S(2)}, u32[]{:S(2)}) collective-permute-start(f32[8,16,384]{2,1,0:T(8,128)S(1)} %bitcast.8), channel_id=1, source_target_pairs={{0,8},{8,16},{16,24},{24,32},{32,40},{40,48},{48,56},{56,64},{64,7... | collective-permute-start | bytes 589832 | tf_op jit(solution)/shard_map/ppermute | solution.py:326
  24.0 1.1 %shard_map.105 = f32[32,8,128]{2,1,0:T(8,128)} custom-call(f32[8,16,384]{2,1,0:T(8,128)S(1)} %bitcast.9, f32[64,3072]{1,0:T(8,128)S(1)} %get-tuple-element.14.up_ref), custom_call_target="tpu_custom_call" | custom-call | flops 1000000 | bytes 1000000 | tf_op jit(solution)/shard_map/pallas_call | solution.py:364
  25.1 8.2 %all-to-all-start.1 = ((f32[32,8,128]{2,1,0:T(8,128)}), f32[32,8,128]{2,1,0:T(8,128)S(1)}, u32[]{:S(2)}, u32[]{:S(2)}) async-start(f32[32,8,128]{2,1,0:T(8,128)} %shard_map.105), calls=%async_computation.1 | async-start | bytes 262144 | tf_op jit(solution)/shard_map/all_to_all | solution.py:319
  33.3 0.0 collective-permute-done.1.high_ref.f_high
  33.3 0.0 collective-permute-done.low_ref.f_low
  33.3 6.4 %shard_map.106.near_ref = f32[128,384]{1,0:T(8,128)S(1)} custom-call(s32[8,4]{1,0:T(8,128)S(1)} %add_select_fusion.ids_ref, f32[8,16,384]{2,1,0:T(8,128)S(1)} %collective-permute-done.low_ref.f_low, f32[8,16,384]{2,1,0:T(8,128)S(1)} %bitcast.10, f32[8,16,384]{2,1,0:T(8,128)S(1)} %collective-permute-done.1.high_ref.f_high, bf16[8,4,384,384]{3,2,1,0:T(8,128)(2,1)} %near_ref.3), custom_call_target="tpu_custom_call" | custom-call | flops 1000000 | bytes 1000000 | tf_op jit(solution)/shard_map/pallas_call | solution.py:366
  39.8 1.1 %all-to-all-done.1.gathered_ref = f32[32,8,128]{2,1,0:T(8,128)S(1)} async-done(((f32[32,8,128]{2,1,0:T(8,128)}), f32[32,8,128]{2,1,0:T(8,128)S(1)}, u32[]{:S(2)}, u32[]{:S(2)}) %all-to-all-start.1) | async-done | bytes 131104 | tf_op jit(solution)/shard_map/all_to_all | solution.py:319
  40.9 0.1 broadcast_in_dim.4.pick_ref
  41.0 0.0 copy-done.1
  41.0 0.0 copy-done
  41.0 0.0 copy-done.3
  41.0 2.3 %shard_map.107 = (f32[8,16,384]{2,1,0:T(8,128)S(1)}, f32[16,128]{1,0:T(8,128)S(1)}, f32[32,16,128]{2,1,0:T(8,128)}) custom-call(f32[128,128]{1,0:T(8,128)S(1)} %broadcast_in_dim.4.pick_ref, f32[32,8,128]{2,1,0:T(8,128)S(1)} %all-to-all-done.1.gathered_ref, f32[128,384]{1,0:T(8,128)S(1)} %shard_map.106.near_ref, f32[8,16,384]{2,1,0:T(8,128)S(1)} %bitcast.11, ...), custom_call_target="tpu_custom_call" | custom-call | flops 1000000 | bytes 1000000 | tf_op jit(solution)/shard_map/pallas_call | solution.py:375
  43.3 6.3 %all-to-all-start.2 = ((f32[32,16,128]{2,1,0:T(8,128)}), f32[32,16,128]{2,1,0:T(8,128)S(1)}, u32[]{:S(2)}, u32[]{:S(2)}) async-start(f32[32,16,128]{2,1,0:T(8,128)} %get-tuple-element.15), calls=%async_computation.2 | async-start | bytes 524288 | tf_op jit(solution)/shard_map/all_to_all | solution.py:319
  49.6 0.3 collective-permute-start.3
  49.9 1.5 %collective-permute-start.2 = (f32[8,16,384]{2,1,0:T(8,128)S(1)}, f32[8,16,384]{2,1,0:T(8,128)S(1)}, u32[]{:S(2)}, u32[]{:S(2)}) collective-permute-start(f32[8,16,384]{2,1,0:T(8,128)S(1)} %get-tuple-element.16.q_own.image_ref), channel_id=1, source_target_pairs={{0,8},{8,16},{16,24},{24,32},{32,40},{40,48},{48,56},{56,64},{64,7... | collective-permute-start | bytes 589832 | tf_op jit(solution)/shard_map/ppermute | solution.py:326
  51.5 5.8 %collective-permute-done.3.q_high = f32[8,16,384]{2,1,0:T(8,128)S(1)} collective-permute-done((f32[8,16,384]{2,1,0:T(8,128)S(1)}, f32[8,16,384]{2,1,0:T(8,128)S(1)}, u32[]{:S(2)}, u32[]{:S(2)}) %collective-permute-start.3) | collective-permute-done | bytes 196640 | tf_op jit(solution)/shard_map/ppermute | solution.py:327
  57.2 0.0 collective-permute-done.2.q_low
  57.2 1.6 %all-to-all-done.2.gathered_ref = f32[32,16,128]{2,1,0:T(8,128)S(1)} async-done(((f32[32,16,128]{2,1,0:T(8,128)}), f32[32,16,128]{2,1,0:T(8,128)S(1)}, u32[]{:S(2)}, u32[]{:S(2)}) %all-to-all-start.2) | async-done | bytes 262176 | tf_op jit(solution)/shard_map/all_to_all | solution.py:319
  58.8 0.0 copy-done.5
  58.8 7.7 %shard_map.108 = (f32[32,8,128]{2,1,0:T(8,128)}, f32[128,384]{1,0:T(8,128)S(1)}, f32[128,384]{1,0:T(8,128)S(1)}, f32[16,128]{1,0:T(8,128)S(1)}) custom-call(s32[8,4]{1,0:T(8,128)S(1)} %add_select_fusion.ids_ref, s32[1,4]{1,0:T(1,128)S(1)} %copy-done.5, f32[32,16,128]{2,1,0:T(8,128)S(1)} %all-to-all-done.2.gathered_ref, ...), custom_call_target="tpu_custom_call" | custom-call | flops 1000000 | bytes 1000000 | tf_op jit(solution)/shard_map/pallas_call | solution.py:383
  66.5 8.0 %all-to-all-start.3 = ((f32[32,8,128]{2,1,0:T(8,128)}), f32[32,8,128]{2,1,0:T(8,128)S(1)}, u32[]{:S(2)}, u32[]{:S(2)}) async-start(f32[32,8,128]{2,1,0:T(8,128)} %get-tuple-element.18), calls=%async_computation.3 | async-start | bytes 262144 | tf_op jit(solution)/shard_map/all_to_all | solution.py:319
  74.5 0.8 shard_map.109
  75.3 6.9 %all-to-all-done.3.gathered_ref = f32[32,8,128]{2,1,0:T(8,128)S(1)} async-done(((f32[32,8,128]{2,1,0:T(8,128)}), f32[32,8,128]{2,1,0:T(8,128)S(1)}, u32[]{:S(2)}, u32[]{:S(2)}) %all-to-all-start.3) | async-done | bytes 131104 | tf_op jit(solution)/shard_map/all_to_all | solution.py:319
  82.2 2.0 %shard_map.110 = (f32[8,2,384]{2,1,0:T(2,128)}, f32[8,2,384]{2,1,0:T(2,128)}) custom-call(f32[16,16]{1,0:T(8,128)S(1)} %get-tuple-element.13.pick_ref, f32[32,8,128]{2,1,0:T(8,128)S(1)} %all-to-all-done.3.gathered_ref, f32[128,384]{1,0:T(8,128)S(1)} %get-tuple-element.19.direction_ref, f32[128,384]{1,0:T(8,128)S(1)} %get-tuple-element.20.image_ref, ...), custom_call_target="tpu_custom_call" | custom-call | flops 1000000 | bytes 1000000 | tf_op jit(solution)/shard_map/pallas_call | solution.py:398
  (2 shorter events, 0.0 us)
Async XLA Ops:
  0.6 40.3 %copy-start.1 = (f32[8,64,64]{2,1,0:T(8,128)S(1)}, f32[8,64,64]{2,1,0:T(8,128)}, u32[]{:S(2)}) copy-start(f32[8,64,64]{2,1,0:T(8,128)} %shift_ref.5) | copy-start | bytes 393220
  0.6 40.3 %copy-start = (f32[8,384,64]{1,2,0:T(8,128)S(1)}, f32[8,384,64]{1,2,0:T(8,128)}, u32[]{:S(2)}) copy-start(f32[8,384,64]{1,2,0:T(8,128)} %param.17) | copy-start | bytes 2359300
  2.2 18.0 %all-to-all-start = ((f32[8,8,2,384]{3,2,1,0:T(2,128)}), f32[8,8,2,384]{3,2,1,0:T(2,128)S(1)}, u32[]{:S(2)}, u32[]{:S(2)}) async-start(f32[8,8,2,384]{3,2,1,0:T(2,128)} %broadcast_in_dim.5), calls=%async_computation | async-start | bytes 393216 | tf_op jit(solution)/shard_map/all_to_all | solution.py:319
  12.8 1.1 %copy-start.2 = (f32[8,64,384]{2,1,0:T(8,128)S(1)}, f32[8,64,384]{2,1,0:T(8,128)}, u32[]{:S(2)}) copy-start(f32[8,64,384]{2,1,0:T(8,128)} %up_ref.1) | copy-start | bytes 2359300
  14.0 0.9 %copy-start.4 = (f32[8,64,64]{2,1,0:T(8,128)S(1)}, f32[8,64,64]{2,1,0:T(8,128)}, u32[]{:S(2)}) copy-start(f32[8,64,64]{2,1,0:T(8,128)} %shift_ref.3) | copy-start | bytes 393220
  14.9 26.1 %copy-start.3 = (f32[1,4,64,64]{3,2,1,0:T(8,128)S(1)}, f32[1,4,64,64]{3,2,1,0:T(8,128)}, u32[]{:S(2)}) copy-start(f32[1,4,64,64]{3,2,1,0:T(8,128)} %param.15) | copy-start | bytes 196612
  14.9 43.9 %copy-start.5 = (s32[1,4]{1,0:T(1,128)S(1)}, s32[1,4]{1,0:T(1,128)}, u32[]{:S(2)}) copy-start(s32[1,4]{1,0:T(1,128)} %far_ref.1) | copy-start | bytes 52
  20.3 13.1 %collective-permute-start.1 = (f32[8,16,384]{2,1,0:T(8,128)S(1)}, f32[8,16,384]{2,1,0:T(8,128)S(1)}, u32[]{:S(2)}, u32[]{:S(2)}) collective-permute-start(f32[8,16,384]{2,1,0:T(8,128)S(1)} %bitcast.7), channel_id=1, source_target_pairs={{8,0},{16,8},{24,16},{32,24},{40,32},{48,40},{56,48},{64,56},{72,6... | collective-permute-start | bytes 589832 | tf_op jit(solution)/shard_map/ppermute | solution.py:327
  22.8 10.6 %collective-permute-start = (f32[8,16,384]{2,1,0:T(8,128)S(1)}, f32[8,16,384]{2,1,0:T(8,128)S(1)}, u32[]{:S(2)}, u32[]{:S(2)}) collective-permute-start(f32[8,16,384]{2,1,0:T(8,128)S(1)} %bitcast.8), channel_id=1, source_target_pairs={{0,8},{8,16},{16,24},{24,32},{32,40},{40,48},{48,56},{56,64},{64,7... | collective-permute-start | bytes 589832 | tf_op jit(solution)/shard_map/ppermute | solution.py:326
  25.1 15.8 %all-to-all-start.1 = ((f32[32,8,128]{2,1,0:T(8,128)}), f32[32,8,128]{2,1,0:T(8,128)S(1)}, u32[]{:S(2)}, u32[]{:S(2)}) async-start(f32[32,8,128]{2,1,0:T(8,128)} %shard_map.105), calls=%async_computation.1 | async-start | bytes 262144 | tf_op jit(solution)/shard_map/all_to_all | solution.py:319
  43.3 15.5 %all-to-all-start.2 = ((f32[32,16,128]{2,1,0:T(8,128)}), f32[32,16,128]{2,1,0:T(8,128)S(1)}, u32[]{:S(2)}, u32[]{:S(2)}) async-start(f32[32,16,128]{2,1,0:T(8,128)} %get-tuple-element.15), calls=%async_computation.2 | async-start | bytes 524288 | tf_op jit(solution)/shard_map/all_to_all | solution.py:319
  49.6 7.6 %collective-permute-start.3 = (f32[8,16,384]{2,1,0:T(8,128)S(1)}, f32[8,16,384]{2,1,0:T(8,128)S(1)}, u32[]{:S(2)}, u32[]{:S(2)}) collective-permute-start(f32[8,16,384]{2,1,0:T(8,128)S(1)} %get-tuple-element.16.q_own.image_ref), channel_id=1, source_target_pairs={{8,0},{16,8},{24,16},{32,24},{40,32},{48,40},{56,48},{64,56},{72,6... | collective-permute-start | bytes 589832 | tf_op jit(solution)/shard_map/ppermute | solution.py:327
  49.9 7.3 %collective-permute-start.2 = (f32[8,16,384]{2,1,0:T(8,128)S(1)}, f32[8,16,384]{2,1,0:T(8,128)S(1)}, u32[]{:S(2)}, u32[]{:S(2)}) collective-permute-start(f32[8,16,384]{2,1,0:T(8,128)S(1)} %get-tuple-element.16.q_own.image_ref), channel_id=1, source_target_pairs={{0,8},{8,16},{16,24},{24,32},{32,40},{40,48},{48,56},{56,64},{64,7... | collective-permute-start | bytes 589832 | tf_op jit(solution)/shard_map/ppermute | solution.py:326
  66.5 15.7 %all-to-all-start.3 = ((f32[32,8,128]{2,1,0:T(8,128)}), f32[32,8,128]{2,1,0:T(8,128)S(1)}, u32[]{:S(2)}, u32[]{:S(2)}) async-start(f32[32,8,128]{2,1,0:T(8,128)} %get-tuple-element.18), calls=%async_computation.3 | async-start | bytes 262144 | tf_op jit(solution)/shard_map/all_to_all | solution.py:319

commit v8 on v7

--- a/solution.py
+++ b/solution.py
@@ -166,12 +166,12 @@
 
 
 def near_kernel(
-    ids_ref, low_ref, own_ref, high_ref, near_ref, out_ref, blocks_ref, rounded_ref, ids_smem, sems
+    ids_ref, partner_ref, own_ref, beyond_ref, near_ref, out_ref, blocks_ref, rounded_ref, ids_smem, sems
 ):
     ids = pltpu.make_async_copy(ids_ref, ids_smem, sems.at[PD])
     ids.start()
     fetch(near_ref, blocks_ref, sems)
-    for i, ref in enumerate((low_ref, own_ref, high_ref)):
+    for i, ref in enumerate((partner_ref, own_ref, beyond_ref)):
         rounded_ref[i * PD : (i + 1) * PD] = ref[...].astype(BF16)
     ids.wait()
     fetched(near_ref, blocks_ref, sems)
@@ -207,7 +207,7 @@
 
 
 def direction_kernel(
-    ids_ref, far_ref, gathered_ref, f_low, f_own, f_high, q_low, q_own, q_high,
+    ids_ref, far_ref, gathered_ref, f_partner, f_own, f_beyond, q_partner, q_own, q_beyond,
     local_ref, table_ref, shift_ref, down_ref, near_ref,
     out_ref, direction_out, image_out, alpha_out,
     blocks_ref, rounded_ref, ids_smem, far_smem, sems,
@@ -239,7 +239,7 @@
 
     coeffs = block_diagonal(-alpha_t)
     both = jnp.concatenate([block_diagonal(lift_t), coeffs], axis=1)
-    for i, (f, q) in enumerate(((f_low, q_low), (f_own, q_own), (f_high, q_high))):
+    for i, (f, q) in enumerate(((f_partner, q_partner), (f_own, q_own), (f_beyond, q_beyond))):
         pair = jnp.concatenate(
             [f[...].reshape(ROWS, W), q[...].reshape(ROWS, W)], axis=0
         )
@@ -321,11 +321,11 @@
 
 def halo(block, axis):
     count = lax.axis_size(axis)
-    forward = [(i, (i + 1) % count) for i in range(count)]
-    backward = [(target, source) for source, target in forward]
-    low = lax.ppermute(block, axis, forward)
-    high = lax.ppermute(block, axis, backward)
-    return low, high
+    partner = lax.ppermute(block, axis, [(i, i ^ 1) for i in range(count)])
+    beyond = lax.ppermute(
+        block, axis, [(i, (i + (1 if i % 2 else -1)) % count) for i in range(count)]
+    )
+    return partner, beyond
 
 
 def on_device(
@@ -342,8 +342,10 @@
     count = lax.axis_size("patch")
     depth = lax.axis_size("rhs")
     place = lax.axis_index("rhs").astype(jnp.int32)
-    first = lax.axis_index("patch") * PD - PD
-    ids = jnp.mod(neighbours - first, PD * count)
+    cell = lax.axis_index("patch")
+    owner = neighbours // PD
+    slot = jnp.where(owner == cell, 1, jnp.where(owner == cell ^ 1, 0, 2))
+    ids = (slot * PD + neighbours % PD).astype(jnp.int32)
 
     message = jnp.broadcast_to(rhs_vectors[None], (depth, *rhs_vectors.shape))
     parts = swap(message, "rhs")
@@ -360,7 +362,7 @@
     table = translations[0]
     down = down_maps.transpose(0, 2, 1)
 
-    f_low, f_high = halo(field, "patch")
+    f_partner, f_beyond = halo(field, "patch")
     message = call(moment_kernel, [VMEM] * 2, shape(count, K // 2, ROWS))(field, up)
     gathered = swap(message, "patch")
     near = call(
@@ -370,7 +372,7 @@
         (*NEAR_SCRATCH, pltpu.SemaphoreType.DMA((PD + 1,))),
         limit=48,
     )(
-        ids, f_low, field, f_high, near_blocks
+        ids, f_partner, field, f_beyond, near_blocks
     )
     image, local_exp, message = call(
         image_kernel,
@@ -378,7 +380,7 @@
         (shape(PD, K, W), shape(K, 2 * E), shape(count, K, ROWS)),
     )(pick_cell, gathered, near, field, up, table, shift_down, down)
 
-    q_low, q_high = halo(image, "patch")
+    q_partner, q_beyond = halo(image, "patch")
     gathered = swap(message, "patch")
     message, direction, image1, alpha = call(
         direction_kernel,
@@ -387,7 +389,7 @@
         (*NEAR_SCRATCH, pltpu.SMEM((1, FL), jnp.int32), pltpu.SemaphoreType.DMA((PD + 2,))),
         limit=48,
     )(
-        ids, far_lists, gathered, f_low, field, f_high, q_low, image, q_high,
+        ids, far_lists, gathered, f_partner, field, f_beyond, q_partner, image, q_beyond,
         local_exp, table, shift_down, down, near_blocks,
     )
 

time: 84.8 us -> 81.7 us (0.963)
  waiting for transfers between devices: 20.2 us -> 16.7 us
    ppermute x4, starting transfers between devices: 5.52 us -> 10.7 us  [the longest x2 5.34 us: halo(): lax.ppermute(block, axis, [(i, (i + (1 if i % 2 else -1)) % count) for i...]
    all_to_all x4, starting transfers between devices: 31.5 us -> 26.7 us  [swap(): return lax.all_to_all(array, axis, 0, 0, tiled=True)]
    ppermute x4, waiting for transfers between devices: 5.79 us -> 2.37 us  [the longest x2 2.36 us: halo(): lax.ppermute(block, axis, [(i, (i + (1 if i % 2 else -1)) % count) for i...]
  transfers between devices with their start and end apart: 8 -> 8, of which waited for: 5 -> 5; matrix products, arithmetic and copies ran while one was open for 2% -> 2% of each run, Pallas kernels for 10% -> 11%
where the time goes in v8:
time: 81.7 us; the launch traced here: 81.1 us
  starting transfers between devices  37.3 us (46%)
  Pallas kernels  20.9 us (26%)
  waiting for transfers between devices  16.7 us (20%)
  local copies, waits for them, and re-layouts  4.62 us (6%)
  other arithmetic  0.82 us (1%)
    all_to_all x4, starting transfers between devices, swap(): return lax.all_to_all(array, axis, 0, 0, tiled=True)  26.7 us
    all_to_all x4, waiting for transfers between devices, swap(): return lax.all_to_all(array, axis, 0, 0, tiled=True)  14.4 us
    pallas_call x1, Pallas kernels, on_device(): call(direction_kernel, [VMEM] * 13 + [HBM], (shape(count, K // 2, ROWS),...  7.68 us
    pallas_call x1, Pallas kernels, on_device(): call(near_kernel, [VMEM] * 4 + [HBM], shape(ROWS, W), (*NEAR_SCRATCH, plt...  6.44 us
    ppermute x2, starting transfers between devices, halo(): lax.ppermute(block, axis, [(i, (i + (1 if i % 2 else -1)) % count) for i...  5.34 us
    ppermute x2, starting transfers between devices, halo(): partner = lax.ppermute(block, axis, [(i, i ^ 1) for i in range(count)])  5.32 us
    unnamed x13, local copies, waits for them, and re-layouts  2.86 us
    ppermute x2, waiting for transfers between devices, halo(): lax.ppermute(block, axis, [(i, (i + (1 if i % 2 else -1)) % count) for i...  2.36 us
  transfers between devices with their start and end apart: 8, of which 5 were waited for; matrix products, arithmetic and copies ran while one was open for 2% of the time, Pallas kernels for 11%

profile of v8, /device:TPU:1, one launch (start us, length us, event | category | flops | bytes accessed | tf_op | source)
XLA Modules:
  0.0 81.1 jit_solution(2986026590880203078)
XLA Ops:
  0.6 0.0 copy-start.1
  0.6 0.0 copy-start
  0.6 1.5 %broadcast_in_dim.14 = f32[8,8,2,384]{3,2,1,0:T(2,128)} broadcast(f32[8,2,384]{2,1,0:T(2,128)} %param.9), dimensions={1,2,3} | broadcast | bytes 221184 | tf_op jit(solution)/shard_map/broadcast_in_dim | solution.py:350
  2.2 9.0 %all-to-all-start = ((f32[8,8,2,384]{3,2,1,0:T(2,128)}), f32[8,8,2,384]{3,2,1,0:T(2,128)S(1)}, u32[]{:S(2)}, u32[]{:S(2)}) async-start(f32[8,8,2,384]{3,2,1,0:T(2,128)} %broadcast_in_dim.14), calls=%async_computation | async-start | bytes 393216 | tf_op jit(solution)/shard_map/all_to_all | solution.py:319
  11.2 0.7 fusion.3
  11.9 0.1 reshape.47
  12.0 0.8 copy.15
  12.8 0.1 fusion.pick_ref
  12.8 0.0 copy-start.2
  12.8 1.1 %copy-done.2 = f32[8,64,384]{2,1,0:T(8,128)S(1)} copy-done((f32[8,64,384]{2,1,0:T(8,128)S(1)}, f32[8,64,384]{2,1,0:T(8,128)}, u32[]{:S(2)}) %copy-start.2) | copy-done | bytes 786456
  14.0 0.0 copy-start.4
  14.0 0.9 %copy-done.4 = f32[8,64,64]{2,1,0:T(8,128)S(1)} copy-done((f32[8,64,64]{2,1,0:T(8,128)S(1)}, f32[8,64,64]{2,1,0:T(8,128)}, u32[]{:S(2)}) %copy-start.4) | copy-done | bytes 131096
  14.9 0.0 copy-start.3
  14.9 0.0 copy-start.5
  14.9 0.4 shard_map.104
  15.4 4.8 %all-to-all-done = f32[8,8,2,384]{3,2,1,0:T(2,128)S(1)} async-done(((f32[8,8,2,384]{3,2,1,0:T(2,128)}), f32[8,8,2,384]{3,2,1,0:T(2,128)S(1)}, u32[]{:S(2)}, u32[]{:S(2)}) %all-to-all-start) | async-done | bytes 196640 | tf_op jit(solution)/shard_map/all_to_all | solution.py:319
  20.2 0.1 copy.21
  20.3 3.6 %collective-permute-start.1 = (f32[8,16,384]{2,1,0:T(8,128)S(1)}, f32[8,16,384]{2,1,0:T(8,128)S(1)}, u32[]{:S(2)}, u32[]{:S(2)}) collective-permute-start(f32[8,16,384]{2,1,0:T(8,128)S(1)} %bitcast.7), channel_id=1, source_target_pairs={{0,248},{8,16},{16,8},{24,32},{32,24},{40,48},{48,40},{56,64},{64,... | collective-permute-start | bytes 589832 | tf_op jit(solution)/shard_map/ppermute | solution.py:325
  23.9 1.8 %collective-permute-start = (f32[8,16,384]{2,1,0:T(8,128)S(1)}, f32[8,16,384]{2,1,0:T(8,128)S(1)}, u32[]{:S(2)}, u32[]{:S(2)}) collective-permute-start(f32[8,16,384]{2,1,0:T(8,128)S(1)} %bitcast.8), channel_id=1, source_target_pairs={{0,8},{8,0},{16,24},{24,16},{32,40},{40,32},{48,56},{56,48},{64,72... | collective-permute-start | bytes 589832 | tf_op jit(solution)/shard_map/ppermute | solution.py:324
  25.7 1.1 %shard_map.105 = f32[32,8,128]{2,1,0:T(8,128)} custom-call(f32[8,16,384]{2,1,0:T(8,128)S(1)} %bitcast.9, f32[64,3072]{1,0:T(8,128)S(1)} %get-tuple-element.14.up_ref), custom_call_target="tpu_custom_call" | custom-call | flops 1000000 | bytes 1000000 | tf_op jit(solution)/shard_map/pallas_call | solution.py:366
  26.8 5.5 %all-to-all-start.1 = ((f32[32,8,128]{2,1,0:T(8,128)}), f32[32,8,128]{2,1,0:T(8,128)S(1)}, u32[]{:S(2)}, u32[]{:S(2)}) async-start(f32[32,8,128]{2,1,0:T(8,128)} %shard_map.105), calls=%async_computation.1 | async-start | bytes 262144 | tf_op jit(solution)/shard_map/all_to_all | solution.py:319
  32.3 0.0 collective-permute-done.1.beyond_ref.f_beyond
  32.4 0.0 collective-permute-done.partner_ref.f_partner
  32.4 6.4 %shard_map.106.near_ref = f32[128,384]{1,0:T(8,128)S(1)} custom-call(s32[8,4]{1,0:T(8,128)S(1)} %fusion.1.ids_ref, f32[8,16,384]{2,1,0:T(8,128)S(1)} %collective-permute-done.partner_ref.f_partner, f32[8,16,384]{2,1,0:T(8,128)S(1)} %bitcast.10, f32[8,16,384]{2,1,0:T(8,128)S(1)} %collective-permute-done.1.beyond_ref.f_beyond, bf16[8,4,384,384]{3,2,1,0:T(8,128)(2,1)} %near_ref.3), custom_call_target="tpu_custom_call" | custom-call | flops 1000000 | bytes 1000000 | tf_op jit(solution)/shard_map/pallas_call | solution.py:368
  38.8 1.1 %all-to-all-done.1.gathered_ref = f32[32,8,128]{2,1,0:T(8,128)S(1)} async-done(((f32[32,8,128]{2,1,0:T(8,128)}), f32[32,8,128]{2,1,0:T(8,128)S(1)}, u32[]{:S(2)}, u32[]{:S(2)}) %all-to-all-start.1) | async-done | bytes 131104 | tf_op jit(solution)/shard_map/all_to_all | solution.py:319
  39.9 0.1 broadcast_in_dim.13.pick_ref
  40.0 0.0 copy-done.1
  40.0 0.0 copy-done
  40.0 0.0 copy-done.3
  40.0 2.3 %shard_map.107 = (f32[8,16,384]{2,1,0:T(8,128)S(1)}, f32[16,128]{1,0:T(8,128)S(1)}, f32[32,16,128]{2,1,0:T(8,128)}) custom-call(f32[128,128]{1,0:T(8,128)S(1)} %broadcast_in_dim.13.pick_ref, f32[32,8,128]{2,1,0:T(8,128)S(1)} %all-to-all-done.1.gathered_ref, f32[128,384]{1,0:T(8,128)S(1)} %shard_map.106.near_ref, f32[8,16,384]{2,1,0:T(8,128)S(1)} %bitcast.11, ...), custom_call_target="tpu_custom_call" | custom-call | flops 1000000 | bytes 1000000 | tf_op jit(solution)/shard_map/pallas_call | solution.py:377
  42.4 6.3 %all-to-all-start.2 = ((f32[32,16,128]{2,1,0:T(8,128)}), f32[32,16,128]{2,1,0:T(8,128)S(1)}, u32[]{:S(2)}, u32[]{:S(2)}) async-start(f32[32,16,128]{2,1,0:T(8,128)} %get-tuple-element.15), calls=%async_computation.2 | async-start | bytes 524288 | tf_op jit(solution)/shard_map/all_to_all | solution.py:319
  48.7 1.7 %collective-permute-start.3 = (f32[8,16,384]{2,1,0:T(8,128)S(1)}, f32[8,16,384]{2,1,0:T(8,128)S(1)}, u32[]{:S(2)}, u32[]{:S(2)}) collective-permute-start(f32[8,16,384]{2,1,0:T(8,128)S(1)} %get-tuple-element.16.q_own.image_ref), channel_id=1, source_target_pairs={{0,248},{8,16},{16,8},{24,32},{32,24},{40,48},{48,40},{56,64},{64,... | collective-permute-start | bytes 589832 | tf_op jit(solution)/shard_map/ppermute | solution.py:325
  50.4 3.5 %collective-permute-start.2 = (f32[8,16,384]{2,1,0:T(8,128)S(1)}, f32[8,16,384]{2,1,0:T(8,128)S(1)}, u32[]{:S(2)}, u32[]{:S(2)}) collective-permute-start(f32[8,16,384]{2,1,0:T(8,128)S(1)} %get-tuple-element.16.q_own.image_ref), channel_id=1, source_target_pairs={{0,8},{8,0},{16,24},{24,16},{32,40},{40,32},{48,56},{56,48},{64,72... | collective-permute-start | bytes 589832 | tf_op jit(solution)/shard_map/ppermute | solution.py:324
  53.9 2.4 %collective-permute-done.3.q_beyond = f32[8,16,384]{2,1,0:T(8,128)S(1)} collective-permute-done((f32[8,16,384]{2,1,0:T(8,128)S(1)}, f32[8,16,384]{2,1,0:T(8,128)S(1)}, u32[]{:S(2)}, u32[]{:S(2)}) %collective-permute-start.3) | collective-permute-done | bytes 196640 | tf_op jit(solution)/shard_map/ppermute | solution.py:325
  56.3 0.0 collective-permute-done.2.q_partner
  56.3 1.6 %all-to-all-done.2.gathered_ref = f32[32,16,128]{2,1,0:T(8,128)S(1)} async-done(((f32[32,16,128]{2,1,0:T(8,128)}), f32[32,16,128]{2,1,0:T(8,128)S(1)}, u32[]{:S(2)}, u32[]{:S(2)}) %all-to-all-start.2) | async-done | bytes 262176 | tf_op jit(solution)/shard_map/all_to_all | solution.py:319
  57.9 0.0 copy-done.5
  57.9 7.7 %shard_map.108 = (f32[32,8,128]{2,1,0:T(8,128)}, f32[128,384]{1,0:T(8,128)S(1)}, f32[128,384]{1,0:T(8,128)S(1)}, f32[16,128]{1,0:T(8,128)S(1)}) custom-call(s32[8,4]{1,0:T(8,128)S(1)} %fusion.1.ids_ref, s32[1,4]{1,0:T(1,128)S(1)} %copy-done.5, f32[32,16,128]{2,1,0:T(8,128)S(1)} %all-to-all-done.2.gathered_ref, ...), custom_call_target="tpu_custom_call" | custom-call | flops 1000000 | bytes 1000000 | tf_op jit(solution)/shard_map/pallas_call | solution.py:385
  65.6 5.9 %all-to-all-start.3 = ((f32[32,8,128]{2,1,0:T(8,128)}), f32[32,8,128]{2,1,0:T(8,128)S(1)}, u32[]{:S(2)}, u32[]{:S(2)}) async-start(f32[32,8,128]{2,1,0:T(8,128)} %get-tuple-element.18), calls=%async_computation.3 | async-start | bytes 262144 | tf_op jit(solution)/shard_map/all_to_all | solution.py:319
  71.5 0.8 shard_map.109
  72.3 6.8 %all-to-all-done.3.gathered_ref = f32[32,8,128]{2,1,0:T(8,128)S(1)} async-done(((f32[32,8,128]{2,1,0:T(8,128)}), f32[32,8,128]{2,1,0:T(8,128)S(1)}, u32[]{:S(2)}, u32[]{:S(2)}) %all-to-all-start.3) | async-done | bytes 131104 | tf_op jit(solution)/shard_map/all_to_all | solution.py:319
  79.1 2.0 %shard_map.110 = (f32[8,2,384]{2,1,0:T(2,128)}, f32[8,2,384]{2,1,0:T(2,128)}) custom-call(f32[16,16]{1,0:T(8,128)S(1)} %get-tuple-element.13.pick_ref, f32[32,8,128]{2,1,0:T(8,128)S(1)} %all-to-all-done.3.gathered_ref, f32[128,384]{1,0:T(8,128)S(1)} %get-tuple-element.19.direction_ref, f32[128,384]{1,0:T(8,128)S(1)} %get-tuple-element.20.image_ref, ...), custom_call_target="tpu_custom_call" | custom-call | flops 1000000 | bytes 1000000 | tf_op jit(solution)/shard_map/pallas_call | solution.py:400
  (2 shorter events, 0.0 us)
Async XLA Ops:
  0.6 39.4 %copy-start.1 = (f32[8,64,64]{2,1,0:T(8,128)S(1)}, f32[8,64,64]{2,1,0:T(8,128)}, u32[]{:S(2)}) copy-start(f32[8,64,64]{2,1,0:T(8,128)} %shift_ref.5) | copy-start | bytes 393220
  0.6 39.4 %copy-start = (f32[8,384,64]{1,2,0:T(8,128)S(1)}, f32[8,384,64]{1,2,0:T(8,128)}, u32[]{:S(2)}) copy-start(f32[8,384,64]{1,2,0:T(8,128)} %param.17) | copy-start | bytes 2359300
  2.2 18.0 %all-to-all-start = ((f32[8,8,2,384]{3,2,1,0:T(2,128)}), f32[8,8,2,384]{3,2,1,0:T(2,128)S(1)}, u32[]{:S(2)}, u32[]{:S(2)}) async-start(f32[8,8,2,384]{3,2,1,0:T(2,128)} %broadcast_in_dim.14), calls=%async_computation | async-start | bytes 393216 | tf_op jit(solution)/shard_map/all_to_all | solution.py:319
  12.8 1.1 %copy-start.2 = (f32[8,64,384]{2,1,0:T(8,128)S(1)}, f32[8,64,384]{2,1,0:T(8,128)}, u32[]{:S(2)}) copy-start(f32[8,64,384]{2,1,0:T(8,128)} %up_ref.1) | copy-start | bytes 2359300
  14.0 0.9 %copy-start.4 = (f32[8,64,64]{2,1,0:T(8,128)S(1)}, f32[8,64,64]{2,1,0:T(8,128)}, u32[]{:S(2)}) copy-start(f32[8,64,64]{2,1,0:T(8,128)} %shift_ref.3) | copy-start | bytes 393220
  14.9 25.1 %copy-start.3 = (f32[1,4,64,64]{3,2,1,0:T(8,128)S(1)}, f32[1,4,64,64]{3,2,1,0:T(8,128)}, u32[]{:S(2)}) copy-start(f32[1,4,64,64]{3,2,1,0:T(8,128)} %param.15) | copy-start | bytes 196612
  14.9 43.0 %copy-start.5 = (s32[1,4]{1,0:T(1,128)S(1)}, s32[1,4]{1,0:T(1,128)}, u32[]{:S(2)}) copy-start(s32[1,4]{1,0:T(1,128)} %far_ref.1) | copy-start | bytes 52
  20.3 12.1 %collective-permute-start.1 = (f32[8,16,384]{2,1,0:T(8,128)S(1)}, f32[8,16,384]{2,1,0:T(8,128)S(1)}, u32[]{:S(2)}, u32[]{:S(2)}) collective-permute-start(f32[8,16,384]{2,1,0:T(8,128)S(1)} %bitcast.7), channel_id=1, source_target_pairs={{0,248},{8,16},{16,8},{24,32},{32,24},{40,48},{48,40},{56,64},{64,... | collective-permute-start | bytes 589832 | tf_op jit(solution)/shard_map/ppermute | solution.py:325
  23.9 8.5 %collective-permute-start = (f32[8,16,384]{2,1,0:T(8,128)S(1)}, f32[8,16,384]{2,1,0:T(8,128)S(1)}, u32[]{:S(2)}, u32[]{:S(2)}) collective-permute-start(f32[8,16,384]{2,1,0:T(8,128)S(1)} %bitcast.8), channel_id=1, source_target_pairs={{0,8},{8,0},{16,24},{24,16},{32,40},{40,32},{48,56},{56,48},{64,72... | collective-permute-start | bytes 589832 | tf_op jit(solution)/shard_map/ppermute | solution.py:324
  26.8 13.1 %all-to-all-start.1 = ((f32[32,8,128]{2,1,0:T(8,128)}), f32[32,8,128]{2,1,0:T(8,128)S(1)}, u32[]{:S(2)}, u32[]{:S(2)}) async-start(f32[32,8,128]{2,1,0:T(8,128)} %shard_map.105), calls=%async_computation.1 | async-start | bytes 262144 | tf_op jit(solution)/shard_map/all_to_all | solution.py:319
  42.4 15.5 %all-to-all-start.2 = ((f32[32,16,128]{2,1,0:T(8,128)}), f32[32,16,128]{2,1,0:T(8,128)S(1)}, u32[]{:S(2)}, u32[]{:S(2)}) async-start(f32[32,16,128]{2,1,0:T(8,128)} %get-tuple-element.15), calls=%async_computation.2 | async-start | bytes 524288 | tf_op jit(solution)/shard_map/all_to_all | solution.py:319
  48.7 7.6 %collective-permute-start.3 = (f32[8,16,384]{2,1,0:T(8,128)S(1)}, f32[8,16,384]{2,1,0:T(8,128)S(1)}, u32[]{:S(2)}, u32[]{:S(2)}) collective-permute-start(f32[8,16,384]{2,1,0:T(8,128)S(1)} %get-tuple-element.16.q_own.image_ref), channel_id=1, source_target_pairs={{0,248},{8,16},{16,8},{24,32},{32,24},{40,48},{48,40},{56,64},{64,... | collective-permute-start | bytes 589832 | tf_op jit(solution)/shard_map/ppermute | solution.py:325
  50.4 5.9 %collective-permute-start.2 = (f32[8,16,384]{2,1,0:T(8,128)S(1)}, f32[8,16,384]{2,1,0:T(8,128)S(1)}, u32[]{:S(2)}, u32[]{:S(2)}) collective-permute-start(f32[8,16,384]{2,1,0:T(8,128)S(1)} %get-tuple-element.16.q_own.image_ref), channel_id=1, source_target_pairs={{0,8},{8,0},{16,24},{24,16},{32,40},{40,32},{48,56},{56,48},{64,72... | collective-permute-start | bytes 589832 | tf_op jit(solution)/shard_map/ppermute | solution.py:324
  65.6 13.5 %all-to-all-start.3 = ((f32[32,8,128]{2,1,0:T(8,128)}), f32[32,8,128]{2,1,0:T(8,128)S(1)}, u32[]{:S(2)}, u32[]{:S(2)}) async-start(f32[32,8,128]{2,1,0:T(8,128)} %get-tuple-element.18), calls=%async_computation.3 | async-start | bytes 262144 | tf_op jit(solution)/shard_map/all_to_all | solution.py:319

commit v9 on v8

--- a/solution.py
+++ b/solution.py
@@ -255,39 +255,37 @@
     image = image.T + far
     image_out[...] = image
     residual = side_by_side(residual)
-    grams = nt(
-        jnp.concatenate([side_by_side(image), residual], axis=0),
-        jnp.concatenate([side_by_side(direction), residual], axis=0),
-    )
-    message = jnp.concatenate([grams[:K, :K], grams[K:, K:]], axis=1)
+    image = side_by_side(image)
+    direction = side_by_side(direction)
+    both = jnp.concatenate([image, residual], axis=0)
+    grams = nt(both, jnp.concatenate([direction, residual], axis=0))
+    message = jnp.concatenate([grams[:K, :K], nt(direction, image), grams[K:, K:]], axis=1)
     message = jnp.concatenate(
-        [message[: K // 2], message[K // 2 :], jnp.zeros((K // 2, ROWS - 4 * K), F32)], axis=1
+        [message[: K // 2], message[K // 2 :], jnp.zeros((K // 2, ROWS - 6 * K), F32)], axis=1
     )
     for i in range(out_ref.shape[0]):
         out_ref[i] = message
 
 
-def own_coeffs(pick, coeffs_t):
+def own_coeffs(rows):
     row, lane = iotas(K, ROWS)
-    return jnp.where(row // 2 == lane // K, tiled(small(pick, coeffs_t)), 0.0)
+    return jnp.where(row // 2 == lane // K, tiled(rows), 0.0)
 
 
 def first_step_kernel(pick_ref, alpha_ref, field_ref, image_ref, x_out, r_out):
     pick = pick_ref[...]
     field = field_ref[...].reshape(ROWS, W)
-    row, lane = iotas(K, ROWS)
-    mine = jnp.where(row // 2 == lane // K, tiled(pick), 0.0)
-    coeffs = own_coeffs(pick, alpha_ref[:, :K])
+    mine = own_coeffs(pick)
+    coeffs = own_coeffs(small(pick, alpha_ref[:, :K]))
     x_out[...] = exact(coeffs, field)
     r_out[...] = exact(mine, field) - exact(coeffs, image_ref[...].reshape(ROWS, W))
 
 
 def last_step_kernel(pick_ref, gathered_ref, direction_ref, image_ref, x_ref, r_ref, x_out, r_out):
     total = total_of(gathered_ref)
-    total = jnp.concatenate([total[:, : 2 * K], total[:, 2 * K : 4 * K]], axis=0)
-    qd = total[:, :K]
-    alpha_t = small(total[:, K : 2 * K], inverse(0.5 * (qd + qd.T)))
-    coeffs = own_coeffs(pick_ref[...], alpha_t)
+    total = jnp.concatenate([total[:, : 3 * K], total[:, 3 * K : 6 * K]], axis=0)
+    mine = small(pick_ref[...], total[:, 2 * K :])
+    coeffs = own_coeffs(small(mine, inverse(0.5 * (total[:, :K] + total[:, K : 2 * K]))))
     x = x_ref[...] + nn(coeffs, direction_ref[...])
     r = r_ref[...] - nn(coeffs, image_ref[...])
     for p in range(PD):

time: 81.7 us -> 82 us (level)
  no operation moved by 1% of the time
where the time goes in v9:
time: 82 us; the launch traced here: 81.5 us
  starting transfers between devices  37.3 us (45%)
  Pallas kernels  21.2 us (26%)
  waiting for transfers between devices  16.7 us (20%)
  local copies, waits for them, and re-layouts  4.62 us (6%)
    all_to_all x4, starting transfers between devices, swap(): return lax.all_to_all(array, axis, 0, 0, tiled=True)  26.7 us
    all_to_all x4, waiting for transfers between devices, swap(): return lax.all_to_all(array, axis, 0, 0, tiled=True)  14.4 us
    pallas_call x1, Pallas kernels, on_device(): call(direction_kernel, [VMEM] * 13 + [HBM], (shape(count, K // 2, ROWS),...  8.12 us
    pallas_call x1, Pallas kernels, on_device(): call(near_kernel, [VMEM] * 4 + [HBM], shape(ROWS, W), (*NEAR_SCRATCH, plt...  6.44 us
    ppermute x2, starting transfers between devices, halo(): lax.ppermute(block, axis, [(i, (i + (1 if i % 2 else -1)) % count) for i...  5.34 us
    ppermute x2, starting transfers between devices, halo(): partner = lax.ppermute(block, axis, [(i, i ^ 1) for i in range(count)])  5.32 us
    unnamed x13, local copies, waits for them, and re-layouts  2.86 us
    ppermute x2, waiting for transfers between devices, halo(): lax.ppermute(block, axis, [(i, (i + (1 if i % 2 else -1)) % count) for i...  2.36 us
  transfers between devices with their start and end apart: 8, of which 5 were waited for; matrix products, arithmetic and copies ran while one was open for 2% of the time, Pallas kernels for 11%

profile of v9, /device:TPU:1, one launch (start us, length us, event | category | flops | bytes accessed | tf_op | source)
XLA Modules:
  0.0 81.5 jit_solution(2473665449421588831)
XLA Ops:
  0.6 0.0 copy-start.1
  0.6 0.0 copy-start
  0.6 1.5 %broadcast_in_dim.14 = f32[8,8,2,384]{3,2,1,0:T(2,128)} broadcast(f32[8,2,384]{2,1,0:T(2,128)} %param.9), dimensions={1,2,3} | broadcast | bytes 221184 | tf_op jit(solution)/shard_map/broadcast_in_dim | solution.py:348
  2.2 9.0 %all-to-all-start = ((f32[8,8,2,384]{3,2,1,0:T(2,128)}), f32[8,8,2,384]{3,2,1,0:T(2,128)S(1)}, u32[]{:S(2)}, u32[]{:S(2)}) async-start(f32[8,8,2,384]{3,2,1,0:T(2,128)} %broadcast_in_dim.14), calls=%async_computation | async-start | bytes 393216 | tf_op jit(solution)/shard_map/all_to_all | solution.py:317
  11.2 0.7 fusion.3
  11.9 0.1 reshape.47
  12.0 0.8 copy.15
  12.8 0.1 fusion.pick_ref
  12.8 0.0 copy-start.2
  12.8 1.1 %copy-done.2 = f32[8,64,384]{2,1,0:T(8,128)S(1)} copy-done((f32[8,64,384]{2,1,0:T(8,128)S(1)}, f32[8,64,384]{2,1,0:T(8,128)}, u32[]{:S(2)}) %copy-start.2) | copy-done | bytes 786456
  14.0 0.0 copy-start.4
  14.0 0.9 %copy-done.4 = f32[8,64,64]{2,1,0:T(8,128)S(1)} copy-done((f32[8,64,64]{2,1,0:T(8,128)S(1)}, f32[8,64,64]{2,1,0:T(8,128)}, u32[]{:S(2)}) %copy-start.4) | copy-done | bytes 131096
  14.9 0.0 copy-start.3
  14.9 0.0 copy-start.5
  14.9 0.4 shard_map.104
  15.4 4.8 %all-to-all-done = f32[8,8,2,384]{3,2,1,0:T(2,128)S(1)} async-done(((f32[8,8,2,384]{3,2,1,0:T(2,128)}), f32[8,8,2,384]{3,2,1,0:T(2,128)S(1)}, u32[]{:S(2)}, u32[]{:S(2)}) %all-to-all-start) | async-done | bytes 196640 | tf_op jit(solution)/shard_map/all_to_all | solution.py:317
  20.2 0.1 copy.21
  20.3 3.6 %collective-permute-start.1 = (f32[8,16,384]{2,1,0:T(8,128)S(1)}, f32[8,16,384]{2,1,0:T(8,128)S(1)}, u32[]{:S(2)}, u32[]{:S(2)}) collective-permute-start(f32[8,16,384]{2,1,0:T(8,128)S(1)} %bitcast.7), channel_id=1, source_target_pairs={{0,248},{8,16},{16,8},{24,32},{32,24},{40,48},{48,40},{56,64},{64,... | collective-permute-start | bytes 589832 | tf_op jit(solution)/shard_map/ppermute | solution.py:323
  23.9 1.8 %collective-permute-start = (f32[8,16,384]{2,1,0:T(8,128)S(1)}, f32[8,16,384]{2,1,0:T(8,128)S(1)}, u32[]{:S(2)}, u32[]{:S(2)}) collective-permute-start(f32[8,16,384]{2,1,0:T(8,128)S(1)} %bitcast.8), channel_id=1, source_target_pairs={{0,8},{8,0},{16,24},{24,16},{32,40},{40,32},{48,56},{56,48},{64,72... | collective-permute-start | bytes 589832 | tf_op jit(solution)/shard_map/ppermute | solution.py:322
  25.7 1.1 %shard_map.105 = f32[32,8,128]{2,1,0:T(8,128)} custom-call(f32[8,16,384]{2,1,0:T(8,128)S(1)} %bitcast.9, f32[64,3072]{1,0:T(8,128)S(1)} %get-tuple-element.14.up_ref), custom_call_target="tpu_custom_call" | custom-call | flops 1000000 | bytes 1000000 | tf_op jit(solution)/shard_map/pallas_call | solution.py:364
  26.8 5.5 %all-to-all-start.1 = ((f32[32,8,128]{2,1,0:T(8,128)}), f32[32,8,128]{2,1,0:T(8,128)S(1)}, u32[]{:S(2)}, u32[]{:S(2)}) async-start(f32[32,8,128]{2,1,0:T(8,128)} %shard_map.105), calls=%async_computation.1 | async-start | bytes 262144 | tf_op jit(solution)/shard_map/all_to_all | solution.py:317
  32.3 0.0 collective-permute-done.1.beyond_ref.f_beyond
  32.4 0.0 collective-permute-done.partner_ref.f_partner
  32.4 6.4 %shard_map.106.near_ref = f32[128,384]{1,0:T(8,128)S(1)} custom-call(s32[8,4]{1,0:T(8,128)S(1)} %fusion.1.ids_ref, f32[8,16,384]{2,1,0:T(8,128)S(1)} %collective-permute-done.partner_ref.f_partner, f32[8,16,384]{2,1,0:T(8,128)S(1)} %bitcast.10, f32[8,16,384]{2,1,0:T(8,128)S(1)} %collective-permute-done.1.beyond_ref.f_beyond, bf16[8,4,384,384]{3,2,1,0:T(8,128)(2,1)} %near_ref.3), custom_call_target="tpu_custom_call" | custom-call | flops 1000000 | bytes 1000000 | tf_op jit(solution)/shard_map/pallas_call | solution.py:366
  38.8 1.1 %all-to-all-done.1.gathered_ref = f32[32,8,128]{2,1,0:T(8,128)S(1)} async-done(((f32[32,8,128]{2,1,0:T(8,128)}), f32[32,8,128]{2,1,0:T(8,128)S(1)}, u32[]{:S(2)}, u32[]{:S(2)}) %all-to-all-start.1) | async-done | bytes 131104 | tf_op jit(solution)/shard_map/all_to_all | solution.py:317
  39.9 0.1 broadcast_in_dim.13.pick_ref
  40.0 0.0 copy-done.1
  40.0 0.0 copy-done
  40.0 0.0 copy-done.3
  40.0 2.3 %shard_map.107 = (f32[8,16,384]{2,1,0:T(8,128)S(1)}, f32[16,128]{1,0:T(8,128)S(1)}, f32[32,16,128]{2,1,0:T(8,128)}) custom-call(f32[128,128]{1,0:T(8,128)S(1)} %broadcast_in_dim.13.pick_ref, f32[32,8,128]{2,1,0:T(8,128)S(1)} %all-to-all-done.1.gathered_ref, f32[128,384]{1,0:T(8,128)S(1)} %shard_map.106.near_ref, f32[8,16,384]{2,1,0:T(8,128)S(1)} %bitcast.11, ...), custom_call_target="tpu_custom_call" | custom-call | flops 1000000 | bytes 1000000 | tf_op jit(solution)/shard_map/pallas_call | solution.py:375
  42.4 6.3 %all-to-all-start.2 = ((f32[32,16,128]{2,1,0:T(8,128)}), f32[32,16,128]{2,1,0:T(8,128)S(1)}, u32[]{:S(2)}, u32[]{:S(2)}) async-start(f32[32,16,128]{2,1,0:T(8,128)} %get-tuple-element.15), calls=%async_computation.2 | async-start | bytes 524288 | tf_op jit(solution)/shard_map/all_to_all | solution.py:317
  48.7 1.7 %collective-permute-start.3 = (f32[8,16,384]{2,1,0:T(8,128)S(1)}, f32[8,16,384]{2,1,0:T(8,128)S(1)}, u32[]{:S(2)}, u32[]{:S(2)}) collective-permute-start(f32[8,16,384]{2,1,0:T(8,128)S(1)} %get-tuple-element.16.q_own.image_ref), channel_id=1, source_target_pairs={{0,248},{8,16},{16,8},{24,32},{32,24},{40,48},{48,40},{56,64},{64,... | collective-permute-start | bytes 589832 | tf_op jit(solution)/shard_map/ppermute | solution.py:323
  50.4 3.5 %collective-permute-start.2 = (f32[8,16,384]{2,1,0:T(8,128)S(1)}, f32[8,16,384]{2,1,0:T(8,128)S(1)}, u32[]{:S(2)}, u32[]{:S(2)}) collective-permute-start(f32[8,16,384]{2,1,0:T(8,128)S(1)} %get-tuple-element.16.q_own.image_ref), channel_id=1, source_target_pairs={{0,8},{8,0},{16,24},{24,16},{32,40},{40,32},{48,56},{56,48},{64,72... | collective-permute-start | bytes 589832 | tf_op jit(solution)/shard_map/ppermute | solution.py:322
  53.9 2.4 %collective-permute-done.3.q_beyond = f32[8,16,384]{2,1,0:T(8,128)S(1)} collective-permute-done((f32[8,16,384]{2,1,0:T(8,128)S(1)}, f32[8,16,384]{2,1,0:T(8,128)S(1)}, u32[]{:S(2)}, u32[]{:S(2)}) %collective-permute-start.3) | collective-permute-done | bytes 196640 | tf_op jit(solution)/shard_map/ppermute | solution.py:323
  56.3 0.0 collective-permute-done.2.q_partner
  56.3 1.6 %all-to-all-done.2.gathered_ref = f32[32,16,128]{2,1,0:T(8,128)S(1)} async-done(((f32[32,16,128]{2,1,0:T(8,128)}), f32[32,16,128]{2,1,0:T(8,128)S(1)}, u32[]{:S(2)}, u32[]{:S(2)}) %all-to-all-start.2) | async-done | bytes 262176 | tf_op jit(solution)/shard_map/all_to_all | solution.py:317
  57.9 0.0 copy-done.5
  57.9 8.1 %shard_map.108 = (f32[32,8,128]{2,1,0:T(8,128)}, f32[128,384]{1,0:T(8,128)S(1)}, f32[128,384]{1,0:T(8,128)S(1)}, f32[16,128]{1,0:T(8,128)S(1)}) custom-call(s32[8,4]{1,0:T(8,128)S(1)} %fusion.1.ids_ref, s32[1,4]{1,0:T(1,128)S(1)} %copy-done.5, f32[32,16,128]{2,1,0:T(8,128)S(1)} %all-to-all-done.2.gathered_ref, ...), custom_call_target="tpu_custom_call" | custom-call | flops 1000000 | bytes 1000000 | tf_op jit(solution)/shard_map/pallas_call | solution.py:383
  66.0 5.9 %all-to-all-start.3 = ((f32[32,8,128]{2,1,0:T(8,128)}), f32[32,8,128]{2,1,0:T(8,128)S(1)}, u32[]{:S(2)}, u32[]{:S(2)}) async-start(f32[32,8,128]{2,1,0:T(8,128)} %get-tuple-element.18), calls=%async_computation.3 | async-start | bytes 262144 | tf_op jit(solution)/shard_map/all_to_all | solution.py:317
  71.9 0.8 shard_map.109
  72.7 6.8 %all-to-all-done.3.gathered_ref = f32[32,8,128]{2,1,0:T(8,128)S(1)} async-done(((f32[32,8,128]{2,1,0:T(8,128)}), f32[32,8,128]{2,1,0:T(8,128)S(1)}, u32[]{:S(2)}, u32[]{:S(2)}) %all-to-all-start.3) | async-done | bytes 131104 | tf_op jit(solution)/shard_map/all_to_all | solution.py:317
  79.5 2.0 %shard_map.110 = (f32[8,2,384]{2,1,0:T(2,128)}, f32[8,2,384]{2,1,0:T(2,128)}) custom-call(f32[16,16]{1,0:T(8,128)S(1)} %get-tuple-element.13.pick_ref, f32[32,8,128]{2,1,0:T(8,128)S(1)} %all-to-all-done.3.gathered_ref, f32[128,384]{1,0:T(8,128)S(1)} %get-tuple-element.19.direction_ref, f32[128,384]{1,0:T(8,128)S(1)} %get-tuple-element.20.image_ref, ...), custom_call_target="tpu_custom_call" | custom-call | flops 1000000 | bytes 1000000 | tf_op jit(solution)/shard_map/pallas_call | solution.py:398
  (2 shorter events, 0.0 us)
Async XLA Ops:
  0.6 39.4 %copy-start.1 = (f32[8,64,64]{2,1,0:T(8,128)S(1)}, f32[8,64,64]{2,1,0:T(8,128)}, u32[]{:S(2)}) copy-start(f32[8,64,64]{2,1,0:T(8,128)} %shift_ref.5) | copy-start | bytes 393220
  0.6 39.4 %copy-start = (f32[8,384,64]{1,2,0:T(8,128)S(1)}, f32[8,384,64]{1,2,0:T(8,128)}, u32[]{:S(2)}) copy-start(f32[8,384,64]{1,2,0:T(8,128)} %param.17) | copy-start | bytes 2359300
  2.2 18.0 %all-to-all-start = ((f32[8,8,2,384]{3,2,1,0:T(2,128)}), f32[8,8,2,384]{3,2,1,0:T(2,128)S(1)}, u32[]{:S(2)}, u32[]{:S(2)}) async-start(f32[8,8,2,384]{3,2,1,0:T(2,128)} %broadcast_in_dim.14), calls=%async_computation | async-start | bytes 393216 | tf_op jit(solution)/shard_map/all_to_all | solution.py:317
  12.8 1.1 %copy-start.2 = (f32[8,64,384]{2,1,0:T(8,128)S(1)}, f32[8,64,384]{2,1,0:T(8,128)}, u32[]{:S(2)}) copy-start(f32[8,64,384]{2,1,0:T(8,128)} %up_ref.1) | copy-start | bytes 2359300
  14.0 0.9 %copy-start.4 = (f32[8,64,64]{2,1,0:T(8,128)S(1)}, f32[8,64,64]{2,1,0:T(8,128)}, u32[]{:S(2)}) copy-start(f32[8,64,64]{2,1,0:T(8,128)} %shift_ref.3) | copy-start | bytes 393220
  14.9 25.1 %copy-start.3 = (f32[1,4,64,64]{3,2,1,0:T(8,128)S(1)}, f32[1,4,64,64]{3,2,1,0:T(8,128)}, u32[]{:S(2)}) copy-start(f32[1,4,64,64]{3,2,1,0:T(8,128)} %param.15) | copy-start | bytes 196612
  14.9 43.0 %copy-start.5 = (s32[1,4]{1,0:T(1,128)S(1)}, s32[1,4]{1,0:T(1,128)}, u32[]{:S(2)}) copy-start(s32[1,4]{1,0:T(1,128)} %far_ref.1) | copy-start | bytes 52
  20.3 12.1 %collective-permute-start.1 = (f32[8,16,384]{2,1,0:T(8,128)S(1)}, f32[8,16,384]{2,1,0:T(8,128)S(1)}, u32[]{:S(2)}, u32[]{:S(2)}) collective-permute-start(f32[8,16,384]{2,1,0:T(8,128)S(1)} %bitcast.7), channel_id=1, source_target_pairs={{0,248},{8,16},{16,8},{24,32},{32,24},{40,48},{48,40},{56,64},{64,... | collective-permute-start | bytes 589832 | tf_op jit(solution)/shard_map/ppermute | solution.py:323
  23.9 8.5 %collective-permute-start = (f32[8,16,384]{2,1,0:T(8,128)S(1)}, f32[8,16,384]{2,1,0:T(8,128)S(1)}, u32[]{:S(2)}, u32[]{:S(2)}) collective-permute-start(f32[8,16,384]{2,1,0:T(8,128)S(1)} %bitcast.8), channel_id=1, source_target_pairs={{0,8},{8,0},{16,24},{24,16},{32,40},{40,32},{48,56},{56,48},{64,72... | collective-permute-start | bytes 589832 | tf_op jit(solution)/shard_map/ppermute | solution.py:322
  26.8 13.1 %all-to-all-start.1 = ((f32[32,8,128]{2,1,0:T(8,128)}), f32[32,8,128]{2,1,0:T(8,128)S(1)}, u32[]{:S(2)}, u32[]{:S(2)}) async-start(f32[32,8,128]{2,1,0:T(8,128)} %shard_map.105), calls=%async_computation.1 | async-start | bytes 262144 | tf_op jit(solution)/shard_map/all_to_all | solution.py:317
  42.4 15.5 %all-to-all-start.2 = ((f32[32,16,128]{2,1,0:T(8,128)}), f32[32,16,128]{2,1,0:T(8,128)S(1)}, u32[]{:S(2)}, u32[]{:S(2)}) async-start(f32[32,16,128]{2,1,0:T(8,128)} %get-tuple-element.15), calls=%async_computation.2 | async-start | bytes 524288 | tf_op jit(solution)/shard_map/all_to_all | solution.py:317
  48.7 7.6 %collective-permute-start.3 = (f32[8,16,384]{2,1,0:T(8,128)S(1)}, f32[8,16,384]{2,1,0:T(8,128)S(1)}, u32[]{:S(2)}, u32[]{:S(2)}) collective-permute-start(f32[8,16,384]{2,1,0:T(8,128)S(1)} %get-tuple-element.16.q_own.image_ref), channel_id=1, source_target_pairs={{0,248},{8,16},{16,8},{24,32},{32,24},{40,48},{48,40},{56,64},{64,... | collective-permute-start | bytes 589832 | tf_op jit(solution)/shard_map/ppermute | solution.py:323
  50.4 5.9 %collective-permute-start.2 = (f32[8,16,384]{2,1,0:T(8,128)S(1)}, f32[8,16,384]{2,1,0:T(8,128)S(1)}, u32[]{:S(2)}, u32[]{:S(2)}) collective-permute-start(f32[8,16,384]{2,1,0:T(8,128)S(1)} %get-tuple-element.16.q_own.image_ref), channel_id=1, source_target_pairs={{0,8},{8,0},{16,24},{24,16},{32,40},{40,32},{48,56},{56,48},{64,72... | collective-permute-start | bytes 589832 | tf_op jit(solution)/shard_map/ppermute | solution.py:322
  66.0 13.5 %all-to-all-start.3 = ((f32[32,8,128]{2,1,0:T(8,128)}), f32[32,8,128]{2,1,0:T(8,128)S(1)}, u32[]{:S(2)}, u32[]{:S(2)}) async-start(f32[32,8,128]{2,1,0:T(8,128)} %get-tuple-element.18), calls=%async_computation.3 | async-start | bytes 262144 | tf_op jit(solution)/shard_map/all_to_all | solution.py:317

commit v10 on v8

--- a/solution.py
+++ b/solution.py
@@ -272,24 +272,24 @@
     return jnp.where(row // 2 == lane // K, tiled(small(pick, coeffs_t)), 0.0)
 
 
-def first_step_kernel(pick_ref, alpha_ref, field_ref, image_ref, x_out, r_out):
+def last_step_kernel(
+    pick_ref, gathered_ref, alpha_ref, field_ref, image0_ref, direction_ref, image_ref,
+    x_out, r_out,
+):
     pick = pick_ref[...]
     field = field_ref[...].reshape(ROWS, W)
     row, lane = iotas(K, ROWS)
     mine = jnp.where(row // 2 == lane // K, tiled(pick), 0.0)
-    coeffs = own_coeffs(pick, alpha_ref[:, :K])
-    x_out[...] = exact(coeffs, field)
-    r_out[...] = exact(mine, field) - exact(coeffs, image_ref[...].reshape(ROWS, W))
-
-
-def last_step_kernel(pick_ref, gathered_ref, direction_ref, image_ref, x_ref, r_ref, x_out, r_out):
+    coeffs0 = own_coeffs(pick, alpha_ref[:, :K])
+    x = exact(coeffs0, field)
+    r = exact(mine, field) - exact(coeffs0, image0_ref[...].reshape(ROWS, W))
     total = total_of(gathered_ref)
     total = jnp.concatenate([total[:, : 2 * K], total[:, 2 * K : 4 * K]], axis=0)
     qd = total[:, :K]
     alpha_t = small(total[:, K : 2 * K], inverse(0.5 * (qd + qd.T)))
-    coeffs = own_coeffs(pick_ref[...], alpha_t)
-    x = x_ref[...] + nn(coeffs, direction_ref[...])
-    r = r_ref[...] - nn(coeffs, image_ref[...])
+    coeffs = own_coeffs(pick, alpha_t)
+    x = x + nn(coeffs, direction_ref[...])
+    r = r - nn(coeffs, image_ref[...])
     for p in range(PD):
         x_out[p] = x[2 * p : 2 * p + 2]
         r_out[p] = r[2 * p : 2 * p + 2]
@@ -394,11 +394,8 @@
     )
 
     gathered = swap(message, "patch")
-    x, r = call(first_step_kernel, [VMEM] * 4, (shape(2 * PD, W),) * 2)(
-        pick_column, alpha, field, image
-    )
-    return call(last_step_kernel, [VMEM] * 6, (shape(PD, 2, W),) * 2)(
-        pick_column, gathered, direction, image1, x, r
+    return call(last_step_kernel, [VMEM] * 7, (shape(PD, 2, W),) * 2)(
+        pick_column, gathered, alpha, field, image, direction, image1
     )
 
 

time: 81.7 us -> 80.9 us (level)
  blocking collectives: 0 us -> 13.3 us
  waiting for transfers between devices: 16.7 us -> 9.89 us
  starting transfers between devices: 37.3 us -> 31.5 us
  Pallas kernels: 20.9 us -> 19.6 us
    all_to_all x0 -> x1, blocking collectives: none -> 13.3 us  [swap(): return lax.all_to_all(array, axis, 0, 0, tiled=True)]
    all_to_all x4 -> x3, waiting for transfers between devices: 14.4 us -> 7.53 us  [swap(): return lax.all_to_all(array, axis, 0, 0, tiled=True)]
    all_to_all x4 -> x3, starting transfers between devices: 26.7 us -> 20.8 us  [swap(): return lax.all_to_all(array, axis, 0, 0, tiled=True)]
    pallas_call x2 -> x1, Pallas kernels: 2.81 us -> 2.14 us  [on_device(): call(last_step_kernel, [VMEM] * 7, (shape(PD, 2, W),) * 2)]
  transfers between devices with their start and end apart: 8 -> 7, of which waited for: 5 -> 4; matrix products, arithmetic and copies ran while one was open for 2% -> 2% of each run, Pallas kernels for 11% -> 10%
where the time goes in v10:
time: 80.9 us; the launch traced here: 80.4 us
  starting transfers between devices  31.5 us (39%)
  Pallas kernels  19.6 us (24%)
  blocking collectives  13.3 us (16%)
  waiting for transfers between devices  9.89 us (12%)
  local copies, waits for them, and re-layouts  4.64 us (6%)
  other arithmetic  0.82 us (1%)
    all_to_all x3, starting transfers between devices, swap(): return lax.all_to_all(array, axis, 0, 0, tiled=True)  20.8 us
    all_to_all x1, blocking collectives, swap(): return lax.all_to_all(array, axis, 0, 0, tiled=True)  13.3 us
    all_to_all x3, waiting for transfers between devices, swap(): return lax.all_to_all(array, axis, 0, 0, tiled=True)  7.53 us
    pallas_call x1, Pallas kernels, on_device(): call(direction_kernel, [VMEM] * 13 + [HBM], (shape(count, K // 2, ROWS),...  7.03 us
    pallas_call x1, Pallas kernels, on_device(): call(near_kernel, [VMEM] * 4 + [HBM], shape(ROWS, W), (*NEAR_SCRATCH, plt...  6.44 us
    ppermute x2, starting transfers between devices, halo(): lax.ppermute(block, axis, [(i, (i + (1 if i % 2 else -1)) % count) for i...  5.34 us
    ppermute x2, starting transfers between devices, halo(): partner = lax.ppermute(block, axis, [(i, i ^ 1) for i in range(count)])  5.32 us
    unnamed x13, local copies, waits for them, and re-layouts  2.86 us
  transfers between devices with their start and end apart: 7, of which 4 were waited for; matrix products, arithmetic and copies ran while one was open for 2% of the time, Pallas kernels for 10%

profile of v10, /device:TPU:1, one launch (start us, length us, event | category | flops | bytes accessed | tf_op | source)
XLA Modules:
  0.0 80.4 jit_solution(10570617893373313696)
XLA Ops:
  0.6 0.0 copy-start.1
  0.6 0.0 copy-start
  0.6 1.6 %broadcast_in_dim.14 = f32[8,8,2,384]{3,2,1,0:T(2,128)} broadcast(f32[8,2,384]{2,1,0:T(2,128)} %param.9), dimensions={1,2,3} | broadcast | bytes 221184 | tf_op jit(solution)/shard_map/broadcast_in_dim | solution.py:350
  2.2 9.0 %all-to-all-start = ((f32[8,8,2,384]{3,2,1,0:T(2,128)}), f32[8,8,2,384]{3,2,1,0:T(2,128)S(1)}, u32[]{:S(2)}, u32[]{:S(2)}) async-start(f32[8,8,2,384]{3,2,1,0:T(2,128)} %broadcast_in_dim.14), calls=%async_computation | async-start | bytes 393216 | tf_op jit(solution)/shard_map/all_to_all | solution.py:319
  11.2 0.7 fusion.3
  11.9 0.1 reshape.47
  12.0 0.8 copy.15
  12.8 0.1 fusion.pick_ref
  12.9 0.0 copy-start.2
  12.9 1.1 %copy-done.2 = f32[8,64,384]{2,1,0:T(8,128)S(1)} copy-done((f32[8,64,384]{2,1,0:T(8,128)S(1)}, f32[8,64,384]{2,1,0:T(8,128)}, u32[]{:S(2)}) %copy-start.2) | copy-done | bytes 786456
  14.0 0.0 copy-start.4
  14.0 0.9 %copy-done.4 = f32[8,64,64]{2,1,0:T(8,128)S(1)} copy-done((f32[8,64,64]{2,1,0:T(8,128)S(1)}, f32[8,64,64]{2,1,0:T(8,128)}, u32[]{:S(2)}) %copy-start.4) | copy-done | bytes 131096
  14.9 0.0 copy-start.3
  15.0 0.0 copy-start.5
  15.0 0.5 shard_map.104
  15.4 4.8 %all-to-all-done = f32[8,8,2,384]{3,2,1,0:T(2,128)S(1)} async-done(((f32[8,8,2,384]{3,2,1,0:T(2,128)}), f32[8,8,2,384]{3,2,1,0:T(2,128)S(1)}, u32[]{:S(2)}, u32[]{:S(2)}) %all-to-all-start) | async-done | bytes 196640 | tf_op jit(solution)/shard_map/all_to_all | solution.py:319
  20.2 0.1 copy.21
  20.3 3.6 %collective-permute-start.1 = (f32[8,16,384]{2,1,0:T(8,128)S(1)}, f32[8,16,384]{2,1,0:T(8,128)S(1)}, u32[]{:S(2)}, u32[]{:S(2)}) collective-permute-start(f32[8,16,384]{2,1,0:T(8,128)S(1)} %bitcast.7), channel_id=1, source_target_pairs={{0,248},{8,16},{16,8},{24,32},{32,24},{40,48},{48,40},{56,64},{64,... | collective-permute-start | bytes 589832 | tf_op jit(solution)/shard_map/ppermute | solution.py:325
  23.9 1.8 %collective-permute-start = (f32[8,16,384]{2,1,0:T(8,128)S(1)}, f32[8,16,384]{2,1,0:T(8,128)S(1)}, u32[]{:S(2)}, u32[]{:S(2)}) collective-permute-start(f32[8,16,384]{2,1,0:T(8,128)S(1)} %bitcast.8), channel_id=1, source_target_pairs={{0,8},{8,0},{16,24},{24,16},{32,40},{40,32},{48,56},{56,48},{64,72... | collective-permute-start | bytes 589832 | tf_op jit(solution)/shard_map/ppermute | solution.py:324
  25.7 1.2 %shard_map.105 = f32[32,8,128]{2,1,0:T(8,128)} custom-call(f32[8,16,384]{2,1,0:T(8,128)S(1)} %bitcast.9, f32[64,3072]{1,0:T(8,128)S(1)} %get-tuple-element.12.up_ref), custom_call_target="tpu_custom_call" | custom-call | flops 1000000 | bytes 1000000 | tf_op jit(solution)/shard_map/pallas_call | solution.py:366
  26.9 5.5 %all-to-all-start.1 = ((f32[32,8,128]{2,1,0:T(8,128)}), f32[32,8,128]{2,1,0:T(8,128)S(1)}, u32[]{:S(2)}, u32[]{:S(2)}) async-start(f32[32,8,128]{2,1,0:T(8,128)} %shard_map.105), calls=%async_computation.1 | async-start | bytes 262144 | tf_op jit(solution)/shard_map/all_to_all | solution.py:319
  32.4 0.0 collective-permute-done.1.beyond_ref.f_beyond
  32.4 0.0 collective-permute-done.partner_ref.f_partner
  32.4 6.4 %shard_map.106.near_ref = f32[128,384]{1,0:T(8,128)S(1)} custom-call(s32[8,4]{1,0:T(8,128)S(1)} %fusion.1.ids_ref, f32[8,16,384]{2,1,0:T(8,128)S(1)} %collective-permute-done.partner_ref.f_partner, f32[8,16,384]{2,1,0:T(8,128)S(1)} %bitcast.10, f32[8,16,384]{2,1,0:T(8,128)S(1)} %collective-permute-done.1.beyond_ref.f_beyond, bf16[8,4,384,384]{3,2,1,0:T(8,128)(2,1)} %near_ref.3), custom_call_target="tpu_custom_call" | custom-call | flops 1000000 | bytes 1000000 | tf_op jit(solution)/shard_map/pallas_call | solution.py:368
  38.9 1.1 %all-to-all-done.1.gathered_ref = f32[32,8,128]{2,1,0:T(8,128)S(1)} async-done(((f32[32,8,128]{2,1,0:T(8,128)}), f32[32,8,128]{2,1,0:T(8,128)S(1)}, u32[]{:S(2)}, u32[]{:S(2)}) %all-to-all-start.1) | async-done | bytes 131104 | tf_op jit(solution)/shard_map/all_to_all | solution.py:319
  40.0 0.1 broadcast_in_dim.13.pick_ref
  40.0 0.0 copy-done.1
  40.1 0.0 copy-done
  40.1 0.0 copy-done.3
  40.1 2.4 %shard_map.107 = (f32[8,16,384]{2,1,0:T(8,128)S(1)}, f32[16,128]{1,0:T(8,128)S(1)}, f32[32,16,128]{2,1,0:T(8,128)}) custom-call(f32[128,128]{1,0:T(8,128)S(1)} %broadcast_in_dim.13.pick_ref, f32[32,8,128]{2,1,0:T(8,128)S(1)} %all-to-all-done.1.gathered_ref, f32[128,384]{1,0:T(8,128)S(1)} %shard_map.106.near_ref, f32[8,16,384]{2,1,0:T(8,128)S(1)} %bitcast.11, ...), custom_call_target="tpu_custom_call" | custom-call | flops 1000000 | bytes 1000000 | tf_op jit(solution)/shard_map/pallas_call | solution.py:377
  42.4 6.3 %all-to-all-start.2 = ((f32[32,16,128]{2,1,0:T(8,128)}), f32[32,16,128]{2,1,0:T(8,128)S(1)}, u32[]{:S(2)}, u32[]{:S(2)}) async-start(f32[32,16,128]{2,1,0:T(8,128)} %get-tuple-element.13), calls=%async_computation.2 | async-start | bytes 524288 | tf_op jit(solution)/shard_map/all_to_all | solution.py:319
  48.7 1.7 %collective-permute-start.3 = (f32[8,16,384]{2,1,0:T(8,128)S(1)}, f32[8,16,384]{2,1,0:T(8,128)S(1)}, u32[]{:S(2)}, u32[]{:S(2)}) collective-permute-start(f32[8,16,384]{2,1,0:T(8,128)S(1)} %get-tuple-element.14.q_own.image0_ref), channel_id=1, source_target_pairs={{0,248},{8,16},{16,8},{24,32},{32,24},{40,48},{48,40},{56,64},{64,... | collective-permute-start | bytes 589832 | tf_op jit(solution)/shard_map/ppermute | solution.py:325
  50.4 3.5 %collective-permute-start.2 = (f32[8,16,384]{2,1,0:T(8,128)S(1)}, f32[8,16,384]{2,1,0:T(8,128)S(1)}, u32[]{:S(2)}, u32[]{:S(2)}) collective-permute-start(f32[8,16,384]{2,1,0:T(8,128)S(1)} %get-tuple-element.14.q_own.image0_ref), channel_id=1, source_target_pairs={{0,8},{8,0},{16,24},{24,16},{32,40},{40,32},{48,56},{56,48},{64,72... | collective-permute-start | bytes 589832 | tf_op jit(solution)/shard_map/ppermute | solution.py:324
  54.0 2.4 %collective-permute-done.3.q_beyond = f32[8,16,384]{2,1,0:T(8,128)S(1)} collective-permute-done((f32[8,16,384]{2,1,0:T(8,128)S(1)}, f32[8,16,384]{2,1,0:T(8,128)S(1)}, u32[]{:S(2)}, u32[]{:S(2)}) %collective-permute-start.3) | collective-permute-done | bytes 196640 | tf_op jit(solution)/shard_map/ppermute | solution.py:325
  56.3 0.0 collective-permute-done.2.q_partner
  56.3 1.6 %all-to-all-done.2.gathered_ref = f32[32,16,128]{2,1,0:T(8,128)S(1)} async-done(((f32[32,16,128]{2,1,0:T(8,128)}), f32[32,16,128]{2,1,0:T(8,128)S(1)}, u32[]{:S(2)}, u32[]{:S(2)}) %all-to-all-start.2) | async-done | bytes 262176 | tf_op jit(solution)/shard_map/all_to_all | solution.py:319
  58.0 0.0 copy-done.5
  58.0 7.0 %shard_map.108 = (f32[32,8,128]{2,1,0:T(8,128)S(1)}, f32[128,384]{1,0:T(8,128)S(1)}, f32[128,384]{1,0:T(8,128)S(1)}, f32[16,128]{1,0:T(8,128)S(1)}) custom-call(s32[8,4]{1,0:T(8,128)S(1)} %fusion.1.ids_ref, s32[1,4]{1,0:T(1,128)S(1)} %copy-done.5, f32[32,16,128]{2,1,0:T(8,128)S(1)} %all-to-all-done.2.gathered_ref, ...), custom_call_target="tpu_custom_call" | custom-call | flops 1000000 | bytes 1000000 | tf_op jit(solution)/shard_map/pallas_call | solution.py:385
  65.0 13.3 %all_to_all.20.gathered_ref = f32[32,8,128]{2,1,0:T(8,128)S(1)} all-to-all(f32[32,8,128]{2,1,0:T(8,128)S(1)} %get-tuple-element.16), channel_id=1, replica_groups=mesh['patch'=32,'rhs'=8] {'patch'}, dimensions={0} | all-to-all | bytes 262144 | tf_op jit(solution)/shard_map/all_to_all | solution.py:319
  78.3 2.1 %shard_map.109 = (f32[8,2,384]{2,1,0:T(2,128)}, f32[8,2,384]{2,1,0:T(2,128)}) custom-call(f32[16,16]{1,0:T(8,128)S(1)} %get-tuple-element.11.pick_ref, f32[32,8,128]{2,1,0:T(8,128)S(1)} %all_to_all.20.gathered_ref, f32[16,128]{1,0:T(8,128)S(1)} %get-tuple-element.17.alpha_ref, f32[8,16,384]{2,1,0:T(8,128)S(1)} %bitcast.13, ...), custom_call_target="tpu_custom_call" | custom-call | flops 1000000 | bytes 1000000 | tf_op jit(solution)/shard_map/pallas_call | solution.py:397
  (2 shorter events, 0.0 us)
Async XLA Ops:
  0.6 39.4 %copy-start.1 = (f32[8,64,64]{2,1,0:T(8,128)S(1)}, f32[8,64,64]{2,1,0:T(8,128)}, u32[]{:S(2)}) copy-start(f32[8,64,64]{2,1,0:T(8,128)} %shift_ref.5) | copy-start | bytes 393220
  0.6 39.4 %copy-start = (f32[8,384,64]{1,2,0:T(8,128)S(1)}, f32[8,384,64]{1,2,0:T(8,128)}, u32[]{:S(2)}) copy-start(f32[8,384,64]{1,2,0:T(8,128)} %param.17) | copy-start | bytes 2359300
  2.2 18.0 %all-to-all-start = ((f32[8,8,2,384]{3,2,1,0:T(2,128)}), f32[8,8,2,384]{3,2,1,0:T(2,128)S(1)}, u32[]{:S(2)}, u32[]{:S(2)}) async-start(f32[8,8,2,384]{3,2,1,0:T(2,128)} %broadcast_in_dim.14), calls=%async_computation | async-start | bytes 393216 | tf_op jit(solution)/shard_map/all_to_all | solution.py:319
  12.9 1.1 %copy-start.2 = (f32[8,64,384]{2,1,0:T(8,128)S(1)}, f32[8,64,384]{2,1,0:T(8,128)}, u32[]{:S(2)}) copy-start(f32[8,64,384]{2,1,0:T(8,128)} %up_ref.1) | copy-start | bytes 2359300
  14.0 0.9 %copy-start.4 = (f32[8,64,64]{2,1,0:T(8,128)S(1)}, f32[8,64,64]{2,1,0:T(8,128)}, u32[]{:S(2)}) copy-start(f32[8,64,64]{2,1,0:T(8,128)} %shift_ref.3) | copy-start | bytes 393220
  14.9 25.1 %copy-start.3 = (f32[1,4,64,64]{3,2,1,0:T(8,128)S(1)}, f32[1,4,64,64]{3,2,1,0:T(8,128)}, u32[]{:S(2)}) copy-start(f32[1,4,64,64]{3,2,1,0:T(8,128)} %param.15) | copy-start | bytes 196612
  15.0 43.0 %copy-start.5 = (s32[1,4]{1,0:T(1,128)S(1)}, s32[1,4]{1,0:T(1,128)}, u32[]{:S(2)}) copy-start(s32[1,4]{1,0:T(1,128)} %far_ref.1) | copy-start | bytes 52
  20.3 12.1 %collective-permute-start.1 = (f32[8,16,384]{2,1,0:T(8,128)S(1)}, f32[8,16,384]{2,1,0:T(8,128)S(1)}, u32[]{:S(2)}, u32[]{:S(2)}) collective-permute-start(f32[8,16,384]{2,1,0:T(8,128)S(1)} %bitcast.7), channel_id=1, source_target_pairs={{0,248},{8,16},{16,8},{24,32},{32,24},{40,48},{48,40},{56,64},{64,... | collective-permute-start | bytes 589832 | tf_op jit(solution)/shard_map/ppermute | solution.py:325
  23.9 8.5 %collective-permute-start = (f32[8,16,384]{2,1,0:T(8,128)S(1)}, f32[8,16,384]{2,1,0:T(8,128)S(1)}, u32[]{:S(2)}, u32[]{:S(2)}) collective-permute-start(f32[8,16,384]{2,1,0:T(8,128)S(1)} %bitcast.8), channel_id=1, source_target_pairs={{0,8},{8,0},{16,24},{24,16},{32,40},{40,32},{48,56},{56,48},{64,72... | collective-permute-start | bytes 589832 | tf_op jit(solution)/shard_map/ppermute | solution.py:324
  26.9 13.1 %all-to-all-start.1 = ((f32[32,8,128]{2,1,0:T(8,128)}), f32[32,8,128]{2,1,0:T(8,128)S(1)}, u32[]{:S(2)}, u32[]{:S(2)}) async-start(f32[32,8,128]{2,1,0:T(8,128)} %shard_map.105), calls=%async_computation.1 | async-start | bytes 262144 | tf_op jit(solution)/shard_map/all_to_all | solution.py:319
  42.4 15.5 %all-to-all-start.2 = ((f32[32,16,128]{2,1,0:T(8,128)}), f32[32,16,128]{2,1,0:T(8,128)S(1)}, u32[]{:S(2)}, u32[]{:S(2)}) async-start(f32[32,16,128]{2,1,0:T(8,128)} %get-tuple-element.13), calls=%async_computation.2 | async-start | bytes 524288 | tf_op jit(solution)/shard_map/all_to_all | solution.py:319
  48.7 7.6 %collective-permute-start.3 = (f32[8,16,384]{2,1,0:T(8,128)S(1)}, f32[8,16,384]{2,1,0:T(8,128)S(1)}, u32[]{:S(2)}, u32[]{:S(2)}) collective-permute-start(f32[8,16,384]{2,1,0:T(8,128)S(1)} %get-tuple-element.14.q_own.image0_ref), channel_id=1, source_target_pairs={{0,248},{8,16},{16,8},{24,32},{32,24},{40,48},{48,40},{56,64},{64,... | collective-permute-start | bytes 589832 | tf_op jit(solution)/shard_map/ppermute | solution.py:325
  50.4 5.9 %collective-permute-start.2 = (f32[8,16,384]{2,1,0:T(8,128)S(1)}, f32[8,16,384]{2,1,0:T(8,128)S(1)}, u32[]{:S(2)}, u32[]{:S(2)}) collective-permute-start(f32[8,16,384]{2,1,0:T(8,128)S(1)} %get-tuple-element.14.q_own.image0_ref), channel_id=1, source_target_pairs={{0,8},{8,0},{16,24},{24,16},{32,40},{40,32},{48,56},{56,48},{64,72... | collective-permute-start | bytes 589832 | tf_op jit(solution)/shard_map/ppermute | solution.py:324

commit v11 on v10

--- a/solution.py
+++ b/solution.py
@@ -207,7 +207,7 @@
 
 
 def direction_kernel(
-    ids_ref, far_ref, gathered_ref, f_partner, f_own, f_beyond, q_partner, q_own, q_beyond,
+    ids_ref, far_ref, gathered_ref, total_ref, f_partner, f_own, f_beyond, q_partner, q_own, q_beyond,
     local_ref, table_ref, shift_ref, down_ref, near_ref,
     out_ref, direction_out, image_out, alpha_out,
     blocks_ref, rounded_ref, ids_smem, far_smem, sems,
@@ -217,7 +217,7 @@
     ids.start()
     far_ids.start()
     fetch(near_ref, blocks_ref, sems)
-    total = total_of(gathered_ref)
+    total = total_ref[...]
     qr = total[:, E : E + K]
     qq = total[:, E + K : E + 2 * K]
     rr = total[:, E + 2 * K : E + 3 * K]
@@ -382,14 +382,15 @@
 
     q_partner, q_beyond = halo(image, "patch")
     gathered = swap(message, "patch")
+    total = gathered.sum(axis=0)
     message, direction, image1, alpha = call(
         direction_kernel,
-        [VMEM] * 13 + [HBM],
+        [VMEM] * 14 + [HBM],
         (shape(count, K // 2, ROWS), shape(ROWS, W), shape(ROWS, W), shape(K, ROWS)),
         (*NEAR_SCRATCH, pltpu.SMEM((1, FL), jnp.int32), pltpu.SemaphoreType.DMA((PD + 2,))),
         limit=48,
     )(
-        ids, far_lists, gathered, f_partner, field, f_beyond, q_partner, image, q_beyond,
+        ids, far_lists, gathered, total, f_partner, field, f_beyond, q_partner, image, q_beyond,
         local_exp, table, shift_down, down, near_blocks,
     )
 

time: 80.9 us -> 80.9 us (level)
    all_to_all x3, waiting for transfers between devices: 7.53 us -> 9.9 us  [swap(): return lax.all_to_all(array, axis, 0, 0, tiled=True)]
    ppermute x2, waiting for transfers between devices: 2.36 us -> 0.01 us  [halo(): lax.ppermute(block, axis, [(i, (i + (1 if i % 2 else -1)) % count) for i...]
  transfers between devices with their start and end apart: 7 -> 7, of which waited for: 4 -> 3; matrix products, arithmetic and copies ran while one was open for 2% -> 2% of each run, Pallas kernels for 10% -> 10%
where the time goes in v11:
time: 80.9 us; the launch traced here: 80.4 us
  starting transfers between devices  31.4 us (39%)
  Pallas kernels  19.6 us (24%)
  blocking collectives  13.2 us (16%)
  waiting for transfers between devices  9.91 us (12%)
  local copies, waits for them, and re-layouts  4.63 us (6%)
  other arithmetic  0.86 us (1%)
    all_to_all x3, starting transfers between devices, swap(): return lax.all_to_all(array, axis, 0, 0, tiled=True)  20.8 us
    all_to_all x1, blocking collectives, swap(): return lax.all_to_all(array, axis, 0, 0, tiled=True)  13.2 us
    all_to_all x3, waiting for transfers between devices, swap(): return lax.all_to_all(array, axis, 0, 0, tiled=True)  9.9 us
    pallas_call x1, Pallas kernels, on_device(): call(direction_kernel, [VMEM] * 14 + [HBM], (shape(count, K // 2, ROWS),...  7.05 us
    pallas_call x1, Pallas kernels, on_device(): call(near_kernel, [VMEM] * 4 + [HBM], shape(ROWS, W), (*NEAR_SCRATCH, plt...  6.44 us
    ppermute x2, starting transfers between devices, halo(): lax.ppermute(block, axis, [(i, (i + (1 if i % 2 else -1)) % count) for i...  5.34 us
    ppermute x2, starting transfers between devices, halo(): partner = lax.ppermute(block, axis, [(i, i ^ 1) for i in range(count)])  5.32 us
    unnamed x13, local copies, waits for them, and re-layouts  2.86 us
  transfers between devices with their start and end apart: 7, of which 3 were waited for; matrix products, arithmetic and copies ran while one was open for 2% of the time, Pallas kernels for 10%

profile of v11, /device:TPU:1, one launch (start us, length us, event | category | flops | bytes accessed | tf_op | source)
XLA Modules:
  0.0 80.4 jit_solution(4228693469368541696)
XLA Ops:
  0.6 0.0 copy-start.1
  0.6 0.0 copy-start
  0.6 1.6 %broadcast_in_dim.14 = f32[8,8,2,384]{3,2,1,0:T(2,128)} broadcast(f32[8,2,384]{2,1,0:T(2,128)} %param.9), dimensions={1,2,3} | broadcast | bytes 221184 | tf_op jit(solution)/shard_map/broadcast_in_dim | solution.py:350
  2.2 9.0 %all-to-all-start = ((f32[8,8,2,384]{3,2,1,0:T(2,128)}), f32[8,8,2,384]{3,2,1,0:T(2,128)S(1)}, u32[]{:S(2)}, u32[]{:S(2)}) async-start(f32[8,8,2,384]{3,2,1,0:T(2,128)} %broadcast_in_dim.14), calls=%async_computation | async-start | bytes 393216 | tf_op jit(solution)/shard_map/all_to_all | solution.py:319
  11.2 0.7 fusion.3
  11.9 0.1 reshape.47
  12.0 0.8 copy.15
  12.8 0.1 fusion.pick_ref
  12.9 0.0 copy-start.2
  12.9 1.1 %copy-done.2 = f32[8,64,384]{2,1,0:T(8,128)S(1)} copy-done((f32[8,64,384]{2,1,0:T(8,128)S(1)}, f32[8,64,384]{2,1,0:T(8,128)}, u32[]{:S(2)}) %copy-start.2) | copy-done | bytes 786456
  14.0 0.0 copy-start.4
  14.0 0.9 %copy-done.4 = f32[8,64,64]{2,1,0:T(8,128)S(1)} copy-done((f32[8,64,64]{2,1,0:T(8,128)S(1)}, f32[8,64,64]{2,1,0:T(8,128)}, u32[]{:S(2)}) %copy-start.4) | copy-done | bytes 131096
  14.9 0.0 copy-start.3
  14.9 0.0 copy-start.5
  14.9 0.4 shard_map.104
  15.4 4.8 %all-to-all-done = f32[8,8,2,384]{3,2,1,0:T(2,128)S(1)} async-done(((f32[8,8,2,384]{3,2,1,0:T(2,128)}), f32[8,8,2,384]{3,2,1,0:T(2,128)S(1)}, u32[]{:S(2)}, u32[]{:S(2)}) %all-to-all-start) | async-done | bytes 196640 | tf_op jit(solution)/shard_map/all_to_all | solution.py:319
  20.2 0.1 copy.21
  20.3 3.6 %collective-permute-start.1 = (f32[8,16,384]{2,1,0:T(8,128)S(1)}, f32[8,16,384]{2,1,0:T(8,128)S(1)}, u32[]{:S(2)}, u32[]{:S(2)}) collective-permute-start(f32[8,16,384]{2,1,0:T(8,128)S(1)} %bitcast.7), channel_id=1, source_target_pairs={{0,248},{8,16},{16,8},{24,32},{32,24},{40,48},{48,40},{56,64},{64,... | collective-permute-start | bytes 589832 | tf_op jit(solution)/shard_map/ppermute | solution.py:325
  23.9 1.8 %collective-permute-start = (f32[8,16,384]{2,1,0:T(8,128)S(1)}, f32[8,16,384]{2,1,0:T(8,128)S(1)}, u32[]{:S(2)}, u32[]{:S(2)}) collective-permute-start(f32[8,16,384]{2,1,0:T(8,128)S(1)} %bitcast.8), channel_id=1, source_target_pairs={{0,8},{8,0},{16,24},{24,16},{32,40},{40,32},{48,56},{56,48},{64,72... | collective-permute-start | bytes 589832 | tf_op jit(solution)/shard_map/ppermute | solution.py:324
  25.7 1.2 %shard_map.105 = f32[32,8,128]{2,1,0:T(8,128)} custom-call(f32[8,16,384]{2,1,0:T(8,128)S(1)} %bitcast.9, f32[64,3072]{1,0:T(8,128)S(1)} %get-tuple-element.12.up_ref), custom_call_target="tpu_custom_call" | custom-call | flops 1000000 | bytes 1000000 | tf_op jit(solution)/shard_map/pallas_call | solution.py:366
  26.8 5.5 %all-to-all-start.1 = ((f32[32,8,128]{2,1,0:T(8,128)}), f32[32,8,128]{2,1,0:T(8,128)S(1)}, u32[]{:S(2)}, u32[]{:S(2)}) async-start(f32[32,8,128]{2,1,0:T(8,128)} %shard_map.105), calls=%async_computation.1 | async-start | bytes 262144 | tf_op jit(solution)/shard_map/all_to_all | solution.py:319
  32.4 0.0 collective-permute-done.1.beyond_ref.f_beyond
  32.4 0.0 collective-permute-done.partner_ref.f_partner
  32.4 6.4 %shard_map.106.near_ref = f32[128,384]{1,0:T(8,128)S(1)} custom-call(s32[8,4]{1,0:T(8,128)S(1)} %fusion.1.ids_ref, f32[8,16,384]{2,1,0:T(8,128)S(1)} %collective-permute-done.partner_ref.f_partner, f32[8,16,384]{2,1,0:T(8,128)S(1)} %bitcast.10, f32[8,16,384]{2,1,0:T(8,128)S(1)} %collective-permute-done.1.beyond_ref.f_beyond, bf16[8,4,384,384]{3,2,1,0:T(8,128)(2,1)} %near_ref.3), custom_call_target="tpu_custom_call" | custom-call | flops 1000000 | bytes 1000000 | tf_op jit(solution)/shard_map/pallas_call | solution.py:368
  38.8 1.1 %all-to-all-done.1.gathered_ref = f32[32,8,128]{2,1,0:T(8,128)S(1)} async-done(((f32[32,8,128]{2,1,0:T(8,128)}), f32[32,8,128]{2,1,0:T(8,128)S(1)}, u32[]{:S(2)}, u32[]{:S(2)}) %all-to-all-start.1) | async-done | bytes 131104 | tf_op jit(solution)/shard_map/all_to_all | solution.py:319
  39.9 0.1 broadcast_in_dim.13.pick_ref
  40.0 0.0 copy-done.1
  40.0 0.0 copy-done
  40.0 0.0 copy-done.3
  40.1 2.3 %shard_map.107 = (f32[8,16,384]{2,1,0:T(8,128)S(1)}, f32[16,128]{1,0:T(8,128)S(1)}, f32[32,16,128]{2,1,0:T(8,128)}) custom-call(f32[128,128]{1,0:T(8,128)S(1)} %broadcast_in_dim.13.pick_ref, f32[32,8,128]{2,1,0:T(8,128)S(1)} %all-to-all-done.1.gathered_ref, f32[128,384]{1,0:T(8,128)S(1)} %shard_map.106.near_ref, f32[8,16,384]{2,1,0:T(8,128)S(1)} %bitcast.11, ...), custom_call_target="tpu_custom_call" | custom-call | flops 1000000 | bytes 1000000 | tf_op jit(solution)/shard_map/pallas_call | solution.py:377
  42.4 6.3 %all-to-all-start.2 = ((f32[32,16,128]{2,1,0:T(8,128)}), f32[32,16,128]{2,1,0:T(8,128)S(1)}, u32[]{:S(2)}, u32[]{:S(2)}) async-start(f32[32,16,128]{2,1,0:T(8,128)} %get-tuple-element.13), calls=%async_computation.2 | async-start | bytes 524288 | tf_op jit(solution)/shard_map/all_to_all | solution.py:319
  48.7 1.7 %collective-permute-start.3 = (f32[8,16,384]{2,1,0:T(8,128)S(1)}, f32[8,16,384]{2,1,0:T(8,128)S(1)}, u32[]{:S(2)}, u32[]{:S(2)}) collective-permute-start(f32[8,16,384]{2,1,0:T(8,128)S(1)} %get-tuple-element.14.q_own.image0_ref), channel_id=1, source_target_pairs={{0,248},{8,16},{16,8},{24,32},{32,24},{40,48},{48,40},{56,64},{64,... | collective-permute-start | bytes 589832 | tf_op jit(solution)/shard_map/ppermute | solution.py:325
  50.4 3.5 %collective-permute-start.2 = (f32[8,16,384]{2,1,0:T(8,128)S(1)}, f32[8,16,384]{2,1,0:T(8,128)S(1)}, u32[]{:S(2)}, u32[]{:S(2)}) collective-permute-start(f32[8,16,384]{2,1,0:T(8,128)S(1)} %get-tuple-element.14.q_own.image0_ref), channel_id=1, source_target_pairs={{0,8},{8,0},{16,24},{24,16},{32,40},{40,32},{48,56},{56,48},{64,72... | collective-permute-start | bytes 589832 | tf_op jit(solution)/shard_map/ppermute | solution.py:324
  53.9 4.0 %all-to-all-done.2.gathered_ref = f32[32,16,128]{2,1,0:T(8,128)S(1)} async-done(((f32[32,16,128]{2,1,0:T(8,128)}), f32[32,16,128]{2,1,0:T(8,128)S(1)}, u32[]{:S(2)}, u32[]{:S(2)}) %all-to-all-start.2) | async-done | bytes 262176 | tf_op jit(solution)/shard_map/all_to_all | solution.py:319
  58.0 0.0 collective-permute-done.3.q_beyond
  58.0 0.0 collective-permute-done.2.q_partner
  58.0 0.0 copy-done.5
  58.0 7.1 %shard_map.108 = (f32[32,8,128]{2,1,0:T(8,128)S(1)}, f32[128,384]{1,0:T(8,128)S(1)}, f32[128,384]{1,0:T(8,128)S(1)}, f32[16,128]{1,0:T(8,128)S(1)}) custom-call(s32[8,4]{1,0:T(8,128)S(1)} %fusion.1.ids_ref, s32[1,4]{1,0:T(1,128)S(1)} %copy-done.5, f32[32,16,128]{2,1,0:T(8,128)S(1)} %all-to-all-done.2.gathered_ref, f32[16,128]{1,0:T(8,128)S(1)} %reduce_sum.9.total_ref, ...), custom_call_target="tpu_custom_call" | custom-call | flops 1000000 | bytes 1000000 | tf_op jit(solution)/shard_map/pallas_call | solution.py:386
  65.1 13.2 %all_to_all.20.gathered_ref = f32[32,8,128]{2,1,0:T(8,128)S(1)} all-to-all(f32[32,8,128]{2,1,0:T(8,128)S(1)} %get-tuple-element.16), channel_id=1, replica_groups=mesh['patch'=32,'rhs'=8] {'patch'}, dimensions={0} | all-to-all | bytes 262144 | tf_op jit(solution)/shard_map/all_to_all | solution.py:319
  78.2 2.1 %shard_map.109 = (f32[8,2,384]{2,1,0:T(2,128)}, f32[8,2,384]{2,1,0:T(2,128)}) custom-call(f32[16,16]{1,0:T(8,128)S(1)} %get-tuple-element.11.pick_ref, f32[32,8,128]{2,1,0:T(8,128)S(1)} %all_to_all.20.gathered_ref, f32[16,128]{1,0:T(8,128)S(1)} %get-tuple-element.17.alpha_ref, f32[8,16,384]{2,1,0:T(8,128)S(1)} %bitcast.13, ...), custom_call_target="tpu_custom_call" | custom-call | flops 1000000 | bytes 1000000 | tf_op jit(solution)/shard_map/pallas_call | solution.py:398
  (3 shorter events, 0.1 us)
Async XLA Ops:
  0.6 39.4 %copy-start.1 = (f32[8,64,64]{2,1,0:T(8,128)S(1)}, f32[8,64,64]{2,1,0:T(8,128)}, u32[]{:S(2)}) copy-start(f32[8,64,64]{2,1,0:T(8,128)} %shift_ref.5) | copy-start | bytes 393220
  0.6 39.4 %copy-start = (f32[8,384,64]{1,2,0:T(8,128)S(1)}, f32[8,384,64]{1,2,0:T(8,128)}, u32[]{:S(2)}) copy-start(f32[8,384,64]{1,2,0:T(8,128)} %param.17) | copy-start | bytes 2359300
  2.2 18.0 %all-to-all-start = ((f32[8,8,2,384]{3,2,1,0:T(2,128)}), f32[8,8,2,384]{3,2,1,0:T(2,128)S(1)}, u32[]{:S(2)}, u32[]{:S(2)}) async-start(f32[8,8,2,384]{3,2,1,0:T(2,128)} %broadcast_in_dim.14), calls=%async_computation | async-start | bytes 393216 | tf_op jit(solution)/shard_map/all_to_all | solution.py:319
  12.9 1.1 %copy-start.2 = (f32[8,64,384]{2,1,0:T(8,128)S(1)}, f32[8,64,384]{2,1,0:T(8,128)}, u32[]{:S(2)}) copy-start(f32[8,64,384]{2,1,0:T(8,128)} %up_ref.1) | copy-start | bytes 2359300
  14.0 0.9 %copy-start.4 = (f32[8,64,64]{2,1,0:T(8,128)S(1)}, f32[8,64,64]{2,1,0:T(8,128)}, u32[]{:S(2)}) copy-start(f32[8,64,64]{2,1,0:T(8,128)} %shift_ref.3) | copy-start | bytes 393220
  14.9 25.1 %copy-start.3 = (f32[1,4,64,64]{3,2,1,0:T(8,128)S(1)}, f32[1,4,64,64]{3,2,1,0:T(8,128)}, u32[]{:S(2)}) copy-start(f32[1,4,64,64]{3,2,1,0:T(8,128)} %param.15) | copy-start | bytes 196612
  14.9 43.0 %copy-start.5 = (s32[1,4]{1,0:T(1,128)S(1)}, s32[1,4]{1,0:T(1,128)}, u32[]{:S(2)}) copy-start(s32[1,4]{1,0:T(1,128)} %far_ref.1) | copy-start | bytes 52
  20.3 12.1 %collective-permute-start.1 = (f32[8,16,384]{2,1,0:T(8,128)S(1)}, f32[8,16,384]{2,1,0:T(8,128)S(1)}, u32[]{:S(2)}, u32[]{:S(2)}) collective-permute-start(f32[8,16,384]{2,1,0:T(8,128)S(1)} %bitcast.7), channel_id=1, source_target_pairs={{0,248},{8,16},{16,8},{24,32},{32,24},{40,48},{48,40},{56,64},{64,... | collective-permute-start | bytes 589832 | tf_op jit(solution)/shard_map/ppermute | solution.py:325
  23.9 8.5 %collective-permute-start = (f32[8,16,384]{2,1,0:T(8,128)S(1)}, f32[8,16,384]{2,1,0:T(8,128)S(1)}, u32[]{:S(2)}, u32[]{:S(2)}) collective-permute-start(f32[8,16,384]{2,1,0:T(8,128)S(1)} %bitcast.8), channel_id=1, source_target_pairs={{0,8},{8,0},{16,24},{24,16},{32,40},{40,32},{48,56},{56,48},{64,72... | collective-permute-start | bytes 589832 | tf_op jit(solution)/shard_map/ppermute | solution.py:324
  26.8 13.1 %all-to-all-start.1 = ((f32[32,8,128]{2,1,0:T(8,128)}), f32[32,8,128]{2,1,0:T(8,128)S(1)}, u32[]{:S(2)}, u32[]{:S(2)}) async-start(f32[32,8,128]{2,1,0:T(8,128)} %shard_map.105), calls=%async_computation.1 | async-start | bytes 262144 | tf_op jit(solution)/shard_map/all_to_all | solution.py:319
  42.4 15.5 %all-to-all-start.2 = ((f32[32,16,128]{2,1,0:T(8,128)}), f32[32,16,128]{2,1,0:T(8,128)S(1)}, u32[]{:S(2)}, u32[]{:S(2)}) async-start(f32[32,16,128]{2,1,0:T(8,128)} %get-tuple-element.13), calls=%async_computation.2 | async-start | bytes 524288 | tf_op jit(solution)/shard_map/all_to_all | solution.py:319
  48.7 9.3 %collective-permute-start.3 = (f32[8,16,384]{2,1,0:T(8,128)S(1)}, f32[8,16,384]{2,1,0:T(8,128)S(1)}, u32[]{:S(2)}, u32[]{:S(2)}) collective-permute-start(f32[8,16,384]{2,1,0:T(8,128)S(1)} %get-tuple-element.14.q_own.image0_ref), channel_id=1, source_target_pairs={{0,248},{8,16},{16,8},{24,32},{32,24},{40,48},{48,40},{56,64},{64,... | collective-permute-start | bytes 589832 | tf_op jit(solution)/shard_map/ppermute | solution.py:325
  50.4 7.6 %collective-permute-start.2 = (f32[8,16,384]{2,1,0:T(8,128)S(1)}, f32[8,16,384]{2,1,0:T(8,128)S(1)}, u32[]{:S(2)}, u32[]{:S(2)}) collective-permute-start(f32[8,16,384]{2,1,0:T(8,128)S(1)} %get-tuple-element.14.q_own.image0_ref), channel_id=1, source_target_pairs={{0,8},{8,0},{16,24},{24,16},{32,40},{40,32},{48,56},{56,48},{64,72... | collective-permute-start | bytes 589832 | tf_op jit(solution)/shard_map/ppermute | solution.py:324
